TPU v7x, 32 devices: a whole 2x2x4 slice. The times are simulated.
32 devices in a mesh: dp: 4 (over x, core), seq: 8 (over z, y).
Axes of the slice: x: 2, y: 2, z: 4, core: 2. Of those that a mesh axis runs over, the one named last changes fastest.
Arguments:
- hidden: bfloat16 [8, 1024, 2048], P('dp', 'seq'), may hold values from -6 to 6
- grad_out: bfloat16 [8, 1024, 2048], P('dp', 'seq'), may hold values from -6 to 6
- lengths: int32 [8], P('dp'), may hold values from 256 to 1024, as said below
- norm_gain: bfloat16 [2048], P('seq'), may hold values from 0.25 to 1.75
- input_weight: bfloat16 [2048, 8192], P('seq'), may hold values from -0.125 to 0.125
- conv_weight: bfloat16 [4, 4096], P(None, 'seq'), may hold values from -3 to 3
- conv_bias: bfloat16 [4096], P('seq'), may hold values from -3 to 3
- select_weight: bfloat16 [160, 4096], P(None, 'seq'), may hold values from -0.09375 to 0.09375
- step_weight: bfloat16 [128, 4096], P(None, 'seq'), may hold values from -0.5 to 0.5
- step_bias: bfloat16 [4096], P('seq'), may hold values from -13 to 0
- decay_log: bfloat16 [16, 4096], P(None, 'seq'), may hold values from -0.69921875 to 1.3984375
- skip_weight: bfloat16 [4096], P('seq'), may hold values from 0.5 to 2
- output_weight: bfloat16 [4096, 2048], P('seq'), may hold values from -0.25 to 0.25
Outputs:
- output: bfloat16 [8, 1024, 2048], P('dp', 'seq')
- grad_hidden: float32 [8, 1024, 2048], P('dp', 'seq')
- grad_norm_gain: float32 [2048], P('seq')
- grad_input_weight: float32 [2048, 8192], P('seq')
- grad_conv_weight: float32 [4, 4096], P(None, 'seq')
- grad_conv_bias: float32 [4096], P('seq')
- grad_select_weight: float32 [160, 4096], P(None, 'seq')
- grad_step_weight: float32 [128, 4096], P(None, 'seq')
- grad_step_bias: float32 [4096], P('seq')
- grad_decay_log: float32 [16, 4096], P(None, 'seq')
- grad_skip_weight: float32 [4096], P('seq')
- grad_output_weight: float32 [4096, 2048], P('seq')
Inputs may be any that keep to these rules, and one draw needn't show every extreme that they name: Row r holds one sequence in slots 0 to lengths[r] - 1 and padding after it; some row is full.
All inputs are finite; a program needn't handle non-finite values.
Results may differ from a plain program's by a relative error of at most 0.012.
Values may be sent and summed in bfloat16 or wider, within the bound.
A program may use at most 320 MiB of HBM per device.

v0:
```python
import jax
import jax.numpy as jnp
from jax import lax
from jax.sharding import PartitionSpec as P

BLOCK = 16


EPSILON = 1e-05


def from_behind(value, axis, steps):
    count = lax.axis_size(axis)
    initial, last = (max(0, -steps), min(count, count - steps))
    return lax.ppermute(value, axis, [(source, source + steps) for source in range(initial, last)])


def prefix(value, axis, combine, identity, reverse):
    size, position = (lax.axis_size(axis), lax.axis_index(axis))
    everything = jax.tree.map(lambda part: lax.all_gather(part, axis), value)
    start = jax.tree.map(
        lambda part, zero: jnp.broadcast_to(jnp.asarray(zero, part.dtype), part.shape),
        value,
        identity,
    )

    def turn(k, before):
        at = size - 1 - k if reverse else k
        reached = at > position if reverse else at < position
        new = combine(before, jax.tree.map(lambda part: part[at], everything))
        return jax.tree.map(lambda a, b: jnp.where(reached, a, b), new, before)

    return lax.fori_loop(0, size, turn, start)


def silu_slope(values):
    sigmoid = jax.nn.sigmoid(values)
    return sigmoid * (1.0 + values * (1.0 - sigmoid))


def compose(earlier_part, later_part):
    return (earlier_part[0] * later_part[0], later_part[1] + later_part[0] * earlier_part[1])


def regroup(values):
    row_count, local_len, last_width = values.shape
    return jnp.moveaxis(values.reshape(row_count, local_len // BLOCK, BLOCK, last_width), 1, 0)


def run_blocks(step_size, conv_vals, input_coef, output_coef, decay_full, state_in):
    row_count, local_len, inner_width = step_size.shape
    decay_rate = -jnp.exp(decay_full)

    def one_block(state_now, block_items):
        step_block, value_block, input_block, output_block = block_items
        outputs = []
        for offset in range(BLOCK):
            factor = jnp.exp(step_block[:, offset, None, :] * decay_rate)
            drive_term = (step_block[:, offset] * value_block[:, offset])[:, None, :] * input_block[
                :, offset, :, None
            ]
            state_now = factor * state_now + drive_term
            outputs.append(jnp.sum(output_block[:, offset, :, None] * state_now, axis=1))
        return (state_now, jnp.stack(outputs, axis=1))

    _, produced = lax.scan(
        jax.checkpoint(one_block),
        state_in,
        (regroup(step_size), regroup(conv_vals), regroup(input_coef), regroup(output_coef)),
    )
    return jnp.moveaxis(produced, 0, 1).reshape(row_count, local_len, inner_width)


def chain_terms(step_size, conv_vals, input_coef, decay_full):
    decay_rate = -jnp.exp(decay_full)
    total_step = jnp.sum(step_size, axis=1)
    remaining = total_step[:, None, :] - jnp.cumsum(step_size, axis=1)

    def add_block(state_sum, block_items):
        remain_block, step_block, value_block, input_block = block_items
        weights_now = jnp.exp(remain_block[:, :, None, :] * decay_rate)
        drive_term = (step_block * value_block)[:, :, None, :] * input_block[:, :, :, None]
        return (state_sum + jnp.sum(weights_now * drive_term, axis=1), None)

    state_zero = jnp.zeros((step_size.shape[0],) + decay_rate.shape, jnp.float32)
    local_state, _ = lax.scan(
        jax.checkpoint(add_block),
        state_zero,
        (regroup(remaining), regroup(step_size), regroup(conv_vals), regroup(input_coef)),
    )
    return (local_state, jnp.exp(total_step[:, None, :] * decay_rate))


def local(
    hidden,
    grad_out,
    lengths,
    norm_gain,
    input_weight,
    conv_weight,
    conv_bias,
    select_weight,
    step_weight,
    step_bias,
    decay_log,
    skip_weight,
    output_weight,
):
    gathered = (
        lax.all_gather(norm_gain, "seq", axis=0, tiled=True),
        lax.all_gather(input_weight, "seq", axis=0, tiled=True),
        lax.all_gather(conv_weight, "seq", axis=1, tiled=True),
        lax.all_gather(conv_bias, "seq", axis=0, tiled=True),
        lax.all_gather(select_weight, "seq", axis=1, tiled=True),
        lax.all_gather(step_weight, "seq", axis=1, tiled=True),
        lax.all_gather(step_bias, "seq", axis=0, tiled=True),
        lax.all_gather(decay_log, "seq", axis=1, tiled=True),
        lax.all_gather(skip_weight, "seq", axis=0, tiled=True),
        lax.all_gather(output_weight, "seq", axis=0, tiled=True),
    )
    gain_full = gathered[0].astype(jnp.float32)
    proj_in = gathered[1]
    conv_taps = gathered[2].astype(jnp.float32)
    conv_shift = gathered[3].astype(jnp.float32)
    proj_select = gathered[4]
    proj_step = gathered[5]
    step_shift = gathered[6].astype(jnp.float32)
    decay_full = gathered[7].astype(jnp.float32)
    skip_full = gathered[8].astype(jnp.float32)
    proj_out = gathered[9]
    row_count, local_len, model_width = hidden.shape
    inner_width = proj_out.shape[0]
    tap_count = conv_taps.shape[0]
    rank_width = proj_step.shape[0]
    state_width = decay_full.shape[0]
    positions = lax.axis_index("seq") * local_len + lax.broadcasted_iota(
        jnp.int32, (row_count, local_len), 1
    )
    valid_mask = (positions < lengths[:, None]).astype(jnp.float32)[..., None]
    source = hidden.astype(jnp.float32)
    inverse = lax.rsqrt(jnp.mean(source * source, axis=-1, keepdims=True) + EPSILON)
    normed = (source * inverse * gain_full).astype(jnp.bfloat16)
    projected = jnp.einsum("rtd,df->rtf", normed, proj_in, preferred_element_type=jnp.float32)
    conv_input = projected[..., :inner_width].astype(jnp.bfloat16)
    gate_input = projected[..., inner_width:]
    rim_rows = from_behind(conv_input[:, local_len - tap_count + 1 :, :], "seq", 1)
    extended = jnp.concatenate([rim_rows, conv_input], axis=1).astype(jnp.float32)
    conv_sum = conv_shift + sum(
        (
            conv_taps[tap_index] * extended[:, tap_index : tap_index + local_len, :]
            for tap_index in range(tap_count)
        )
    )
    conv_low = jax.nn.silu(conv_sum).astype(jnp.bfloat16)
    conv_vals = conv_low.astype(jnp.float32)
    selected = jnp.einsum("rte,ce->rtc", conv_low, proj_select, preferred_element_type=jnp.float32)
    step_low = selected[..., :rank_width].astype(jnp.bfloat16)
    input_coef = selected[..., rank_width : rank_width + state_width]
    output_coef = selected[..., rank_width + state_width :]
    step_pre = (
        jnp.einsum("rtk,ke->rte", step_low, proj_step, preferred_element_type=jnp.float32)
        + step_shift
    )
    step_size = jax.nn.softplus(step_pre)
    (local_state, decay_total), chain_back = jax.vjp(
        chain_terms, step_size, conv_vals, input_coef, decay_full
    )
    carried = prefix(
        (decay_total, local_state),
        "seq",
        compose,
        (jnp.ones_like(decay_total), jnp.zeros_like(local_state)),
        False,
    )
    state_in = carried[1]
    scanned, scan_back = jax.vjp(
        run_blocks, step_size, conv_vals, input_coef, output_coef, decay_full, state_in
    )
    ssm_out = scanned + skip_full * conv_vals
    gate_act = jax.nn.silu(gate_input)
    gated_low = (ssm_out * gate_act).astype(jnp.bfloat16)
    mixed_out = jnp.einsum("rte,ed->rtd", gated_low, proj_out, preferred_element_type=jnp.float32)
    output = ((source + mixed_out) * valid_mask).astype(jnp.bfloat16)
    cotangent = grad_out.astype(jnp.float32) * valid_mask
    grad_mixed = cotangent.astype(jnp.bfloat16)
    regathered = (
        lax.all_gather(norm_gain, "seq", axis=0, tiled=True),
        lax.all_gather(input_weight, "seq", axis=0, tiled=True),
        lax.all_gather(conv_weight, "seq", axis=1, tiled=True),
        lax.all_gather(select_weight, "seq", axis=1, tiled=True),
        lax.all_gather(step_weight, "seq", axis=1, tiled=True),
        lax.all_gather(skip_weight, "seq", axis=0, tiled=True),
        lax.all_gather(output_weight, "seq", axis=0, tiled=True),
    )
    gain_back = regathered[0].astype(jnp.float32)
    in_back = regathered[1]
    taps_back = regathered[2].astype(jnp.float32)
    select_back = regathered[3]
    step_back = regathered[4]
    skip_back = regathered[5].astype(jnp.float32)
    out_back = regathered[6]
    out_term = jnp.einsum("rte,rtd->ed", gated_low, grad_mixed, preferred_element_type=jnp.float32)
    grad_gated = jnp.einsum("rtd,ed->rte", grad_mixed, out_back, preferred_element_type=jnp.float32)
    grad_ssm = grad_gated * gate_act
    grad_gate = grad_gated * ssm_out * silu_slope(gate_input)
    skip_term = jnp.sum(grad_ssm * conv_vals, axis=(0, 1))
    scan_steps, scan_values, scan_inputs, scan_outputs, scan_decay, scan_state = scan_back(grad_ssm)
    returned = prefix(
        (decay_total, scan_state),
        "seq",
        compose,
        (jnp.ones_like(decay_total), jnp.zeros_like(scan_state)),
        True,
    )
    state_grad = returned[1]
    chain_steps, chain_values, chain_inputs, chain_decay = chain_back(
        (state_grad, state_grad * state_in)
    )
    grad_pre = ((scan_steps + chain_steps) * jax.nn.sigmoid(step_pre)).astype(jnp.bfloat16)
    step_term = jnp.einsum("rtk,rte->ke", step_low, grad_pre, preferred_element_type=jnp.float32)
    step_bias_term = jnp.sum(grad_pre.astype(jnp.float32), axis=(0, 1))
    grad_rank = jnp.einsum("rte,ke->rtk", grad_pre, step_back, preferred_element_type=jnp.float32)
    grad_selected = jnp.concatenate(
        [grad_rank, scan_inputs + chain_inputs, scan_outputs], axis=-1
    ).astype(jnp.bfloat16)
    select_term = jnp.einsum(
        "rtc,rte->ce", grad_selected, conv_low, preferred_element_type=jnp.float32
    )
    grad_vals = (
        grad_ssm * skip_back
        + scan_values
        + chain_values
        + jnp.einsum("rtc,ce->rte", grad_selected, select_back, preferred_element_type=jnp.float32)
    )
    grad_conv = grad_vals * silu_slope(conv_sum)
    conv_bias_term = jnp.sum(grad_conv, axis=(0, 1))
    taps_term = jnp.stack(
        [
            jnp.sum(grad_conv * extended[:, tap_index : tap_index + local_len, :], axis=(0, 1))
            for tap_index in range(tap_count)
        ]
    )
    grad_extended = sum(
        (
            jnp.pad(
                taps_back[tap_index] * grad_conv,
                ((0, 0), (tap_index, tap_count - 1 - tap_index), (0, 0)),
            )
            for tap_index in range(tap_count)
        )
    )
    sent_back = from_behind(
        grad_extended[:, : tap_count - 1, :].astype(jnp.bfloat16), "seq", -1
    ).astype(jnp.float32)
    grad_input = grad_extended[:, tap_count - 1 :, :] + jnp.pad(
        sent_back, ((0, 0), (local_len - tap_count + 1, 0), (0, 0))
    )
    grad_projected = jnp.concatenate([grad_input, grad_gate], axis=-1).astype(jnp.bfloat16)
    in_term = jnp.einsum("rtd,rtf->df", normed, grad_projected, preferred_element_type=jnp.float32)
    grad_normed = jnp.einsum(
        "rtf,df->rtd", grad_projected, in_back, preferred_element_type=jnp.float32
    )
    scaled_grad = grad_normed * gain_back
    grad_hidden = (
        inverse * scaled_grad
        - source * inverse**3 * jnp.mean(scaled_grad * source, axis=-1, keepdims=True)
        + cotangent
    )
    gain_term = jnp.sum(grad_normed * source * inverse, axis=(0, 1))
    decay_term = scan_decay + chain_decay
    shares = (
        lax.psum_scatter(gain_term, "seq", scatter_dimension=0, tiled=True),
        lax.psum_scatter(in_term, "seq", scatter_dimension=0, tiled=True),
        lax.psum_scatter(taps_term, "seq", scatter_dimension=1, tiled=True),
        lax.psum_scatter(conv_bias_term, "seq", scatter_dimension=0, tiled=True),
        lax.psum_scatter(select_term, "seq", scatter_dimension=1, tiled=True),
        lax.psum_scatter(step_term, "seq", scatter_dimension=1, tiled=True),
        lax.psum_scatter(step_bias_term, "seq", scatter_dimension=0, tiled=True),
        lax.psum_scatter(decay_term, "seq", scatter_dimension=1, tiled=True),
        lax.psum_scatter(skip_term, "seq", scatter_dimension=0, tiled=True),
        lax.psum_scatter(out_term, "seq", scatter_dimension=0, tiled=True),
    )
    totals = lax.psum(
        (
            shares[0],
            shares[1],
            shares[2],
            shares[3],
            shares[4],
            shares[5],
            shares[6],
            shares[7],
            shares[8],
            shares[9],
        ),
        "dp",
    )
    return (
        output,
        grad_hidden,
        totals[0],
        totals[1],
        totals[2],
        totals[3],
        totals[4],
        totals[5],
        totals[6],
        totals[7],
        totals[8],
        totals[9],
    )


def solution(mesh):
    return jax.shard_map(
        local,
        mesh=mesh,
        in_specs=(
            P("dp", "seq", None),
            P("dp", "seq", None),
            P("dp"),
            P("seq"),
            P("seq", None),
            P(None, "seq"),
            P("seq"),
            P(None, "seq"),
            P(None, "seq"),
            P("seq"),
            P(None, "seq"),
            P("seq"),
            P("seq", None),
        ),
        out_specs=(
            P("dp", "seq", None),
            P("dp", "seq", None),
            P("seq"),
            P("seq", None),
            P(None, "seq"),
            P("seq"),
            P(None, "seq"),
            P(None, "seq"),
            P("seq"),
            P(None, "seq"),
            P("seq"),
            P("seq", None),
        ),
        check_vma=False,
    )
```

profile of v0, /device:TPU:0, one launch (start us, length us, event | category | flops | bytes accessed | tf_op | source)
XLA Modules:
  0.0 3985.2 jit_solution(16613098918659256102)
XLA Ops:
  11.0 62.5 %all-gather.3 = bf16[8,1,256]{2,1,0:T(2,128)(2,1)S(1)} all-gather(bf16[1,1,256]{2,1,0:T(2,128)(2,1)S(1)} %reshape.698), channel_id=1, replica_groups=mesh['dp'=4,'seq'=8] {'seq'}, dimensions={0}, use_global_device_ids=true | all-gather | bytes 4608 | tf_op jit(solution)/shard_map/all_gather | solution.py:110
  73.5 44.9 %all_gather.56 = bf16[4,4096]{1,0:T(4,128)(2,1)S(1)} all-gather(bf16[4,512]{1,0:T(4,128)(2,1)S(1)} %copy-done.55), channel_id=1, replica_groups=mesh['dp'=4,'seq'=8] {'seq'}, dimensions={1}, use_global_device_ids=true | all-gather | bytes 36864 | tf_op jit(solution)/shard_map/all_gather | solution.py:112
  118.6 47.0 %all_gather.62 = bf16[16,4096]{1,0:T(8,128)(2,1)S(1)} all-gather(bf16[16,512]{1,0:T(8,128)(2,1)S(1)} %copy-done.43), channel_id=1, replica_groups=mesh['dp'=4,'seq'=8] {'seq'}, dimensions={1}, use_global_device_ids=true | all-gather | bytes 147456 | tf_op jit(solution)/shard_map/all_gather | solution.py:117
  166.4 486.8 %all-gather.14.cloned.1.call-done = bf16[2048,8192]{1,0:T(8,128)(2,1)} async-done(((bf16[256,8192]{1,0:T(8,128)(2,1)}), bf16[2048,8192]{1,0:T(8,128)(2,1)}) %all-gather.14.cloned.1.call-update) | async-done | bytes 33554448 | tf_op jit(solution)/shard_map/all_gather | solution.py:111
  653.2 18.9 fusion.82
  674.4 32.6 all-gather.2
  707.1 27.7 all-gather.4
  739.3 145.0 %all-gather.22.cloned.1.call-done = bf16[4096,2048]{1,0:T(8,128)(2,1)} async-done(((bf16[512,2048]{1,0:T(8,128)(2,1)}), bf16[4096,2048]{1,0:T(8,128)(2,1)}) %all-gather.22.cloned.1.call-update) | async-done | bytes 16777232 | tf_op jit(solution)/shard_map/all_gather | solution.py:119
  884.2 22.0 multiply_reduce_fusion.101
  908.9 17.1 all-gather.16.cloned.1.call-done
  928.5 37.2 all-gather.18.cloned.1.call-done
  988.8 27.8 while.107
  1040.3 49.1 %all-gather.24.cloned.1.call-done = f32[16,16,4096]{2,1,0:T(8,128)} async-done(((f32[2,16,4096]{2,1,0:T(8,128)}), f32[16,16,4096]{2,1,0:T(8,128)}) %all-gather.24.cloned.1.call-update) | async-done | bytes 4194320 | tf_op jit(solution)/shard_map/all_gather | solution.py:20
  1089.4 73.3 %all-gather.20.cloned.1.call-done = f32[8,2,16,4096]{3,2,1,0:T(8,128)} async-done(((f32[1,2,16,4096]{3,2,1,0:T(8,128)}), f32[8,2,16,4096]{3,2,1,0:T(8,128)}) %all-gather.20.cloned.1.call-update) | async-done | bytes 4194320 | tf_op jit(solution)/shard_map/all_gather | solution.py:20
  1162.7 13.9 while.108
  1181.6 125.6 %while.106 = (s32[]{:T(128)}, f32[2,16,4096]{2,1,0:T(8,128)S(1)}, f32[8,2,16,4096]{3,2,1,0:T(8,128)}, f32[8,2,16,4096]{3,2,1,0:T(8,128)}, f32[8,2,16,4096]{3,1,2...) while((s32[]{:T(128)}, f32[2,16,4096]{2,1,0:T(8,128)S(1)}, ...), condition=%wide.region_25.26_spmd, body=%wide.region_8.25_spmd.sunk | while | flops 18874368 | bytes 18241652 | solution.py:66
  1315.9 198.2 %while.109 = (s32[]{:T(128)}, f32[16,4096]{1,0:T(8,128)}, f32[2,16,4096]{2,1,0:T(8,128)S(1)}, f32[8,2,16,4096]{3,1,2,0:T(2,128)}, f32[8,2,16,4096]{3,1,2,0:T(2,1...) while((s32[]{:T(128)}, f32[16,4096]{1,0:T(8,128)}, ...), condition=%wide.region_107.108_spmd.clone, body=%wide.region_26.107_spmd.clone.sunk | while | flops 62732292 | bytes 50186764 | solution.py:66
  1521.6 64.8 %all-gather.26.cloned.1.call-done = f32[16,16,4096]{2,1,0:T(8,128)} async-done(((f32[2,16,4096]{2,1,0:T(8,128)}), f32[16,16,4096]{2,1,0:T(8,128)}) %all-gather.26.cloned.1.call-update) | async-done | bytes 4194320 | tf_op jit(solution)/shard_map/all_gather | solution.py:20
  1586.4 13.5 while.110
  1607.5 97.2 %while.111 = (s32[]{:T(128)}, f32[16,4096]{1,0:T(8,128)S(1)}, f32[2,16,4096]{2,1,0:T(8,128)S(1)}, f32[8,2,16,4096]{3,2,0,1:T(8,128)}, f32[8,2,16,4096]{3,2,1,0:T...) while((s32[]{:T(128)}, f32[16,4096]{1,0:T(8,128)S(1)}, ...), condition=%wide.region_115.116_spmd.clone, body=%wide.region_110.115_spmd.clone.sunk | while | flops 27459076 | bytes 12361915 | solution.py:86
  1711.9 130.6 %reduce_window_sum.26 = f32[2,128,4096]{2,1,0:T(8,128)} reduce-window(f32[2,128,4096]{2,1,0:T(8,128)} %bitcast.794, f32[]{:T(128)} %constant.225.clone.1), window={size=1x128x1 pad=0_0x0_127x0_0}, to_apply=%region_116.117 | reduce-window | flops 133169152 | bytes 8388612 | tf_op jit(solution)/shard_map/transpose(jvp(jit(cumsum)))/reduce_window_sum | solution.py:77
  1857.8 26.3 all-gather.5
  1901.8 17.8 convolution_bitcast_fusion.1
  1920.9 14.3 multiply_reduce_fusion.105
  1950.8 25.9 convolution_bitcast_fusion
  1979.9 14.4 reduce-scatter.11.cloned.1.call-done
  1994.3 541.8 %reduce-scatter.17.cloned.1.call-done = f32[512,2048]{1,0:T(8,128)} async-done(((f32[4096,2048]{1,0:T(8,128)}), f32[512,2048]{1,0:T(8,128)}) %reduce-scatter.17.cloned.1.call-update) | async-done | bytes 4194320 | tf_op jit(solution)/shard_map/reduce_scatter | solution.py:281
  2536.1 1061.4 %reduce-scatter.9.cloned.1.call-done = f32[256,8192]{1,0:T(8,128)} async-done(((f32[2048,8192]{1,0:T(8,128)}), f32[256,8192]{1,0:T(8,128)}) %reduce-scatter.9.cloned.1.call-update) | async-done | bytes 8388624 | tf_op jit(solution)/shard_map/reduce_scatter | solution.py:273
  3611.8 16.5 fusion.56
  3628.2 34.6 all-reduce.89
  3671.1 63.9 %reduce-scatter.15.cloned.1.call-done = f32[16,512]{1,0:T(8,128)} async-done(((f32[16,4096]{1,0:T(8,128)}), f32[16,512]{1,0:T(8,128)}) %reduce-scatter.15.cloned.1.call-update) | async-done | bytes 32784 | tf_op jit(solution)/shard_map/reduce_scatter | solution.py:279
  3747.3 219.8 %all-reduce.94.cloned.1.call-done = (f32[256,8192]{1,0:T(8,128)}, f32[160,512]{1,0:T(8,128)}, f32[128,512]{1,0:T(8,128)}, f32[512,2048]{1,0:T(8,128)}) async-done(((f32[256,8192]{1,0:T(8,128)}, f32[160,512]{1,0:T(8,128)}, f32[128,512]{1,0:T(8,128)}, f32[512,2048]{1,0:T(8,128)}), (f32[256,8192]{1,0:T(8,128)}, f32[160,512]{1,0:T(8,128)}, f32[128,512]{1,0:T(8,128)}, ...) | async-done | bytes 13172752 | tf_op jit(solution)/shard_map/psum | solution.py:283
  (899 shorter events, 668.1 us)
Async XLA Ops:
  7.2 66.3 %copy-start.55 = (bf16[4,512]{1,0:T(4,128)(2,1)S(1)}, bf16[4,512]{1,0:T(4,128)(2,1)}, u32[]{:S(2)}) copy-start(bf16[4,512]{1,0:T(4,128)(2,1)} %param.30) | copy-start | bytes 12292
  7.2 111.3 %copy-start.43 = (bf16[16,512]{1,0:T(8,128)(2,1)S(1)}, bf16[16,512]{1,0:T(8,128)(2,1)}, u32[]{:S(2)}) copy-start(bf16[16,512]{1,0:T(8,128)(2,1)} %param.35) | copy-start | bytes 49156
  7.2 645.9 %all-gather.14.cloned.1.call-start = ((), (), s32[]{:S(2)}) async-start(), calls=%async_computation.6 | async-start | bytes 37748736 | tf_op jit(solution)/shard_map/all_gather | solution.py:111
  8.0 876.3 %all-gather.22.cloned.1.call-start = ((), (), s32[]{:S(2)}) async-start(), calls=%async_computation.10 | async-start | bytes 18874368 | tf_op jit(solution)/shard_map/all_gather | solution.py:119
  8.7 917.3 %all-gather.16.cloned.1.call-start = ((), (), s32[]{:S(2)}) async-start(), calls=%async_computation.7 | async-start | bytes 1474560 | tf_op jit(solution)/shard_map/all_gather | solution.py:114
  9.4 956.3 %all-gather.18.cloned.1.call-start = ((), (), s32[]{:S(2)}) async-start(), calls=%async_computation.8 | async-start | bytes 1179648 | tf_op jit(solution)/shard_map/all_gather | solution.py:115
  10.0 1079.4 %all-gather.24.cloned.1.call-start = ((), (), s32[]{:S(2)}) async-start(), calls=%async_computation.16 | async-start | bytes 4718592 | tf_op jit(solution)/shard_map/all_gather | solution.py:20
  10.9 661.1 %copy-start.41 = (f32[2,128]{1,0:T(2,128)}, f32[2,128]{1,0:T(2,128)S(1)}, u32[]{:S(2)}) copy-start(f32[2,128]{1,0:T(2,128)S(1)} %get-tuple-element.1666) | copy-start | bytes 3076
  73.5 598.6 %copy-start.30 = (f32[8,1,256]{2,1,0:T(1,128)}, f32[8,1,256]{2,1,0:T(1,128)S(1)}, u32[]{:S(2)}) copy-start(f32[8,1,256]{2,1,0:T(1,128)S(1)} %convert_element_type.96) | copy-start | bytes 24580
  118.5 765.7 %copy-start.45 = (f32[1,4096]{1,0:T(1,128)}, f32[1,4096]{1,0:T(1,128)S(1)}, u32[]{:S(2)}) copy-start(f32[1,4096]{1,0:T(1,128)S(1)} %get-tuple-element.1660) | copy-start | bytes 49156
  118.5 765.7 %copy-start.47 = (f32[1,4096]{1,0:T(1,128)}, f32[1,4096]{1,0:T(1,128)S(1)}, u32[]{:S(2)}) copy-start(f32[1,4096]{1,0:T(1,128)S(1)} %get-tuple-element.1661) | copy-start | bytes 49156
  118.5 765.7 %copy-start.49 = (f32[1,4096]{1,0:T(1,128)}, f32[1,4096]{1,0:T(1,128)S(1)}, u32[]{:S(2)}) copy-start(f32[1,4096]{1,0:T(1,128)S(1)} %get-tuple-element.1662) | copy-start | bytes 49156
  118.6 765.7 %copy-start.51 = (f32[1,4096]{1,0:T(1,128)}, f32[1,4096]{1,0:T(1,128)S(1)}, u32[]{:S(2)}) copy-start(f32[1,4096]{1,0:T(1,128)S(1)} %get-tuple-element.1663) | copy-start | bytes 49156
  165.6 506.5 %copy-start.28 = (bf16[16,4096]{1,0:T(8,128)(2,1)}, bf16[16,4096]{1,0:T(8,128)(2,1)S(1)}, u32[]{:S(2)}) copy-start(bf16[16,4096]{1,0:T(8,128)(2,1)S(1)} %all_gather.62) | copy-start | bytes 393220
  653.2 53.9 %copy-start.58 = (bf16[512]{0:T(512)(128)(2,1)S(1)}, bf16[512]{0:T(512)(128)(2,1)}, u32[]{:S(2)}) copy-start(bf16[512]{0:T(512)(128)(2,1)} %param.34) | copy-start | bytes 3076
  673.0 63.5 %collective-permute-start = (bf16[2,3,4096]{2,1,0:T(4,128)(2,1)S(1)}, bf16[2,3,4096]{2,1,0:T(4,128)(2,1)S(1)}, u32[]{:S(2)}, u32[]{:S(2)}) collective-permute-start(bf16[2,3,4096]{2,1,0:T(4,128)(2,1)S(1)} %slice.1069), channel_id=1, source_target_pairs={{0,1},{1,2},{2,3},{3,4},{4,5},{5,6},{6,7},{8,9},{9,10},{10,11},{11... | collective-permute-start | bytes 147464 | tf_op jit(solution)/shard_map/ppermute | solution.py:15
  674.4 209.8 %copy-start.53 = (f32[2,128]{1,0:T(2,128)}, f32[2,128]{1,0:T(2,128)S(1)}, u32[]{:S(2)}) copy-start(f32[2,128]{1,0:T(2,128)S(1)} %compare_convert_fusion) | copy-start | bytes 3076
  928.2 44.2 %copy-start.26 = (f32[2,128,160]{1,2,0:T(8,128)}, f32[2,128,160]{1,2,0:T(8,128)S(1)}, u32[]{:S(2)}) copy-start(f32[2,128,160]{1,2,0:T(8,128)S(1)} %fusion.59) | copy-start | bytes 491524
  972.4 45.1 %copy-start.33 = (f32[2,4096]{1,0:T(2,128)}, f32[2,4096]{1,0:T(2,128)S(1)}, u32[]{:S(2)}) copy-start(f32[2,4096]{1,0:T(2,128)S(1)} %get-tuple-element.1457) | copy-start | bytes 98308
  1017.4 145.3 %all-gather.20.cloned.1.call-start = ((), (), s32[]{:S(2)}) async-start(), calls=%async_computation.9 | async-start | bytes 4718592 | tf_op jit(solution)/shard_map/all_gather | solution.py:20
  1018.4 568.0 %all-gather.26.cloned.1.call-start = ((), (), s32[]{:S(2)}) async-start(), calls=%async_computation.17 | async-start | bytes 4718592 | tf_op jit(solution)/shard_map/all_gather | solution.py:20
  1514.9 465.0 %reduce-scatter.13.cloned.1.call-start = ((), (), s32[]{:S(2)}) async-start(), calls=%async_computation.13 | async-start | bytes 2359296 | tf_op jit(solution)/shard_map/reduce_scatter | solution.py:277
  1852.6 141.7 %reduce-scatter.11.cloned.1.call-start = ((), (), s32[]{:S(2)}) async-start(), calls=%async_computation.12 | async-start | bytes 2949120 | tf_op jit(solution)/shard_map/reduce_scatter | solution.py:276
  1857.8 678.3 %reduce-scatter.17.cloned.1.call-start = ((), (), s32[]{:S(2)}) async-start(), calls=%async_computation.15 | async-start | bytes 37748736 | tf_op jit(solution)/shard_map/reduce_scatter | solution.py:281
  1919.6 1677.9 %reduce-scatter.9.cloned.1.call-start = ((), (), s32[]{:S(2)}) async-start(), calls=%async_computation.11 | async-start | bytes 75497472 | tf_op jit(solution)/shard_map/reduce_scatter | solution.py:273
  1942.3 6.7 collective-permute-start.1
  1976.8 1693.2 %reduce-scatter.19.cloned.1.call-start = ((), (), s32[]{:S(2)}) async-start(), calls=%async_computation.18 | async-start | bytes 2359296
  1979.0 1756.1 %reduce-scatter.15.cloned.1.call-start = ((), (), s32[]{:S(2)}) async-start(), calls=%async_computation.14 | async-start | bytes 294912 | tf_op jit(solution)/shard_map/reduce_scatter | solution.py:279
  1979.8 1987.3 %all-reduce.94.cloned.1.call-start = ((), (), s32[]{:S(2)}) async-start(), calls=%async_computation.19 | async-start | bytes 26345472 | tf_op jit(solution)/shard_map/psum | solution.py:283
  3611.7 51.4 %copy-start.17 = (bf16[2,128,2048]{2,1,0:T(8,128)(2,1)S(1)}, bf16[2,128,2048]{2,1,0:T(8,128)(2,1)}, u32[]{:S(2)}) copy-start(bf16[2,128,2048]{2,1,0:T(8,128)(2,1)} %param.25) | copy-start | bytes 3145732
  3611.8 51.4 %copy-start.24 = (bf16[2,128,2048]{2,1,0:T(8,128)(2,1)S(1)}, bf16[2,128,2048]{2,1,0:T(8,128)(2,1)}, u32[]{:S(2)}) copy-start(bf16[2,128,2048]{2,1,0:T(8,128)(2,1)} %param.26) | copy-start | bytes 3145732
  3611.8 51.4 %copy-start.56 = (f32[2,128]{1,0:T(2,128)S(1)}, f32[2,128]{1,0:T(2,128)}, u32[]{:S(2)}) copy-start(f32[2,128]{1,0:T(2,128)} %get-tuple-element.1665) | copy-start | bytes 3076
  (61 other events, 343.9 us)
Sparse Core Ops, SparseCore 0:
  9.6 643.5 all-gather.13
  655.3 228.8 all-gather.21
  886.3 39.7 all-gather.15
  927.9 37.7 all-gather.17
  1017.6 71.7 all-gather.23
  1091.4 71.3 all-gather.19
  1515.1 71.3 all-gather.25
  1852.7 67.5 reduce-scatter.12
  1923.8 70.4 reduce-scatter.10
  1998.0 538.1 reduce-scatter.16
  2539.9 1057.5 reduce-scatter.8
  3601.4 68.5 reduce-scatter.18
  3674.0 61.0 reduce-scatter.14
  3737.7 229.4 all-reduce.93
where the time goes:
time: 4000 us; the launch traced here: 3990 us
  waiting for transfers between devices  2790 us (70%)
  other arithmetic  505 us (13%)
  blocking collectives  288 us (7%)
  local copies, waits for them, and re-layouts  244 us (6%)
  matrix products  138 us (3%)
    reduce_scatter x1, waiting for transfers between devices, local(): lax.psum_scatter(in_term, 'seq', scatter_dimension=0, tiled=True)  1060 us
    reduce_scatter x1, waiting for transfers between devices, local(): lax.psum_scatter(out_term, 'seq', scatter_dimension=0, tiled=True)  542 us
    all_gather x1, waiting for transfers between devices, local(): lax.all_gather(input_weight, 'seq', axis=0, tiled=True)  487 us
    psum x1, waiting for transfers between devices, local(): lax.psum((shares[0], shares[1], shares[2], shares[3], shares[4], shares[5...  220 us
    all_gather x3, waiting for transfers between devices, prefix(): everything = jax.tree.map(lambda part: lax.all_gather(part, axis), value)  187 us
    all_gather x1, waiting for transfers between devices, local(): lax.all_gather(output_weight, 'seq', axis=0, tiled=True)  145 us
    another operation x2, other arithmetic, chain_terms(): remaining = total_step[:, None, :] - jnp.cumsum(step_size, axis=1)  137 us
    reduce_sum x64, other arithmetic, one_block(): factor = jnp.exp(step_block[:, offset, None, :] * decay_rate)  103 us
  transfers between devices with their start and end apart: 16, of which 14 were waited for; matrix products, arithmetic and copies ran while one was open for 5% of the time, Pallas kernels for 0%

commit v1 on v0

v1 whole, which is shorter than its diff:
```python
import functools
import jax
import jax.numpy as jnp
from jax import lax
from jax.experimental import pallas as pl
from jax.experimental.pallas import tpu as pltpu

BLOCK = 16
LOG2E = 1.4426950408889634
F32 = jnp.float32
BF16 = jnp.bfloat16


def softplus(v):
    return jnp.maximum(v, 0.0) + jnp.log(1.0 + jnp.exp(-jnp.abs(v)))


def sigmoid(v):
    return 1.0 / (1.0 + jnp.exp(-v))


def nt_dot(a, b):
    return lax.dot_general(a, b, (((1,), (1,)), ((), ())), preferred_element_type=F32)


def tile_matrix(n, wide):
    col = lax.broadcasted_iota(jnp.int32, (n, wide), 1)
    row = lax.broadcasted_iota(jnp.int32, (n, wide), 0)
    return (col % n == row).astype(F32)


def diagonal_mask(rows, n, wide):
    col = lax.broadcasted_iota(jnp.int32, (rows, wide), 1)
    row = lax.broadcasted_iota(jnp.int32, (rows, wide), 0)
    return col // n == row % BLOCK


def scan_forward_kernel(sel_ref, x_ref, gate_ref, stepw_ref, bias_ref, decay_ref, skip_ref,
                        gated_ref, ssm_ref, start_ref,
                        dt_s, u_s, y_s, coef_s, bt_s, hist_s, state_s, *, rank, n):
    chunk = pl.program_id(1)
    length = x_ref.shape[-2]
    wide = BLOCK * n

    @pl.when(chunk == 0)
    def _():
        state_s[...] = jnp.zeros_like(state_s)

    start_ref[...] = state_s[...].reshape(start_ref.shape)
    selected = sel_ref[...].reshape(sel_ref.shape[-2:])
    x = x_ref[...].reshape(x_ref.shape[-2:]).astype(F32)
    low = selected[:, :rank].astype(BF16)
    pre = jnp.dot(low, stepw_ref[...], preferred_element_type=F32) + bias_ref[...]
    dt = softplus(pre)
    dt_s[...] = dt
    u_s[...] = dt * x
    tail = selected[:, rank:]
    bt_s[...] = tail.T
    spread = jnp.dot(tail[:, n:], tile_matrix(n, wide), preferred_element_type=F32)
    coef_s[...] = jnp.where(diagonal_mask(length, n, wide), spread, 0.0).astype(BF16)
    rate = -jnp.exp(decay_ref[...].astype(F32)) * LOG2E

    def block(k, state):
        at = pl.multiple_of(k * BLOCK, BLOCK)
        dts = dt_s[pl.ds(at, BLOCK), :]
        us = u_s[pl.ds(at, BLOCK), :]
        bs = pltpu.roll(bt_s[0:n, :], length - at, 1)
        for i in range(BLOCK):
            factor = jnp.exp2(dts[i:i + 1, :] * rate)
            state = factor * state + us[i:i + 1, :] * bs[:, i:i + 1]
            hist_s[i * n:(i + 1) * n, :] = state.astype(BF16)
        y_s[pl.ds(at, BLOCK), :] = jnp.dot(coef_s[pl.ds(at, BLOCK), :], hist_s[...], preferred_element_type=F32)
        return state

    state_s[...] = lax.fori_loop(0, length // BLOCK, block, state_s[...])
    gate = gate_ref[...].reshape(x.shape)
    ssm = y_s[...] + skip_ref[...] * x
    ssm_ref[...] = ssm.astype(ssm_ref.dtype).reshape(ssm_ref.shape)
    gated_ref[...] = (ssm * gate * sigmoid(gate)).astype(BF16).reshape(gated_ref.shape)


def scan_forward(sel, x, gate, stepw, bias, decay, skip, n):
    chunks, rows, length, width = x.shape
    rank = stepw.shape[0]
    wide = BLOCK * n
    tok = lambda feat: pl.BlockSpec((1, 1, length, feat), lambda r, c: (c, r, 0, 0))
    whole = lambda a: pl.BlockSpec(a.shape, lambda r, c: (0,) * a.ndim)
    return pl.pallas_call(
        functools.partial(scan_forward_kernel, rank=rank, n=n),
        grid=(rows, chunks),
        in_specs=[tok(sel.shape[-1]), tok(width), tok(width), whole(stepw), whole(bias), whole(decay), whole(skip)],
        out_specs=[tok(width), tok(width), pl.BlockSpec((1, 1, n, width), lambda r, c: (c, r, 0, 0))],
        out_shape=[
            jax.ShapeDtypeStruct((chunks, rows, length, width), BF16),
            jax.ShapeDtypeStruct((chunks, rows, length, width), BF16),
            jax.ShapeDtypeStruct((chunks, rows, n, width), F32),
        ],
        scratch_shapes=[
            pltpu.VMEM((length, width), F32), pltpu.VMEM((length, width), F32), pltpu.VMEM((length, width), F32),
            pltpu.VMEM((length, wide), BF16), pltpu.VMEM((2 * n, length), F32),
            pltpu.VMEM((wide, width), BF16), pltpu.VMEM((n, width), F32),
        ],
        name="scan_forward",
    )(sel, x, gate, stepw, bias, decay, skip)


def scan_backward_kernel(sel_ref, x_ref, gate_ref, gg_ref, ssm_ref, start_ref, stepw_ref, bias_ref, decay_ref, skip_ref,
                         ggate_ref, gvals_ref, gpre_ref, gsel_ref, gstepw_ref, gbias_ref, gdecay_ref, gskip_ref,
                         dt_s, u_s, gy_s, gu_s, ah_s, bcoef_s, bt_s, hist_s, adj_s, harm_s, db_s, dc_s, carry_s, gd_s, *, rank, n):
    row, step = pl.program_id(0), pl.program_id(1)
    length = x_ref.shape[-2]
    wide = BLOCK * n
    blocks = length // BLOCK
    flat = lambda ref: ref[...].reshape(ref.shape[-2:])

    @pl.when(step == 0)
    def _():
        carry_s[...] = jnp.zeros_like(carry_s)

    @pl.when((step == 0) & (row == 0))
    def _():
        gstepw_ref[...] = jnp.zeros_like(gstepw_ref)
        gbias_ref[...] = jnp.zeros_like(gbias_ref)
        gskip_ref[...] = jnp.zeros_like(gskip_ref)
        gd_s[...] = jnp.zeros_like(gd_s)

    selected = flat(sel_ref)
    x = flat(x_ref).astype(F32)
    gate = flat(gate_ref)
    gg = flat(gg_ref)
    ssm = flat(ssm_ref).astype(F32)
    sg = sigmoid(gate)
    gy = gg * gate * sg
    ggate_ref[...] = (gg * ssm * sg * (1.0 + gate * (1.0 - sg))).astype(BF16).reshape(ggate_ref.shape)
    gskip_ref[...] += jnp.sum(gy * x, axis=0, keepdims=True)
    gy_s[...] = gy
    low = selected[:, :rank].astype(BF16)
    pre = jnp.dot(low, stepw_ref[...], preferred_element_type=F32) + bias_ref[...]
    dt = softplus(pre)
    dt_s[...] = dt
    u_s[...] = dt * x
    tail = selected[:, rank:]
    bt_s[...] = tail.T
    tiles = tile_matrix(n, wide)
    spread = jnp.dot(tail[:, :n], tiles, preferred_element_type=F32)
    bcoef_s[...] = jnp.where(diagonal_mask(length, n, wide), spread, 0.0).astype(BF16)
    decay = -jnp.exp(decay_ref[...].astype(F32))
    rate = decay * LOG2E
    keep = diagonal_mask(BLOCK, n, wide)
    ones = keep.astype(BF16)
    start = start_ref[...].reshape(carry_s.shape)

    def again(k, state):
        at = pl.multiple_of(k * BLOCK, BLOCK)
        dts = dt_s[pl.ds(at, BLOCK), :]
        us = u_s[pl.ds(at, BLOCK), :]
        bs = pltpu.roll(bt_s[0:n, :], length - at, 1)
        for i in range(BLOCK):
            hist_s[pl.ds(pl.multiple_of((at + i) * n, n), n), :] = state.astype(BF16)
            factor = jnp.exp2(dts[i:i + 1, :] * rate)
            state = factor * state + us[i:i + 1, :] * bs[:, i:i + 1]
        return state

    last = lax.fori_loop(0, blocks, again, start)
    hist_s[pl.ds(length * n, n), :] = last.astype(BF16)

    def back(j, carried):
        carry, gd = carried
        k = blocks - 1 - j
        at = pl.multiple_of(k * BLOCK, BLOCK)
        dts = dt_s[pl.ds(at, BLOCK), :]
        gys = gy_s[pl.ds(at, BLOCK), :]
        cs = pltpu.roll(bt_s[n:2 * n, :], length - at, 1)
        for i in range(BLOCK - 1, -1, -1):
            dt_i = dts[i:i + 1, :]
            g = cs[:, i:i + 1] * gys[i:i + 1, :] + carry
            adj_s[i * n:(i + 1) * n, :] = g.astype(BF16)
            carry = jnp.exp2(dt_i * rate) * g
            h = carry * hist_s[pl.ds(pl.multiple_of((at + i) * n, n), n), :].astype(F32)
            harm_s[i * n:(i + 1) * n, :] = (h * decay).astype(BF16)
            gd = gd + dt_i * h
        adj = adj_s[...]
        rows = pl.ds(at, BLOCK)
        gu_s[rows, :] = jnp.dot(bcoef_s[rows, :], adj, preferred_element_type=F32)
        ah_s[rows, :] = jnp.dot(ones, harm_s[...], preferred_element_type=F32)
        db_s[rows, :] = jnp.where(keep, nt_dot(u_s[rows, :].astype(BF16), adj), 0.0)
        states = hist_s[pl.ds(pl.multiple_of((at + 1) * n, n), wide), :]
        dc_s[rows, :] = jnp.where(keep, nt_dot(gys.astype(BF16), states), 0.0)
        return carry, gd

    carry, gd = lax.fori_loop(0, blocks, back, (carry_s[...], gd_s[...]))
    carry_s[...] = carry
    gd_s[...] = gd
    gu = gu_s[...]
    gpre = ((x * gu + ah_s[...]) * sigmoid(pre)).astype(BF16)
    gpre_ref[...] = gpre.reshape(gpre_ref.shape)
    gvals_ref[...] = (gy * skip_ref[...] + dt * gu).astype(gvals_ref.dtype).reshape(gvals_ref.shape)
    gbias_ref[...] += jnp.sum(gpre.astype(F32), axis=0, keepdims=True)
    gstepw_ref[...] += jnp.dot(selected[:, :rank].T.astype(BF16), gpre, preferred_element_type=F32)
    fold = lambda ref: lax.dot_general(ref[...], tiles, (((1,), (1,)), ((), ())), preferred_element_type=F32, precision=lax.Precision.HIGHEST)
    lead = (0,) * (len(gsel_ref.shape) - 2)
    gsel_ref[lead + (slice(None), slice(0, rank))] = nt_dot(gpre, stepw_ref[...])
    gsel_ref[lead + (slice(None), slice(rank, rank + n))] = fold(db_s)
    gsel_ref[lead + (slice(None), slice(rank + n, rank + 2 * n))] = fold(dc_s)

    @pl.when((row == pl.num_programs(0) - 1) & (step == pl.num_programs(1) - 1))
    def _():
        gdecay_ref[...] = gd * decay


def scan_backward(sel, x, gate, gg, ssm, starts, stepw, bias, decay, skip, n):
    chunks, rows, length, width = x.shape
    rank = stepw.shape[0]
    wide = BLOCK * n
    at = lambda r, c: (chunks - 1 - c, r, 0, 0)
    tok = lambda feat: pl.BlockSpec((1, 1, length, feat), at)
    whole = lambda shape: pl.BlockSpec(shape, lambda r, c: (0,) * len(shape))
    sds = jax.ShapeDtypeStruct
    return pl.pallas_call(
        functools.partial(scan_backward_kernel, rank=rank, n=n),
        grid=(rows, chunks),
        in_specs=[tok(sel.shape[-1]), tok(width), tok(width), tok(width), tok(width), pl.BlockSpec((1, 1, n, width), at),
                  whole(stepw.shape), whole(bias.shape), whole(decay.shape), whole(skip.shape)],
        out_specs=[tok(width), tok(width), tok(width), tok(sel.shape[-1]), whole((rank, width)), whole((1, width)), whole((n, width)), whole((1, width))],
        out_shape=[
            sds(x.shape, BF16), sds(x.shape, F32), sds(x.shape, BF16), sds(sel.shape, F32),
            sds((rank, width), F32), sds((1, width), F32), sds((n, width), F32), sds((1, width), F32),
        ],
        scratch_shapes=[
            pltpu.VMEM((length, width), F32), pltpu.VMEM((length, width), F32), pltpu.VMEM((length, width), F32),
            pltpu.VMEM((length, width), F32), pltpu.VMEM((length, width), F32),
            pltpu.VMEM((length, wide), BF16), pltpu.VMEM((2 * n, length), F32),
            pltpu.VMEM(((length + 1) * n, width), BF16), pltpu.VMEM((wide, width), BF16), pltpu.VMEM((wide, width), BF16),
            pltpu.VMEM((length, wide), F32), pltpu.VMEM((length, wide), F32),
            pltpu.VMEM((n, width), F32), pltpu.VMEM((n, width), F32),
        ],
        name="scan_backward",
    )(sel, x, gate, gg, ssm, starts, stepw, bias, decay, skip)
def conv_forward_kernel(ci_ref, taps_ref, bias_ref, selw_ref, x_ref, sel_ref, ext_s):
    length = ci_ref.shape[-2]
    tap_count = taps_ref.shape[0]

    @pl.when(pl.program_id(1) == 0)
    def _():
        ext_s[0:8, :] = jnp.zeros((8, ext_s.shape[1]), F32)

    ext_s[8:, :] = ci_ref[...].reshape(ci_ref.shape[-2:]).astype(F32)
    total = bias_ref[...].astype(F32)
    for k in range(tap_count):
        total = total + taps_ref[k:k + 1, :].astype(F32) * ext_s[pl.ds(8 - tap_count + 1 + k, length), :]
    ext_s[0:8, :] = ext_s[length:length + 8, :]
    x = (total * sigmoid(total)).astype(BF16)
    x_ref[...] = x.reshape(x_ref.shape)
    sel_ref[...] = nt_dot(x, selw_ref[...]).reshape(sel_ref.shape)


def conv_forward(ci, taps, bias, selw):
    chunks, rows, length, width = ci.shape
    tok = lambda feat: pl.BlockSpec((1, 1, length, feat), lambda r, c: (c, r, 0, 0))
    whole = lambda a: pl.BlockSpec(a.shape, lambda r, c: (0,) * a.ndim)
    return pl.pallas_call(
        conv_forward_kernel,
        grid=(rows, chunks),
        in_specs=[tok(width), whole(taps), whole(bias), whole(selw)],
        out_specs=[tok(width), tok(selw.shape[0])],
        out_shape=[jax.ShapeDtypeStruct(ci.shape, BF16), jax.ShapeDtypeStruct((chunks, rows, length, selw.shape[0]), F32)],
        scratch_shapes=[pltpu.VMEM((length + 8, width), F32)],
        name="conv_forward",
    )(ci, taps, bias, selw)


def conv_backward_kernel(ci_ref, prev_ref, gvals_ref, gsel_ref, taps_ref, bias_ref, selw_ref,
                         gci_ref, gtaps_ref, gbias_ref, gselw_ref, ext_s, gext_s):
    row, step = pl.program_id(0), pl.program_id(1)
    length = ci_ref.shape[-2]
    tap_count = taps_ref.shape[0]
    flat = lambda ref: ref[...].reshape(ref.shape[-2:])

    @pl.when(step == 0)
    def _():
        gext_s[length:, :] = jnp.zeros((8, gext_s.shape[1]), F32)

    @pl.when((step == 0) & (row == 0))
    def _():
        gtaps_ref[...] = jnp.zeros_like(gtaps_ref)
        gbias_ref[...] = jnp.zeros_like(gbias_ref)
        gselw_ref[...] = jnp.zeros_like(gselw_ref)

    first = step == pl.num_programs(1) - 1
    ext_s[8:, :] = flat(ci_ref).astype(F32)
    before = flat(prev_ref)[length - 16:, :].astype(F32)[8:, :]
    ext_s[0:8, :] = jnp.where(first, 0.0, before)
    total = bias_ref[...].astype(F32)
    for k in range(tap_count):
        total = total + taps_ref[k:k + 1, :].astype(F32) * ext_s[pl.ds(8 - tap_count + 1 + k, length), :]
    sg = sigmoid(total)
    x = (total * sg).astype(BF16)
    gsel = flat(gsel_ref).astype(BF16)
    gvals = flat(gvals_ref) + jnp.dot(gsel, selw_ref[...], preferred_element_type=F32)
    gconv = gvals * sg * (1.0 + total * (1.0 - sg))
    gbias_ref[...] += jnp.sum(gconv, axis=0, keepdims=True)
    for k in range(tap_count):
        gtaps_ref[k:k + 1, :] += jnp.sum(gconv * ext_s[pl.ds(8 - tap_count + 1 + k, length), :], axis=0, keepdims=True)
    gselw_ref[...] += jnp.dot(flat(gsel_ref).T.astype(BF16), x, preferred_element_type=F32)
    gext_s[0:length, :] = gconv
    gci = jnp.zeros_like(gconv)
    for k in range(tap_count):
        gci = gci + taps_ref[k:k + 1, :].astype(F32) * gext_s[pl.ds(tap_count - 1 - k, length), :]
    gci_ref[...] = gci.astype(BF16).reshape(gci_ref.shape)
    gext_s[length:, :] = gconv[0:8, :]


def conv_backward(ci, gvals, gsel, taps, bias, selw):
    chunks, rows, length, width = ci.shape
    at = lambda r, c: (chunks - 1 - c, r, 0, 0)
    before = lambda r, c: (jnp.maximum(chunks - 2 - c, 0), r, 0, 0)
    tok = lambda feat, where: pl.BlockSpec((1, 1, length, feat), where)
    whole = lambda shape: pl.BlockSpec(shape, lambda r, c: (0,) * len(shape))
    sds = jax.ShapeDtypeStruct
    return pl.pallas_call(
        conv_backward_kernel,
        grid=(rows, chunks),
        in_specs=[tok(width, at), tok(width, before), tok(width, at), tok(gsel.shape[-1], at), whole(taps.shape), whole(bias.shape), whole(selw.shape)],
        out_specs=[tok(width, at), whole(taps.shape), whole(bias.shape), whole(selw.shape)],
        out_shape=[sds(ci.shape, BF16), sds(taps.shape, F32), sds(bias.shape, F32), sds(selw.shape, F32)],
        scratch_shapes=[pltpu.VMEM((length + 8, width), F32), pltpu.VMEM((length + 8, width), F32)],
        name="conv_backward",
    )(ci, ci, gvals, gsel, taps, bias, selw)
from jax.sharding import PartitionSpec as P

EPSILON = 1e-05


def local(hidden, grad_out, lengths, norm_gain, input_weight, conv_weight, conv_bias, select_weight,
          step_weight, step_bias, decay_log, skip_weight, output_weight):
    rows, length, model = hidden.shape
    chunks = lax.axis_size("seq")
    copies = lax.axis_size("dp")
    width = output_weight.shape[0]
    share = input_weight.shape[0]
    rank = step_weight.shape[0]
    n = decay_log.shape[0]
    tokens = chunks * rows * length
    here = lax.axis_index("seq")

    hidden_all = lax.all_gather(hidden, "seq", axis=0)
    gain_all = lax.all_gather(norm_gain, "seq", axis=0, tiled=True).astype(F32)
    blocks = input_weight.reshape(share, 2, chunks, width)
    blocks = lax.all_to_all(blocks, "seq", split_axis=2, concat_axis=0, tiled=False)
    w_conv = blocks[:, :, 0].reshape(model, width)
    w_gate = blocks[:, :, 1].reshape(model, width)
    slots = here * length + lax.broadcasted_iota(jnp.int32, (rows, length), 1)
    valid = (slots < lengths[:, None]).astype(F32)[..., None]
    cotangent = grad_out.astype(F32) * valid
    gm = lax.all_gather(cotangent.astype(BF16), "seq", axis=0).reshape(tokens, model)

    source_all = hidden_all.reshape(tokens, model).astype(F32)
    inverse_all = lax.rsqrt(jnp.mean(source_all * source_all, axis=-1, keepdims=True) + EPSILON)
    normed = (source_all * inverse_all * gain_all).astype(BF16)
    shaped = lambda a: a.reshape(chunks, rows, length, a.shape[-1])
    ci = shaped(jnp.dot(normed, w_conv, preferred_element_type=F32).astype(BF16))
    gate = shaped(jnp.dot(normed, w_gate, preferred_element_type=F32))
    bias_row = conv_bias.reshape(1, width)
    x, partial = conv_forward(ci, conv_weight, bias_row, select_weight)
    sel = lax.psum(partial, "seq")
    step_row = step_bias.reshape(1, width)
    skip_row = skip_weight.reshape(1, width)
    gated, ssm, starts = scan_forward(sel, x, gate, step_weight, step_row, decay_log, skip_row, n)
    gated2 = gated.reshape(tokens, width)
    mixed = jnp.dot(gated2, output_weight, preferred_element_type=F32).astype(BF16)
    mixed = lax.psum_scatter(shaped(mixed), "seq", scatter_dimension=0, tiled=False)
    source = hidden.astype(F32)
    output = ((source + mixed.astype(F32)) * valid).astype(BF16)

    gg = shaped(lax.dot_general(gm, output_weight, (((1,), (1,)), ((), ())), preferred_element_type=F32))
    ggate, gvals, gpre, gpart, gstepw, gstepb, gdecay, gskip = scan_backward(
        sel, x, gate, gg, ssm, starts, step_weight, step_row, decay_log, skip_row, n)
    gsel = lax.psum(gpart, "seq")
    tn = lambda a, b: lax.dot_general(a, b, (((0,), (0,)), ((), ())), preferred_element_type=F32)
    gout = tn(gated2, gm)
    gci, gtaps, gconvb, gselw = conv_backward(ci, gvals, gsel, conv_weight, bias_row, select_weight)
    gci2 = gci.reshape(tokens, width)
    ggate2 = ggate.reshape(tokens, width)
    gin = jnp.stack([tn(normed, gci2).astype(BF16), tn(normed, ggate2).astype(BF16)], axis=1)
    gin = gin.reshape(chunks, copies, share // copies, 2, width)
    gin = lax.psum_scatter(gin, "dp", scatter_dimension=1, tiled=False)
    gin = lax.all_to_all(gin, "seq", split_axis=0, concat_axis=2, tiled=False)
    gin = lax.all_gather(gin.reshape(share // copies, 2 * chunks * width), "dp", axis=0, tiled=True).astype(F32)
    both = lambda g, w: lax.dot_general(g, w, (((1,), (1,)), ((), ())), preferred_element_type=F32)
    gnormed = (both(gci2, w_conv) + both(ggate2, w_gate)).astype(BF16)
    gnormed = lax.psum_scatter(shaped(gnormed), "seq", scatter_dimension=0, tiled=False).astype(F32)
    inverse = lax.rsqrt(jnp.mean(source * source, axis=-1, keepdims=True) + EPSILON)
    scaled = gnormed * gain_all
    ghidden = inverse * scaled - source * inverse ** 3 * jnp.mean(scaled * source, axis=-1, keepdims=True) + cotangent
    ggain = jnp.sum(gnormed * source * inverse, axis=(0, 1))
    ggain = lax.psum(ggain, ("dp", "seq"))
    ggain = lax.dynamic_slice(ggain, (here * share,), (share,))
    gtaps, gconvb, gselw, gstepw, gstepb, gdecay, gskip, gout = lax.psum(
        (gtaps, gconvb, gselw, gstepw, gstepb, gdecay, gskip, gout), "dp")
    return (output, ghidden, ggain, gin, gtaps, gconvb.reshape(width), gselw, gstepw, gstepb.reshape(width),
            gdecay, gskip.reshape(width), gout)


def solution(mesh):
    tok, vec, col, row = P("dp", "seq", None), P("seq"), P(None, "seq"), P("seq", None)
    return jax.shard_map(
        local,
        mesh=mesh,
        in_specs=(tok, tok, P("dp"), vec, row, col, vec, col, col, vec, col, vec, row),
        out_specs=(tok, tok, vec, row, col, vec, col, col, vec, col, vec, row),
        check_vma=False,
    )
```

time: 4000 us -> 1320 us (0.33)
  waiting for transfers between devices: 2790 us -> 729 us
  other arithmetic: 505 us -> 33.1 us
  local copies, waits for them, and re-layouts: 244 us -> 34.7 us
  Pallas kernels: 0 us -> 197 us
  blocking collectives: 288 us -> 205 us
  matrix products: 138 us -> 90.5 us
    reduce_scatter x5 -> x2, waiting for transfers between devices: 1680 us -> 226 us  [the longest x1 121 us: local(): lax.psum_scatter(shaped(gnormed), 'seq', scatter_dimension=0, tiled=False)]
    all_gather x7 -> x3, waiting for transfers between devices: 873 us -> 86.8 us  [the longest x1 79.1 us: local(): lax.all_gather(cotangent.astype(BF16), 'seq', axis=0).reshape(tokens, model)]
    reduce_sum x123 -> x2, other arithmetic: 227 us -> 6.95 us  [the longest x1 5.09 us: local(): jnp.mean(source_all * source_all, axis=-1, keepdims=True) + EPSILON]
    pallas_call x0 -> x4, Pallas kernels: none -> 197 us  [the longest x1 118 us: scan_backward(): pl.pallas_call(functools.partial(scan_backward_kernel, rank=rank, n=n), g...]
    another operation x13 -> x1, other arithmetic: 147 us -> 2.38 us  [local(): jnp.stack([tn(normed, gci2).astype(BF16), tn(normed, ggate2).astype(BF16)...]
    all_gather x6 -> x1, blocking collectives: 241 us -> 120 us  [local(): gain_all = lax.all_gather(norm_gain, 'seq', axis=0, tiled=True).astype(F32)]
    squeeze x88 -> x0, local copies, waits for them, and re-layouts: 87 us -> none  [chain_terms(): lax.scan(jax.checkpoint(add_block), state_zero, (regroup(remaining), regr...]
    unnamed x15 -> x10, waiting for transfers between devices: 5.97 us -> 84.5 us
  transfers between devices with their start and end apart: 16 -> 10, of which waited for: 14 -> 9; matrix products, arithmetic and copies ran while one was open for 5% -> 10% of each run, Pallas kernels for 0% -> 1%
where the time goes in v1:
time: 1320 us; the launch traced here: 1310 us
  waiting for transfers between devices  729 us (55%)
  blocking collectives  205 us (16%)
  Pallas kernels  197 us (15%)
  matrix products  90.5 us (7%)
  local copies, waits for them, and re-layouts  34.7 us (3%)
  other arithmetic  33.1 us (3%)
  between operations  14.3 us (1%)
    reduce_scatter x1, waiting for transfers between devices, local(): lax.psum_scatter(shaped(gnormed), 'seq', scatter_dimension=0, tiled=False)  121 us
    all_gather x1, blocking collectives, local(): gain_all = lax.all_gather(norm_gain, 'seq', axis=0, tiled=True).astype(F32)  120 us
    pallas_call x1, Pallas kernels, scan_backward(): pl.pallas_call(functools.partial(scan_backward_kernel, rank=rank, n=n), g...  118 us
    reduce_scatter x1, waiting for transfers between devices, local(): lax.psum_scatter(shaped(mixed), 'seq', scatter_dimension=0, tiled=False)  106 us
    psum x1, waiting for transfers between devices, local(): sel = lax.psum(partial, 'seq')  94.5 us
    psum x1, waiting for transfers between devices, local(): lax.psum((gtaps, gconvb, gselw, gstepw, gstepb, gdecay, gskip, gout), 'dp')  93.3 us
    psum x1, waiting for transfers between devices, local(): gsel = lax.psum(gpart, 'seq')  91.4 us
    unnamed x10, waiting for transfers between devices  84.5 us
  transfers between devices with their start and end apart: 10, of which 9 were waited for; matrix products, arithmetic and copies ran while one was open for 10% of the time, Pallas kernels for 1%

profile of v1, /device:TPU:0, one launch (start us, length us, event | category | flops | bytes accessed | tf_op | source)
XLA Modules:
  0.0 1312.3 jit_solution(15034553575328597148)
XLA Ops:
  11.2 6.4 copy.39
  17.5 6.5 copy.40
  24.0 7.5 all-to-all-start
  33.4 119.6 %all-gather.2 = bf16[8,1,256]{2,1,0:T(2,128)(2,1)S(1)} all-gather(bf16[1,1,256]{2,1,0:T(2,128)(2,1)S(1)} %reshape.192), channel_id=1, replica_groups=mesh['dp'=4,'seq'=8] {'seq'}, dimensions={0}, use_global_device_ids=true | all-gather | bytes 4608 | tf_op jit(solution)/shard_map/all_gather | solution.py:347
  153.0 52.1 %all-to-all-done = bf16[1,256,2,8,512]{4,1,2,0,3:T(8,128)(2,1)} async-done(((bf16[1,256,2,8,512]{4,1,2,0,3:T(8,128)(2,1)}), bf16[1,256,2,8,512]{4,1,2,0,3:T(8,128)(2,1)}, u32[]{:S(2)}, u32[]{:S(2)}) %all-to-all-start) | async-done | bytes 4194336 | tf_op jit(solution)/shard_map/all_to_all | solution.py:349
  209.8 7.6 all-gather.9.cloned.1.call-done
  217.5 5.1 fusion
  222.6 9.0 fusion.2
  231.6 9.2 convolution_convert_fusion.1
  240.8 12.5 conv_forward.1
  253.6 10.5 fusion.17.gate_ref
  264.1 79.1 %all-gather.11.cloned.1.call-done = bf16[16,128,2048]{2,1,0:T(8,128)(2,1)} async-done(((bf16[2,128,2048]{2,1,0:T(8,128)(2,1)}), bf16[16,128,2048]{2,1,0:T(8,128)(2,1)}) %all-gather.11.cloned.1.call-update) | async-done | bytes 8388624 | tf_op jit(solution)/shard_map/all_gather | solution.py:355
  343.2 9.6 fusion.13.gg_ref
  352.8 94.5 %all-reduce.8.cloned.1.call-done.sel_ref = f32[8,2,128,160]{3,2,1,0:T(8,128)} async-done(((f32[8,2,128,160]{3,2,1,0:T(8,128)}), f32[8,2,128,160]{3,2,1,0:T(8,128)}) %all-reduce.8.cloned.1.call-update) | async-done | bytes 1310736 | tf_op jit(solution)/shard_map/psum | solution.py:365
  447.3 49.2 %scan_forward.1 = (bf16[8,2,128,512]{3,2,1,0:T(8,128)(2,1)}, bf16[8,2,128,512]{3,2,1,0:T(8,128)(2,1)}, f32[8,2,16,512]{3,2,1,0:T(8,128)}) custom-call(f32[8,2,128,160]{3,2,1,0:T(8,128)} %all-reduce.8.cloned.1.call-done.sel_ref, bf16[8,2,128,512]{3,2,1,0:T(8,128)(2,1)} %get-tuple-element.29.x_ref, f32[8,2,128,512]{3,2,1,0:T(8,128)} %fusion.17.gate_ref, ...), custom_call_target="tpu_custom_call" | custom-call | tf_op jit(solution)/shard_map/scan_forward/pallas_call | solution.py:88
  496.5 117.7 %scan_backward.1 = (bf16[8,2,128,512]{3,2,1,0:T(8,128)(2,1)}, f32[8,2,128,512]{3,2,1,0:T(8,128)}, bf16[8,2,128,512]{3,2,1,0:T(8,128)(2,1)}, f32[8,2,128,160]{3,2...) custom-call(f32[8,2,128,160]{3,2,1,0:T(8,128)} %all-reduce.8.cloned.1.call-done.sel, ...), custom_call_target="tpu_custom_call" | custom-call | tf_op jit(solution)/shard_map/scan_backward/pallas_call | solution.py:219
  614.7 9.9 bitcast_convert_fusion
  624.6 91.4 %all-reduce.10.cloned.1.call-done.gsel_ref = f32[8,2,128,160]{3,2,1,0:T(8,128)} async-done(((f32[8,2,128,160]{3,2,1,0:T(8,128)}), f32[8,2,128,160]{3,2,1,0:T(8,128)}) %all-reduce.10.cloned.1.call-update) | async-done | bytes 1310736 | tf_op jit(solution)/shard_map/psum | solution.py:378
  716.0 17.2 %conv_backward.1 = (bf16[8,2,128,512]{3,2,1,0:T(8,128)(2,1)}, f32[4,512]{1,0:T(4,128)}, f32[1,512]{1,0:T(1,128)}, f32[160,512]{1,0:T(8,128)}) custom-call(bf16[8,2,128,512]{3,2,1,0:T(8,128)(2,1)} %bitcast.91, bf16[8,2,128,512]{3,2,1,0:T(8,128)(2,1)} %bitcast.92, f32[8,2,128,512]{3,2,1,0:T(8,128)} %get-tuple-element.33.gvals_ref, ...), custom_call_target="tpu_custom_call" | custom-call | tf_op jit(solution)/shard_map/conv_backward/pallas_call | solution.py:320
  733.2 8.7 bitcast_convert_fusion.1
  745.5 83.7 %all-reduce.12.cloned.1.call-done = bf16[8,4,64,2,512]{4,2,1,0,3:T(8,128)(2,1)} async-done(((bf16[8,4,64,2,512]{4,2,1,0,3:T(8,128)(2,1)}), bf16[8,4,64,2,512]{4,2,1,0,3:T(8,128)(2,1)}) %all-reduce.12.cloned.1.call-update) | async-done | bytes 4194320
  831.3 30.8 %all_to_all.30 = bf16[8,64,2,1,512]{4,1,2,3,0:T(8,128)(2,1)S(1)} all-to-all(bf16[8,64,2,1,512]{4,1,2,3,0:T(8,128)(2,1)S(1)} %copy.43), channel_id=1, replica_groups=mesh['dp'=4,'seq'=8] {'seq'}, dimensions={0} | all-to-all | bytes 2097152 | tf_op jit(solution)/shard_map/all_to_all | solution.py:387
  864.2 12.8 fusion.18
  877.0 10.9 add_convert_fusion
  887.9 8.4 convolution_convert_fusion
  896.6 10.6 convolution_bitcast_fusion
  909.1 11.9 all-reduce.1
  921.0 6.6 convert_element_type.87
  927.6 120.6 %reduce-scatter.8.cloned.1.call-done = bf16[1,2,128,2048]{3,2,1,0:T(8,128)(2,1)} async-done(((bf16[8,2,128,2048]{3,2,1,0:T(8,128)(2,1)}), bf16[1,2,128,2048]{3,2,1,0:T(8,128)(2,1)}) %reduce-scatter.8.cloned.1.call-update) | async-done | bytes 1048592 | tf_op jit(solution)/shard_map/reduce_scatter | solution.py:391
  1050.0 43.1 %psum.79 = f32[2048]{0:T(1024)S(1)} all-reduce(f32[2048]{0:T(1024)S(1)} %get-tuple-element.44), channel_id=1, replica_groups=mesh['dp'=4,'seq'=8] {'dp','seq'}, use_global_device_ids=true, to_apply=%region_8.0 | all-reduce | flops 2048 | bytes 16384 | tf_op jit(solution)/shard_map/psum | solution.py:396
  1093.8 105.7 %reduce-scatter.6.cloned.1.call-done = bf16[1,2,128,2048]{3,2,1,0:T(8,128)(2,1)} async-done(((bf16[8,2,128,2048]{3,2,1,0:T(8,128)(2,1)}), bf16[1,2,128,2048]{3,2,1,0:T(8,128)(2,1)}) %reduce-scatter.6.cloned.1.call-update) | async-done | bytes 1048592 | tf_op jit(solution)/shard_map/reduce_scatter | solution.py:371
  1204.1 93.3 %all-reduce.14.cloned.1.call-done = (f32[160,512]{1,0:T(8,128)}, f32[128,512]{1,0:T(8,128)}, f32[512,2048]{1,0:T(8,128)}) async-done(((f32[160,512]{1,0:T(8,128)}, f32[128,512]{1,0:T(8,128)}, f32[512,2048]{1,0:T(8,128)}), (f32[160,512]{1,0:T(8,128)}, f32[128,512]{1,0:T(8,128)}, f32[512,2048]{1,0:T(8,128)})) %all-reduce.14.cloned.1.call-update) | async-done | bytes 4784144 | tf_op jit(solution)/shard_map/psum | solution.py:398
  (74 shorter events, 36.3 us)
Async XLA Ops:
  7.2 336.0 %copy-start = (bf16[512,2048]{1,0:T(8,128)(2,1)S(1)}, bf16[512,2048]{1,0:T(8,128)(2,1)}, u32[]{:S(2)}) copy-start(bf16[512,2048]{1,0:T(8,128)(2,1)} %param.25) | copy-start | bytes 6291460
  7.2 210.3 %all-gather.9.cloned.1.call-start = ((), (), s32[]{:S(2)}) async-start(), calls=%async_computation.9 | async-start | bytes 9437184 | tf_op jit(solution)/shard_map/all_gather | solution.py:346
  7.9 335.3 %all-gather.11.cloned.1.call-start = ((), (), s32[]{:S(2)}) async-start(), calls=%async_computation.10 | async-start | bytes 9437184 | tf_op jit(solution)/shard_map/all_gather | solution.py:355
  24.0 7.6 copy-start.13
  24.0 7.6 copy-start.10
  24.0 8.2 copy-start.11
  24.0 8.8 copy-start.12
  24.0 181.1 %all-to-all-start = ((bf16[1,256,2,8,512]{4,1,2,0,3:T(8,128)(2,1)}), bf16[1,256,2,8,512]{4,1,2,0,3:T(8,128)(2,1)}, u32[]{:S(2)}, u32[]{:S(2)}) async-start(bf16[1,256,2,8,512]{4,1,2,0,3:T(8,128)(2,1)} %copy.40), calls=%async_computation | async-start | bytes 8388608 | tf_op jit(solution)/shard_map/all_to_all | solution.py:349
  31.6 415.7 %all-reduce.8.cloned.1.call-start = ((), (), s32[]{:S(2)}) async-start(), calls=%async_computation.4 | async-start | bytes 4194304 | tf_op jit(solution)/shard_map/psum | solution.py:365
  222.6 9.1 copy-start.3
  253.3 462.7 %all-reduce.10.cloned.1.call-start = ((), (), s32[]{:S(2)}) async-start(), calls=%async_computation.6 | async-start | bytes 4194304 | tf_op jit(solution)/shard_map/psum | solution.py:378
  614.3 214.9 %all-reduce.12.cloned.1.call-start = ((), (), s32[]{:S(2)}) async-start(), calls=%async_computation.11 | async-start | bytes 8388608
  733.2 8.7 copy-start.4
  744.2 0.7 copy-start.14
  744.3 176.7 %all-gather.7.cloned.1.call-start = ((), (), s32[]{:S(2)}) async-start(), calls=%async_computation.8 | async-start | bytes 5242880 | tf_op jit(solution)/shard_map/all_gather | solution.py:388
  864.0 184.2 %reduce-scatter.8.cloned.1.call-start = ((), (), s32[]{:S(2)}) async-start(), calls=%async_computation.7 | async-start | bytes 9437184 | tf_op jit(solution)/shard_map/reduce_scatter | solution.py:391
  864.2 12.8 copy-start.2
  887.9 311.6 %reduce-scatter.6.cloned.1.call-start = ((), (), s32[]{:S(2)}) async-start(), calls=%async_computation.5 | async-start | bytes 9437184 | tf_op jit(solution)/shard_map/reduce_scatter | solution.py:371
  896.3 401.1 %all-reduce.14.cloned.1.call-start = ((), (), s32[]{:S(2)}) async-start(), calls=%async_computation.12 | async-start | bytes 9568256 | tf_op jit(solution)/shard_map/psum | solution.py:398
  907.2 1.5 copy-start.1
  907.2 1.8 copy-start.5
  907.2 1.8 copy-start.6
  907.2 1.9 copy-start.7
  907.2 1.9 copy-start.8
  907.2 1.9 copy-start.9
Sparse Core Ops, SparseCore 0:
  10.1 207.3 all-gather.8
  220.2 122.9 all-gather.10
  346.8 100.4 all-reduce.7
  614.4 101.5 all-reduce.9
  744.4 84.7 all-reduce.11
  864.1 32.9 all-gather.6
  900.7 147.4 reduce-scatter.7
  1051.8 147.6 reduce-scatter.5
  1203.2 94.2 all-reduce.13

commit v2 on v1

--- a/solution.py
+++ b/solution.py
@@ -6,6 +6,7 @@
 from jax.experimental.pallas import tpu as pltpu
 
 BLOCK = 16
+EPSILON = 1e-05
 LOG2E = 1.4426950408889634
 F32 = jnp.float32
 BF16 = jnp.bfloat16
@@ -47,16 +48,15 @@
         state_s[...] = jnp.zeros_like(state_s)
 
     start_ref[...] = state_s[...].reshape(start_ref.shape)
-    selected = sel_ref[...].reshape(sel_ref.shape[-2:])
+    selected = sel_ref[...].reshape(sel_ref.shape[-2:]).astype(F32)
     x = x_ref[...].reshape(x_ref.shape[-2:]).astype(F32)
-    low = selected[:, :rank].astype(BF16)
+    low = selected[:rank].T.astype(BF16)
     pre = jnp.dot(low, stepw_ref[...], preferred_element_type=F32) + bias_ref[...]
     dt = softplus(pre)
     dt_s[...] = dt
     u_s[...] = dt * x
-    tail = selected[:, rank:]
-    bt_s[...] = tail.T
-    spread = jnp.dot(tail[:, n:], tile_matrix(n, wide), preferred_element_type=F32)
+    bt_s[...] = selected[rank:]
+    spread = jnp.dot(selected[rank:].T[:, n:], tile_matrix(n, wide), preferred_element_type=F32)
     coef_s[...] = jnp.where(diagonal_mask(length, n, wide), spread, 0.0).astype(BF16)
     rate = -jnp.exp(decay_ref[...].astype(F32)) * LOG2E
 
@@ -88,7 +88,7 @@
     return pl.pallas_call(
         functools.partial(scan_forward_kernel, rank=rank, n=n),
         grid=(rows, chunks),
-        in_specs=[tok(sel.shape[-1]), tok(width), tok(width), whole(stepw), whole(bias), whole(decay), whole(skip)],
+        in_specs=[pl.BlockSpec((1, 1) + sel.shape[2:], lambda r, c: (c, r, 0, 0)), tok(width), tok(width), whole(stepw), whole(bias), whole(decay), whole(skip)],
         out_specs=[tok(width), tok(width), pl.BlockSpec((1, 1, n, width), lambda r, c: (c, r, 0, 0))],
         out_shape=[
             jax.ShapeDtypeStruct((chunks, rows, length, width), BF16),
@@ -124,7 +124,7 @@
         gskip_ref[...] = jnp.zeros_like(gskip_ref)
         gd_s[...] = jnp.zeros_like(gd_s)
 
-    selected = flat(sel_ref)
+    selected = flat(sel_ref).astype(F32)
     x = flat(x_ref).astype(F32)
     gate = flat(gate_ref)
     gg = flat(gg_ref)
@@ -134,15 +134,14 @@
     ggate_ref[...] = (gg * ssm * sg * (1.0 + gate * (1.0 - sg))).astype(BF16).reshape(ggate_ref.shape)
     gskip_ref[...] += jnp.sum(gy * x, axis=0, keepdims=True)
     gy_s[...] = gy
-    low = selected[:, :rank].astype(BF16)
+    low = selected[:rank].T.astype(BF16)
     pre = jnp.dot(low, stepw_ref[...], preferred_element_type=F32) + bias_ref[...]
     dt = softplus(pre)
     dt_s[...] = dt
     u_s[...] = dt * x
-    tail = selected[:, rank:]
-    bt_s[...] = tail.T
+    bt_s[...] = selected[rank:]
     tiles = tile_matrix(n, wide)
-    spread = jnp.dot(tail[:, :n], tiles, preferred_element_type=F32)
+    spread = jnp.dot(selected[rank:].T[:, :n], tiles, preferred_element_type=F32)
     bcoef_s[...] = jnp.where(diagonal_mask(length, n, wide), spread, 0.0).astype(BF16)
     decay = -jnp.exp(decay_ref[...].astype(F32))
     rate = decay * LOG2E
@@ -196,12 +195,11 @@
     gpre_ref[...] = gpre.reshape(gpre_ref.shape)
     gvals_ref[...] = (gy * skip_ref[...] + dt * gu).astype(gvals_ref.dtype).reshape(gvals_ref.shape)
     gbias_ref[...] += jnp.sum(gpre.astype(F32), axis=0, keepdims=True)
-    gstepw_ref[...] += jnp.dot(selected[:, :rank].T.astype(BF16), gpre, preferred_element_type=F32)
-    fold = lambda ref: lax.dot_general(ref[...], tiles, (((1,), (1,)), ((), ())), preferred_element_type=F32, precision=lax.Precision.HIGHEST)
-    lead = (0,) * (len(gsel_ref.shape) - 2)
-    gsel_ref[lead + (slice(None), slice(0, rank))] = nt_dot(gpre, stepw_ref[...])
-    gsel_ref[lead + (slice(None), slice(rank, rank + n))] = fold(db_s)
-    gsel_ref[lead + (slice(None), slice(rank + n, rank + 2 * n))] = fold(dc_s)
+    gstepw_ref[...] += jnp.dot(selected[:rank].astype(BF16), gpre, preferred_element_type=F32)
+    fold = lambda ref: lax.dot_general(tiles, ref[...], (((1,), (1,)), ((), ())), preferred_element_type=F32, precision=lax.Precision.HIGHEST)
+    gsel_ref[0, 0, 0:rank, :] = nt_dot(stepw_ref[...], gpre).astype(BF16)
+    gsel_ref[0, 0, rank:rank + n, :] = fold(db_s).astype(BF16)
+    gsel_ref[0, 0, rank + n:rank + 2 * n, :] = fold(dc_s).astype(BF16)
 
     @pl.when((row == pl.num_programs(0) - 1) & (step == pl.num_programs(1) - 1))
     def _():
@@ -219,11 +217,11 @@
     return pl.pallas_call(
         functools.partial(scan_backward_kernel, rank=rank, n=n),
         grid=(rows, chunks),
-        in_specs=[tok(sel.shape[-1]), tok(width), tok(width), tok(width), tok(width), pl.BlockSpec((1, 1, n, width), at),
+        in_specs=[pl.BlockSpec((1, 1) + sel.shape[2:], at), tok(width), tok(width), tok(width), tok(width), pl.BlockSpec((1, 1, n, width), at),
                   whole(stepw.shape), whole(bias.shape), whole(decay.shape), whole(skip.shape)],
-        out_specs=[tok(width), tok(width), tok(width), tok(sel.shape[-1]), whole((rank, width)), whole((1, width)), whole((n, width)), whole((1, width))],
+        out_specs=[tok(width), tok(width), tok(width), pl.BlockSpec((1, 1) + sel.shape[2:], at), whole((rank, width)), whole((1, width)), whole((n, width)), whole((1, width))],
         out_shape=[
-            sds(x.shape, BF16), sds(x.shape, F32), sds(x.shape, BF16), sds(sel.shape, F32),
+            sds(x.shape, BF16), sds(x.shape, F32), sds(x.shape, BF16), sds(sel.shape, BF16),
             sds((rank, width), F32), sds((1, width), F32), sds((n, width), F32), sds((1, width), F32),
         ],
         scratch_shapes=[
@@ -251,19 +249,20 @@
     ext_s[0:8, :] = ext_s[length:length + 8, :]
     x = (total * sigmoid(total)).astype(BF16)
     x_ref[...] = x.reshape(x_ref.shape)
-    sel_ref[...] = nt_dot(x, selw_ref[...]).reshape(sel_ref.shape)
+    sel_ref[...] = nt_dot(selw_ref[...], x).astype(BF16).reshape(sel_ref.shape)
 
 
 def conv_forward(ci, taps, bias, selw):
     chunks, rows, length, width = ci.shape
     tok = lambda feat: pl.BlockSpec((1, 1, length, feat), lambda r, c: (c, r, 0, 0))
     whole = lambda a: pl.BlockSpec(a.shape, lambda r, c: (0,) * a.ndim)
+    coef = (selw.shape[0], length)
     return pl.pallas_call(
         conv_forward_kernel,
         grid=(rows, chunks),
         in_specs=[tok(width), whole(taps), whole(bias), whole(selw)],
-        out_specs=[tok(width), tok(selw.shape[0])],
-        out_shape=[jax.ShapeDtypeStruct(ci.shape, BF16), jax.ShapeDtypeStruct((chunks, rows, length, selw.shape[0]), F32)],
+        out_specs=[tok(width), pl.BlockSpec((1, 1) + coef, lambda r, c: (c, r, 0, 0))],
+        out_shape=[jax.ShapeDtypeStruct(ci.shape, BF16), jax.ShapeDtypeStruct((chunks, rows) + coef, BF16)],
         scratch_shapes=[pltpu.VMEM((length + 8, width), F32)],
         name="conv_forward",
     )(ci, taps, bias, selw)
@@ -295,13 +294,13 @@
         total = total + taps_ref[k:k + 1, :].astype(F32) * ext_s[pl.ds(8 - tap_count + 1 + k, length), :]
     sg = sigmoid(total)
     x = (total * sg).astype(BF16)
-    gsel = flat(gsel_ref).astype(BF16)
-    gvals = flat(gvals_ref) + jnp.dot(gsel, selw_ref[...], preferred_element_type=F32)
+    gsel = flat(gsel_ref)
+    gvals = flat(gvals_ref) + jnp.dot(gsel.astype(F32).T.astype(BF16), selw_ref[...], preferred_element_type=F32)
     gconv = gvals * sg * (1.0 + total * (1.0 - sg))
     gbias_ref[...] += jnp.sum(gconv, axis=0, keepdims=True)
     for k in range(tap_count):
         gtaps_ref[k:k + 1, :] += jnp.sum(gconv * ext_s[pl.ds(8 - tap_count + 1 + k, length), :], axis=0, keepdims=True)
-    gselw_ref[...] += jnp.dot(flat(gsel_ref).T.astype(BF16), x, preferred_element_type=F32)
+    gselw_ref[...] += jnp.dot(gsel, x, preferred_element_type=F32)
     gext_s[0:length, :] = gconv
     gci = jnp.zeros_like(gconv)
     for k in range(tap_count):
@@ -320,15 +319,685 @@
     return pl.pallas_call(
         conv_backward_kernel,
         grid=(rows, chunks),
-        in_specs=[tok(width, at), tok(width, before), tok(width, at), tok(gsel.shape[-1], at), whole(taps.shape), whole(bias.shape), whole(selw.shape)],
+        in_specs=[tok(width, at), tok(width, before), tok(width, at), pl.BlockSpec((1, 1) + gsel.shape[2:], at), whole(taps.shape), whole(bias.shape), whole(selw.shape)],
         out_specs=[tok(width, at), whole(taps.shape), whole(bias.shape), whole(selw.shape)],
         out_shape=[sds(ci.shape, BF16), sds(taps.shape, F32), sds(bias.shape, F32), sds(selw.shape, F32)],
         scratch_shapes=[pltpu.VMEM((length + 8, width), F32), pltpu.VMEM((length + 8, width), F32)],
         name="conv_backward",
     )(ci, ci, gvals, gsel, taps, bias, selw)
+MESH = pl.DeviceIdType.MESH
+
+
+def remote(src, dst, send, recv, device):
+    return pltpu.make_async_remote_copy(src_ref=src, dst_ref=dst, send_sem=send, recv_sem=recv, device_id=device, device_id_type=MESH)
+
+
+def grid_of(chunks, copies):
+    deep = max(1, copies // 2)
+    return (chunks // deep, deep) if chunks % deep == 0 else (chunks, 1)
+
+
+def meet(chunks, copies):
+    me, mine = lax.axis_index("seq"), lax.axis_index("dp")
+    barrier = pltpu.get_barrier_semaphore()
+
+    def greet(k, _):
+        pl.semaphore_signal(barrier, inc=1, device_id={"seq": lax.rem(me + k, chunks)}, device_id_type=MESH)
+        return 0
+
+    def greet_copy(k, _):
+        pl.semaphore_signal(barrier, inc=1, device_id={"dp": lax.rem(mine + k, copies)}, device_id_type=MESH)
+        return 0
+
+    lax.fori_loop(1, chunks, greet, 0)
+    if copies > 1:
+        lax.fori_loop(1, copies, greet_copy, 0)
+    pl.semaphore_wait(barrier, chunks - 1 + max(copies - 1, 0))
+
+
+def gather_project_kernel(hid_ref, wq_ref, gain_ref, n_ref, ci_ref, gate_ref, w_ref, row_ref,
+                          hid_v, gain_v, w_v, n_v, ci_v, gate_v,
+                          load_sem, out_sem, hrecv, hside, hup, hdown,
+                          w1send, w1recv, w2recv, w2send, w3send, gsend, grecv, *, chunks, copies, share, split):
+    zs, ys = grid_of(chunks, copies)
+    xs = copies // 2
+    me, mine = lax.axis_index("seq"), lax.axis_index("dp")
+    z, y = me // ys, me % ys
+    x, c = mine // 2, mine % 2
+    tokens, model = hid_v.shape[1:]
+    width = ci_v.shape[1]
+    inner = chunks * width
+    half = tokens // 2
+    piece = share // (copies if split else 1)
+    spot = mine if split else 0
+    load = pltpu.make_async_copy(hid_ref, hid_v.at[me], load_sem)
+    load.start()
+    meet(chunks, copies)
+    load.wait()
+
+    def w_rows(s, d):
+        return pl.ds(pl.multiple_of(s * share + d * piece, piece), piece)
+
+    def w_first(s, part):
+        src = wq_ref.at[pl.ds(pl.multiple_of(spot * piece, piece), piece), pl.ds(pl.multiple_of(part * inner + s * width, width), width)]
+        return remote(src, w_v.at[w_rows(me, spot), pl.ds(part * width, width)], w1send.at[s, part], w1recv.at[me, part], {"seq": s})
+
+    def w_landed(s, part):
+        dst = w_v.at[w_rows(s, spot), pl.ds(part * width, width)]
+        return remote(dst, dst, w1send.at[s, part], w1recv.at[s, part], {"seq": s})
+
+    def w_own(part):
+        src = wq_ref.at[pl.ds(pl.multiple_of(spot * piece, piece), piece), pl.ds(pl.multiple_of(part * inner + me * width, width), width)]
+        return pltpu.make_async_copy(src, w_v.at[w_rows(me, spot), pl.ds(part * width, width)], out_sem.at[part])
+
+    def every_other(fn):
+        def one(k, _):
+            fn(lax.rem(me + k, chunks))
+            return 0
+        lax.fori_loop(1, chunks, one, 0)
+
+    def gain_to(s):
+        return remote(gain_ref, gain_v.at[me], gsend.at[s], grecv.at[me], {"seq": s})
+
+    def gain_from(s):
+        return remote(gain_v.at[s], gain_v.at[s], gsend.at[s], grecv.at[s], {"seq": s})
+
+    def send_first(s):
+        gain_to(s).start()
+        w_first(s, 0).start()
+        w_first(s, 1).start()
+
+    def block(o, yy, h):
+        return hid_v.at[o * ys + yy, pl.ds(h * half, half)]
+
+    def up(o, h):
+        return remote(block(o, y, h), block(o, y, h), hup.at[o, h], hrecv.at[o * ys + y, h], {"seq": (z + 1) * ys + y})
+
+    def down(o, h):
+        return remote(block(o, y, h), block(o, y, h), hdown.at[o, h], hrecv.at[o * ys + y, h], {"seq": (z - 1) * ys + y})
+
+    def side(o, j, h):
+        other = lax.rem(y + j, ys)
+        return remote(block(o, y, h), block(o, y, h), hside.at[o, j - 1, h], hrecv.at[o * ys + y, h], {"seq": z * ys + other})
+
+    def landed(o, yy, h):
+        return remote(block(o, yy, h), block(o, yy, h), hside.at[o, 0, h], hrecv.at[o * ys + yy, h], {"seq": lax.rem(me + 1, chunks)})
+
+    def when(cond, fn):
+        pl.when(cond)(fn)
+
+    gain_own = pltpu.make_async_copy(gain_ref, gain_v.at[me], out_sem.at[2])
+    gain_own.start()
+    for part in range(2):
+        w_own(part).start()
+    for h in range(2):
+        when(z + 1 < zs, lambda: up(z, h).start())
+        when(z > 0, lambda: down(z, h).start())
+        for j in range(1, ys):
+            side(z, j, h).start()
+    every_other(send_first)
+
+    def relay(k):
+        for h in range(2):
+            @pl.when(z - k >= 0)
+            def _():
+                landed(z - k, y, h).wait_recv()
+                when(z + 1 < zs, lambda: up(z - k, h).start())
+                for j in range(1, ys):
+                    side(z - k, j, h).start()
+
+            @pl.when(z + k < zs)
+            def _():
+                landed(z + k, y, h).wait_recv()
+                when(z > 0, lambda: down(z + k, h).start())
+                for j in range(1, ys):
+                    side(z + k, j, h).start()
+
+    def shared(s, d, sems, k, device):
+        return remote(w_v.at[w_rows(s, d)], w_v.at[w_rows(s, d)], sems.at[s, k], w2recv.at[s, d], device)
+
+    def spread(s):
+        for j in range(1, xs):
+            shared(s, mine, w2send, j - 1, {"dp": lax.rem(x + j, xs) * 2 + c}).start()
+        shared(s, mine, w3send, 0, {"dp": x * 2 + 1 - c}).start()
+
+    gain_own.wait()
+    for part in range(2):
+        w_own(part).wait()
+    if split:
+        spread(me)
+
+    def take_first(s):
+        gain_from(s).wait_recv()
+        for part in range(2):
+            w_landed(s, part).wait_recv()
+        if split:
+            spread(s)
+
+    every_other(take_first)
+    if zs > 1:
+        relay(1)
+
+    def take_second(s, _):
+        for j in range(1, xs):
+            d = lax.rem(x + j, xs) * 2 + c
+            shared(s, d, w2send, j - 1, {"dp": d}).wait_recv()
+            shared(s, d, w3send, j, {"dp": x * 2 + 1 - c}).start()
+        return 0
+
+    def take_third(s, _):
+        for j in range(xs):
+            d = lax.rem(x + j, xs) * 2 + 1 - c
+            shared(s, d, w2send, 0, {"dp": d}).wait_recv()
+        return 0
+
+    if split:
+        lax.fori_loop(0, chunks, take_second, 0)
+    if zs > 2:
+        relay(2)
+    if split:
+        lax.fori_loop(0, chunks, take_third, 0)
+
+    row_ref[...] = jnp.concatenate([gain_v[s] for s in range(chunks)], axis=-1)
+    w_out = pltpu.make_async_copy(w_v, w_ref, load_sem)
+    w_out.start()
+    steps = 4 if width >= 512 else 1
+    tile = 2 * width // steps
+
+    def project(at):
+        def rows(i, _):
+            sl = pl.ds(pl.multiple_of(i * 32, 32), 32)
+            h = hid_v[at, sl, :].astype(F32)
+            inverse = lax.rsqrt(jnp.mean(h * h, axis=-1, keepdims=True) + EPSILON)
+            n_v[sl, :] = (h * inverse * row_ref[...]).astype(BF16)
+            return 0
+        lax.fori_loop(0, tokens // 32, rows, 0)
+        n_out = pltpu.make_async_copy(n_v, n_ref.at[at], out_sem.at[0])
+        n_out.start()
+
+        def columns(i, _):
+            sl = pl.ds(pl.multiple_of(i * tile, tile), tile)
+            got = jnp.dot(n_v[...], w_v[:, sl], preferred_element_type=F32)
+            if steps == 1:
+                ci_v[...] = got[:, :width].astype(BF16)
+                gate_v[...] = got[:, width:]
+            else:
+                @pl.when(i < steps // 2)
+                def _():
+                    ci_v[:, sl] = got.astype(BF16)
+
+                @pl.when(i >= steps // 2)
+                def _():
+                    gate_v[:, pl.ds(pl.multiple_of(i * tile - width, tile), tile)] = got
+            return 0
+        lax.fori_loop(0, steps, columns, 0)
+        ci_out = pltpu.make_async_copy(ci_v, ci_ref.at[at], out_sem.at[1])
+        gate_out = pltpu.make_async_copy(gate_v, gate_ref.at[at], out_sem.at[2])
+        ci_out.start()
+        gate_out.start()
+        n_out.wait()
+        ci_out.wait()
+        gate_out.wait()
+
+    def work(first, last):
+        def one(i, _):
+            k0, j = i // (2 * ys), i % (2 * ys)
+            lower, yy = j // ys, j % ys
+            own = yy == y
+            k = k0 - jnp.where(own, 0, 1)
+            o = z + k * (2 * lower - 1)
+            ok = (k >= 0) & (k < zs) & (o >= 0) & (o < zs) & ((lower == 0) | (k > 0))
+
+            @pl.when(ok & jnp.logical_not(own))
+            def _():
+                for h in range(2):
+                    landed(o, yy, h).wait_recv()
+
+            @pl.when(ok)
+            def _():
+                project(o * ys + yy)
+            return 0
+        lax.fori_loop(first * 2 * ys, last * 2 * ys, one, 0)
+
+    work(0, min(3, zs))
+
+    def later(k, _):
+        relay(k)
+        work(k, k + 1)
+        return 0
+
+    lax.fori_loop(3, zs, later, 0)
+    work(zs, zs + 1)
+    w_out.wait()
+
+    def drain_first(s):
+        gain_to(s).wait_send()
+        for part in range(2):
+            w_first(s, part).wait_send()
+
+    every_other(drain_first)
+
+    def drain_second(s, _):
+        for j in range(1, xs):
+            shared(s, mine, w2send, j - 1, {"dp": mine}).wait_send()
+        for j in range(xs):
+            shared(s, mine, w3send, j, {"dp": mine}).wait_send()
+        return 0
+
+    if split:
+        lax.fori_loop(0, chunks, drain_second, 0)
+
+    def drain(k, _):
+        for h in range(2):
+            @pl.when(z - k >= 0)
+            def _():
+                when(z + 1 < zs, lambda: up(z - k, h).wait_send())
+                for j in range(1, ys):
+                    side(z - k, j, h).wait_send()
+
+            @pl.when((z + k < zs) & (k > 0))
+            def _():
+                when(z > 0, lambda: down(z + k, h).wait_send())
+                for j in range(1, ys):
+                    side(z + k, j, h).wait_send()
+        return 0
+
+    lax.fori_loop(0, zs, drain, 0)
+    for h in range(2):
+        when(z > 0, lambda: down(z, h).wait_send())
+
+
+def gather_project(hidden, wq, gain, chunks, copies, share, split):
+    tokens, model = hidden.shape
+    width = wq.shape[1] // 2 // chunks
+    zs, ys = grid_of(chunks, copies)
+    any_spec = pl.BlockSpec(memory_space=pl.ANY)
+    sds = jax.ShapeDtypeStruct
+    dma = pltpu.SemaphoreType.DMA
+    return pl.pallas_call(
+        functools.partial(gather_project_kernel, chunks=chunks, copies=copies, share=share, split=split),
+        in_specs=[any_spec] * 3,
+        out_specs=[any_spec] * 4 + [pl.BlockSpec(memory_space=pltpu.VMEM)],
+        out_shape=[sds((chunks, tokens, model), BF16), sds((chunks, tokens, width), BF16),
+                   sds((chunks, tokens, width), F32), sds((model, 2 * width), BF16), sds((1, model), F32)],
+        scratch_shapes=[
+            pltpu.VMEM((chunks, tokens, model), BF16), pltpu.VMEM((chunks, 1, share), F32), pltpu.VMEM((model, 2 * width), BF16),
+            pltpu.VMEM((tokens, model), BF16), pltpu.VMEM((tokens, width), BF16), pltpu.VMEM((tokens, width), F32),
+            dma(()), dma((3,)), dma((chunks, 2)), dma((zs, max(1, ys - 1), 2)), dma((zs, 2)), dma((zs, 2)),
+            dma((chunks, 2)), dma((chunks, 2)), dma((chunks, copies)), dma((chunks, max(1, copies // 2))), dma((chunks, max(1, copies // 2))),
+            dma((chunks,)), dma((chunks,)),
+        ],
+        compiler_params=pltpu.CompilerParams(collective_id=0, has_side_effects=True, vmem_limit_bytes=60 * 1024 * 1024),
+        name="gather_project",
+    )(hidden, wq, gain)
+
+
+def total_kernel(part_ref, out_ref, recv_v, send1, recv1, send2, recv2, own_sem, *, chunks):
+    me = lax.axis_index("seq")
+    meet(chunks, 1)
+
+    def first(s):
+        return remote(part_ref.at[s], recv_v.at[me], send1.at[s], recv1.at[me], {"seq": s})
+
+    def landed_first(s):
+        return remote(part_ref.at[s], recv_v.at[s], send1.at[s], recv1.at[s], {"seq": s})
+
+    def second(s):
+        return remote(out_ref.at[me], out_ref.at[me], send2.at[s], recv2.at[me], {"seq": s})
+
+    def landed_second(s):
+        return remote(out_ref.at[s], out_ref.at[s], send2.at[s], recv2.at[s], {"seq": s})
+
+    def every_other(fn):
+        def one(k, _):
+            fn(lax.rem(me + k, chunks))
+            return 0
+        lax.fori_loop(1, chunks, one, 0)
+
+    every_other(lambda s: first(s).start())
+    recv_v[me] = part_ref[me]
+    every_other(lambda s: landed_first(s).wait_recv())
+    total = recv_v[0].astype(F32)
+    for s in range(1, chunks):
+        total = total + recv_v[s].astype(F32)
+    out_ref[me] = total.astype(BF16)
+    every_other(lambda s: second(s).start())
+    every_other(lambda s: landed_second(s).wait_recv())
+    every_other(lambda s: first(s).wait_send())
+    every_other(lambda s: second(s).wait_send())
+
+
+def total_over_seq(part, chunks, key):
+    vmem = pl.BlockSpec(memory_space=pltpu.VMEM)
+    dma = pltpu.SemaphoreType.DMA
+    return pl.pallas_call(
+        functools.partial(total_kernel, chunks=chunks),
+        in_specs=[vmem],
+        out_specs=vmem,
+        out_shape=jax.ShapeDtypeStruct(part.shape, BF16),
+        scratch_shapes=[pltpu.VMEM(part.shape, BF16),
+                        dma((chunks,)), dma((chunks,)), dma((chunks,)), dma((chunks,)), dma(())],
+        compiler_params=pltpu.CompilerParams(collective_id=key, has_side_effects=True, vmem_limit_bytes=60 * 1024 * 1024),
+        name=f"total_over_seq_{key}",
+    )(part)
+def order_of(zs):
+    return [sorted(range(zs), key=lambda t: (-abs(t - z), t)) for z in range(zs)]
+
+
+def scatter_kernel(*refs, chunks, copies, split):
+    if split:
+        (gc_ref, gg_ref, w_ref, late_ref, gin_ref, red_ref, sum_ref, all_ref,
+         ysend_v, yrecv_v, own_v, zrecv_v, late_v, w_v, g1_v, mine_v, g2_v, t_v, fin_v, load_sem,
+         ysend, yrecv, zup, zdown, zrecv, lsend, lrecv,
+         g1send, g1recv, g2send, g2recv, g3send, g3recv, g4send, g4recv) = refs
+    else:
+        (gc_ref, gg_ref, w_ref, late_ref, red_ref, sum_ref,
+         ysend_v, yrecv_v, own_v, zrecv_v, late_v, w_v, load_sem,
+         ysend, yrecv, zup, zdown, zrecv, lsend, lrecv) = refs
+    zs, ys = grid_of(chunks, copies)
+    xs = copies // 2
+    me, mine = lax.axis_index("seq"), lax.axis_index("dp")
+    z, y = me // ys, me % ys
+    x, c = mine // 2, mine % 2
+    tokens, width = gc_ref.shape[1:]
+    model = w_ref.shape[0]
+    half = tokens // 2
+    tile = min(256, model)
+    tables = order_of(zs)
+
+    def dest(i):
+        got = 0
+        for k in range(zs):
+            got = got + jnp.where(z == k, tables[k][i], 0)
+        return got
+
+    w_in = pltpu.make_async_copy(w_ref, w_v, load_sem.at[0])
+    w_in.start()
+    if split:
+        piece, inner2 = fin_v.shape
+        inner = inner2 // 2
+        loads = [pltpu.make_async_copy(gin_ref.at[:, q * 2 + c], mine_v.at[q], load_sem.at[1 + q]) for q in range(xs)]
+        for one in loads:
+            one.start()
+    meet(chunks, copies)
+
+    def late_to(d):
+        return remote(late_ref, late_v.at[mine], lsend.at[d], lrecv.at[mine], {"dp": d})
+
+    def late_from(d):
+        return remote(late_v.at[d], late_v.at[d], lsend.at[d], lrecv.at[d], {"dp": d})
+
+    def every_copy(fn):
+        def one(k, _):
+            fn(lax.rem(mine + k, copies))
+            return 0
+        lax.fori_loop(1, copies, one, 0)
+
+    if split:
+        def g1(q):
+            return remote(gin_ref.at[:, q * 2 + 1 - c], g1_v.at[q], g1send.at[q], g1recv.at[q], {"dp": x * 2 + 1 - c})
+
+        for q in range(xs):
+            g1(q).start()
+    every_copy(lambda d: late_to(d).start())
+    w_in.wait()
+
+    def partial(s, out, at):
+        def one(i, _):
+            sl = pl.ds(pl.multiple_of(i * tile, tile), tile)
+            got = nt_dot(gc_ref[s], w_v[sl, :width]) + nt_dot(gg_ref[s], w_v[sl, width:])
+            out[at, :, sl] = got.astype(BF16)
+            return 0
+        lax.fori_loop(0, model // tile, one, 0)
+
+    def to_side(i, j, h):
+        rows = pl.ds(h * half, half)
+        k = i * (ys - 1) + j - 1
+        return remote(ysend_v.at[k % ysend_v.shape[0], rows], yrecv_v.at[k, rows], ysend.at[k, h], yrecv.at[k, h], {"seq": z * ys + lax.rem(y + j, ys)})
+
+    slots = ysend_v.shape[0]
+    for i in range(zs):
+        for j in range(1, ys):
+            k = i * (ys - 1) + j - 1
+            if k >= slots:
+                for h in range(2):
+                    to_side((k - slots) // (ys - 1), (k - slots) % (ys - 1) + 1, h).wait_send()
+            partial(dest(i) * ys + lax.rem(y + j, ys), ysend_v, k % slots)
+            for h in range(2):
+                to_side(i, j, h).start()
+
+    def add_into(total, terms):
+        def one(r, _):
+            sl = pl.ds(pl.multiple_of(r * 32, 32), 32)
+            total(sl, terms)
+            return 0
+        return one
+
+    if split:
+        def g2(q):
+            return remote(mine_v.at[q], g2_v.at[x], g2send.at[q], g2recv.at[x], {"dp": q * 2 + c})
+
+        def g2_from(q):
+            return remote(g2_v.at[q], g2_v.at[q], g2send.at[q], g2recv.at[q], {"dp": q * 2 + c})
+
+        for q in range(xs):
+            loads[q].wait()
+            g1(q).wait_recv()
+
+            def fold(s, _):
+                mine_v[q, s] = (mine_v[q, s].astype(F32) + g1_v[q, s].astype(F32)).astype(BF16)
+                return 0
+            lax.fori_loop(0, chunks, fold, 0)
+
+            @pl.when(q != x)
+            def _():
+                g2(q).start()
+
+        def columns(part, s):
+            return pl.ds(pl.multiple_of(part * inner + s * width, width), width)
+
+        def g3(s, part):
+            return remote(t_v.at[s, :, pl.ds(part * width, width)], fin_v.at[:, columns(part, me)], g3send.at[s, part], g3recv.at[me, part], {"seq": s})
+
+        def g3_from(s, part):
+            return remote(fin_v.at[:, columns(part, s)], fin_v.at[:, columns(part, s)], g3send.at[s, part], g3recv.at[s, part], {"seq": s})
+
+        def every_other(fn):
+            def one(k, _):
+                fn(lax.rem(me + k, chunks))
+                return 0
+            lax.fori_loop(1, chunks, one, 0)
+
+        def third():
+            for q in range(xs):
+                @pl.when(q != x)
+                def _():
+                    g2_from(q).wait_recv()
+
+            def fold(s, _):
+                total = mine_v[x, s].astype(F32)
+                for q in range(1, xs):
+                    total = total + g2_v[lax.rem(x + q, xs), s].astype(F32)
+                t_v[s] = total.astype(BF16)
+                return 0
+            lax.fori_loop(0, chunks, fold, 0)
+            for part in range(2):
+                every_other(lambda s: g3(s, part).start())
+                fin_v[:, columns(part, me)] = t_v[me, :, part * width:(part + 1) * width]
+
+        def rows_of(d):
+            return pl.ds(pl.multiple_of(d * piece, piece), piece)
+
+        def g4(d_src, k, d):
+            src = fin_v if d_src is None else all_ref.at[rows_of(d_src)]
+            row = mine if d_src is None else d_src
+            return remote(src, all_ref.at[rows_of(row)], g4send.at[k], g4recv.at[row], {"dp": d})
+
+        def g4_from(d):
+            return remote(all_ref.at[rows_of(d)], all_ref.at[rows_of(d)], g4send.at[0], g4recv.at[d], {"dp": d})
+
+        keep = pltpu.make_async_copy(fin_v, all_ref.at[rows_of(mine)], load_sem.at[0])
+
+        def fourth():
+            for part in range(2):
+                every_other(lambda s: g3_from(s, part).wait_recv())
+            for j in range(1, xs):
+                g4(None, j, lax.rem(x + j, xs) * 2 + c).start()
+            g4(None, 0, x * 2 + 1 - c).start()
+            keep.start()
+
+    def arrived(i, j, h):
+        rows = pl.ds(h * half, half)
+        k = i * (ys - 1) + j - 1
+        return remote(yrecv_v.at[k, rows], yrecv_v.at[k, rows], ysend.at[k, h], yrecv.at[k, h], {"seq": z * ys + lax.rem(y + j, ys)})
+
+    def climb(t, h):
+        rows = pl.ds(h * half, half)
+        return remote(own_v.at[t, rows], zrecv_v.at[t, rows], zup.at[t, h], zrecv.at[t, h], {"seq": (z + 1) * ys + y})
+
+    def sink(t, h):
+        rows = pl.ds(h * half, half)
+        slot = jnp.where(t == z - 1, zs, t)
+        return remote(own_v.at[t, rows], zrecv_v.at[slot, rows], zdown.at[t, h], zrecv.at[slot, h], {"seq": (z - 1) * ys + y})
+
+    def from_z(slot, h):
+        rows = pl.ds(h * half, half)
+        return remote(zrecv_v.at[slot, rows], zrecv_v.at[slot, rows], zup.at[0, h], zrecv.at[slot, h], {"seq": lax.rem(me + 1, chunks)})
+
+    def accumulate(t, h, read):
+        def one(r, _):
+            sl = pl.ds(pl.multiple_of(h * half + r * 32, 32), 32)
+            own_v[t, sl, :] = (own_v[t, sl, :].astype(F32) + read(sl)).astype(BF16)
+            return 0
+        lax.fori_loop(0, half // 32, one, 0)
+
+    for i in range(zs):
+        t = dest(i)
+        partial(t * ys + y, own_v, t)
+        for h in range(2):
+            for j in range(1, ys):
+                arrived(i, ys - j, h).wait_recv()
+
+            def side_sum(sl):
+                total = yrecv_v[i * (ys - 1), sl, :].astype(F32)
+                for j in range(2, ys):
+                    total = total + yrecv_v[i * (ys - 1) + j - 1, sl, :].astype(F32)
+                return total
+
+            if ys > 1:
+                accumulate(t, h, side_sum)
+
+            @pl.when(((t > z) & (z > 0)) | ((t == z) & (z > 0)))
+            def _():
+                from_z(t, h).wait_recv()
+                accumulate(t, h, lambda sl: zrecv_v[t, sl, :].astype(F32))
+
+            @pl.when((t < z) & (z + 1 < zs))
+            def _():
+                from_z(t, h).wait_recv()
+                accumulate(t, h, lambda sl: zrecv_v[t, sl, :].astype(F32))
+
+            @pl.when((t == z) & (z + 1 < zs))
+            def _():
+                from_z(zs, h).wait_recv()
+                accumulate(t, h, lambda sl: zrecv_v[zs, sl, :].astype(F32))
+
+            @pl.when(t > z)
+            def _():
+                climb(t, h).start()
+
+            @pl.when(t < z)
+            def _():
+                sink(t, h).start()
+        if split and i == 0:
+            third()
+        if split and i == max(0, zs - 2):
+            fourth()
+
+    red_ref[...] = own_v[z]
+    every_copy(lambda d: late_from(d).wait_recv())
+    total = late_ref[...]
+    for k in range(1, copies):
+        total = total + late_v[lax.rem(mine + k, copies)]
+    sum_ref[...] = total
+    if split:
+        for j in range(1, xs):
+            d = lax.rem(x + j, xs) * 2 + c
+            g4_from(d).wait_recv()
+            g4(d, xs - 1 + j, x * 2 + 1 - c).start()
+        keep.wait()
+        for j in range(xs):
+            g4_from(lax.rem(x + j, xs) * 2 + 1 - c).wait_recv()
+
+    every_copy(lambda d: late_to(d).wait_send())
+    count = zs * (ys - 1)
+    for k in range(max(0, count - slots), count):
+        for h in range(2):
+            to_side(k // (ys - 1), k % (ys - 1) + 1, h).wait_send()
+    for i in range(zs):
+        t = dest(i)
+        for h in range(2):
+            @pl.when(t > z)
+            def _():
+                climb(t, h).wait_send()
+
+            @pl.when(t < z)
+            def _():
+                sink(t, h).wait_send()
+    if split:
+        for q in range(xs):
+            g1(q).wait_send()
+
+            @pl.when(q != x)
+            def _():
+                g2(q).wait_send()
+        for part in range(2):
+            every_other(lambda s: g3(s, part).wait_send())
+        for j in range(xs):
+            g4(None, j, mine).wait_send()
+        for j in range(1, xs):
+            g4(lax.rem(x + j, xs) * 2 + c, xs - 1 + j, mine).wait_send()
+
+
+def scatter_sums(gc, gg, w_all, late, gin, chunks, copies, split):
+    tokens, width = gc.shape[1:]
+    model = w_all.shape[0]
+    zs, ys = grid_of(chunks, copies)
+    xs = max(1, copies // 2)
+    others = max(1, zs * (ys - 1))
+    slots = min(others, 4)
+    any_spec = pl.BlockSpec(memory_space=pl.ANY)
+    vmem = pl.BlockSpec(memory_space=pltpu.VMEM)
+    sds = jax.ShapeDtypeStruct
+    dma = pltpu.SemaphoreType.DMA
+    args = [gc, gg, w_all, late]
+    in_specs = [vmem, vmem, any_spec, vmem]
+    out_specs = [vmem, vmem]
+    out_shape = [sds((tokens, model), BF16), sds(late.shape, F32)]
+    scratch = [pltpu.VMEM((slots, tokens, model), BF16), pltpu.VMEM((others, tokens, model), BF16),
+               pltpu.VMEM((zs, tokens, model), BF16), pltpu.VMEM((zs + 1, tokens, model), BF16),
+               pltpu.VMEM((copies,) + late.shape, F32), pltpu.VMEM(w_all.shape, BF16)]
+    sems = [dma((1 + xs,)), dma((others, 2)), dma((others, 2)), dma((zs, 2)), dma((zs, 2)), dma((zs + 1, 2)), dma((copies,)), dma((copies,))]
+    if split:
+        piece = gin.shape[2]
+        slab = (xs, chunks, piece, 2 * width)
+        args.append(gin)
+        in_specs.append(any_spec)
+        out_specs.append(any_spec)
+        out_shape.append(sds((copies * piece, 2 * chunks * width), BF16))
+        scratch += [pltpu.VMEM(slab, BF16), pltpu.VMEM(slab, BF16), pltpu.VMEM(slab, BF16), pltpu.VMEM(slab[1:], BF16),
+                    pltpu.VMEM((piece, 2 * chunks * width), BF16)]
+        sems += [dma((xs,)), dma((xs,)), dma((xs,)), dma((xs,)), dma((chunks, 2)), dma((chunks, 2)), dma((2 * xs,)), dma((copies,))]
+    return pl.pallas_call(
+        functools.partial(scatter_kernel, chunks=chunks, copies=copies, split=split),
+        in_specs=in_specs,
+        out_specs=out_specs,
+        out_shape=out_shape,
+        scratch_shapes=scratch + sems,
+        compiler_params=pltpu.CompilerParams(collective_id=3, has_side_effects=True, vmem_limit_bytes=62 * 1024 * 1024),
+        name="scatter_sums",
+    )(*args)
 from jax.sharding import PartitionSpec as P
-
-EPSILON = 1e-05
 
 
 def local(hidden, grad_out, lengths, norm_gain, input_weight, conv_weight, conv_bias, select_weight,
@@ -343,26 +1012,21 @@
     tokens = chunks * rows * length
     here = lax.axis_index("seq")
 
-    hidden_all = lax.all_gather(hidden, "seq", axis=0)
-    gain_all = lax.all_gather(norm_gain, "seq", axis=0, tiled=True).astype(F32)
-    blocks = input_weight.reshape(share, 2, chunks, width)
-    blocks = lax.all_to_all(blocks, "seq", split_axis=2, concat_axis=0, tiled=False)
-    w_conv = blocks[:, :, 0].reshape(model, width)
-    w_gate = blocks[:, :, 1].reshape(model, width)
+    split = (share // copies) % 16 == 0 and copies % 2 == 0
+    normed, ci, gate, w_all, gain_row = gather_project(
+        hidden.reshape(rows * length, model), input_weight, norm_gain.astype(F32).reshape(1, share), chunks, copies, share, split)
+    normed = normed.reshape(tokens, model)
     slots = here * length + lax.broadcasted_iota(jnp.int32, (rows, length), 1)
     valid = (slots < lengths[:, None]).astype(F32)[..., None]
     cotangent = grad_out.astype(F32) * valid
-    gm = lax.all_gather(cotangent.astype(BF16), "seq", axis=0).reshape(tokens, model)
-
-    source_all = hidden_all.reshape(tokens, model).astype(F32)
-    inverse_all = lax.rsqrt(jnp.mean(source_all * source_all, axis=-1, keepdims=True) + EPSILON)
-    normed = (source_all * inverse_all * gain_all).astype(BF16)
+    behind, gain_row = lax.optimization_barrier((cotangent.astype(BF16), gain_row))
+    gm = lax.all_gather(behind, "seq", axis=0).reshape(tokens, model)
+
     shaped = lambda a: a.reshape(chunks, rows, length, a.shape[-1])
-    ci = shaped(jnp.dot(normed, w_conv, preferred_element_type=F32).astype(BF16))
-    gate = shaped(jnp.dot(normed, w_gate, preferred_element_type=F32))
+    ci, gate = shaped(ci), shaped(gate)
     bias_row = conv_bias.reshape(1, width)
     x, partial = conv_forward(ci, conv_weight, bias_row, select_weight)
-    sel = lax.psum(partial, "seq")
+    sel = total_over_seq(partial, chunks, 1)
     step_row = step_bias.reshape(1, width)
     skip_row = skip_weight.reshape(1, width)
     gated, ssm, starts = scan_forward(sel, x, gate, step_weight, step_row, decay_log, skip_row, n)
@@ -375,29 +1039,35 @@
     gg = shaped(lax.dot_general(gm, output_weight, (((1,), (1,)), ((), ())), preferred_element_type=F32))
     ggate, gvals, gpre, gpart, gstepw, gstepb, gdecay, gskip = scan_backward(
         sel, x, gate, gg, ssm, starts, step_weight, step_row, decay_log, skip_row, n)
-    gsel = lax.psum(gpart, "seq")
+    gsel = total_over_seq(gpart, chunks, 2)
     tn = lambda a, b: lax.dot_general(a, b, (((0,), (0,)), ((), ())), preferred_element_type=F32)
     gout = tn(gated2, gm)
+    gstepw, gstepb, gdecay, gskip, gout = lax.psum((gstepw, gstepb, gdecay, gskip, gout), "dp")
     gci, gtaps, gconvb, gselw = conv_backward(ci, gvals, gsel, conv_weight, bias_row, select_weight)
+    tap_count = gtaps.shape[0]
     gci2 = gci.reshape(tokens, width)
     ggate2 = ggate.reshape(tokens, width)
-    gin = jnp.stack([tn(normed, gci2).astype(BF16), tn(normed, ggate2).astype(BF16)], axis=1)
-    gin = gin.reshape(chunks, copies, share // copies, 2, width)
-    gin = lax.psum_scatter(gin, "dp", scatter_dimension=1, tiled=False)
-    gin = lax.all_to_all(gin, "seq", split_axis=0, concat_axis=2, tiled=False)
-    gin = lax.all_gather(gin.reshape(share // copies, 2 * chunks * width), "dp", axis=0, tiled=True).astype(F32)
-    both = lambda g, w: lax.dot_general(g, w, (((1,), (1,)), ((), ())), preferred_element_type=F32)
-    gnormed = (both(gci2, w_conv) + both(ggate2, w_gate)).astype(BF16)
-    gnormed = lax.psum_scatter(shaped(gnormed), "seq", scatter_dimension=0, tiled=False).astype(F32)
+    gin = jnp.concatenate([tn(normed, gci2).astype(BF16), tn(normed, ggate2).astype(BF16)], axis=1)
+    gin = gin.reshape(chunks, copies, share // copies, 2 * width)
+    late = jnp.concatenate([gselw, gtaps, gconvb], axis=0)
+    late = jnp.pad(late, ((0, -late.shape[0] % 8), (0, 0)))
+    flat = lambda a: a.reshape(chunks, rows * length, width)
+    got = scatter_sums(flat(gci), flat(ggate), w_all, late, gin, chunks, copies, split)
+    scaled, late = got[:2]
+    if split:
+        gin = got[2].astype(F32)
+    else:
+        gin = gin.reshape(chunks, copies, share // copies, 2, width)
+        gin = lax.psum_scatter(gin, "dp", scatter_dimension=1, tiled=False)
+        gin = lax.all_to_all(gin, "seq", split_axis=0, concat_axis=2, tiled=False)
+        gin = lax.all_gather(gin.reshape(share // copies, 2 * chunks * width), "dp", axis=0, tiled=True).astype(F32)
+    ggain = jnp.sum(gin * input_weight.astype(F32), axis=1) / norm_gain.astype(F32)
+    scaled = scaled.reshape(rows, length, model).astype(F32) * gain_row
     inverse = lax.rsqrt(jnp.mean(source * source, axis=-1, keepdims=True) + EPSILON)
-    scaled = gnormed * gain_all
     ghidden = inverse * scaled - source * inverse ** 3 * jnp.mean(scaled * source, axis=-1, keepdims=True) + cotangent
-    ggain = jnp.sum(gnormed * source * inverse, axis=(0, 1))
-    ggain = lax.psum(ggain, ("dp", "seq"))
-    ggain = lax.dynamic_slice(ggain, (here * share,), (share,))
-    gtaps, gconvb, gselw, gstepw, gstepb, gdecay, gskip, gout = lax.psum(
-        (gtaps, gconvb, gselw, gstepw, gstepb, gdecay, gskip, gout), "dp")
-    return (output, ghidden, ggain, gin, gtaps, gconvb.reshape(width), gselw, gstepw, gstepb.reshape(width),
+    picked = gselw.shape[0]
+    gselw, gtaps, gconvb = late[:picked], late[picked:picked + tap_count], late[picked + tap_count]
+    return (output, ghidden, ggain, gin, gtaps, gconvb, gselw, gstepw, gstepb.reshape(width),
             gdecay, gskip.reshape(width), gout)
 
 

time: 1320 us -> 707 us (0.54)
  waiting for transfers between devices: 729 us -> 27.4 us
  Pallas kernels: 197 us -> 563 us
  blocking collectives: 205 us -> 11.9 us
  matrix products: 90.5 us -> 42.7 us
  local copies, waits for them, and re-layouts: 34.7 us -> 20.6 us
    pallas_call x0 -> x4, Pallas kernels: none -> 361 us  [the longest x1 140 us: scatter_sums(): pl.pallas_call(functools.partial(scatter_kernel, chunks=chunks, copies=co...]
    psum x3 -> x1, waiting for transfers between devices: 279 us -> 0.01 us  [local(): lax.psum((gstepw, gstepb, gdecay, gskip, gout), 'dp')]
    reduce_scatter x1 -> x0, waiting for transfers between devices: 121 us -> none  [local(): lax.psum_scatter(shaped(gnormed), 'seq', scatter_dimension=0, tiled=False)]
    all_gather x1 -> x0, blocking collectives: 120 us -> none  [local(): gain_all = lax.all_gather(norm_gain, 'seq', axis=0, tiled=True).astype(F32)]
    reduce_scatter x1, waiting for transfers between devices: 106 us -> 0.02 us  [local(): lax.psum_scatter(shaped(mixed), 'seq', scatter_dimension=0, tiled=False)]
    unnamed x10 -> x3, waiting for transfers between devices: 84.5 us -> 0.05 us
    all_gather x3 -> x1, waiting for transfers between devices: 86.8 us -> 27.3 us  [local(): gm = lax.all_gather(behind, 'seq', axis=0).reshape(tokens, model)]
    all_to_all x1 -> x0, waiting for transfers between devices: 52.1 us -> none  [local(): lax.all_to_all(blocks, 'seq', split_axis=2, concat_axis=0, tiled=False)]
  transfers between devices with their start and end apart: 10 -> 3, of which waited for: 9 -> 1; matrix products, arithmetic and copies ran while one was open for 10% -> 10% of each run, Pallas kernels for 1% -> 63%
where the time goes in v2:
time: 707 us; the launch traced here: 703 us
  Pallas kernels  563 us (80%)
  matrix products  42.7 us (6%)
  waiting for transfers between devices  27.4 us (4%)
  other arithmetic  22.8 us (3%)
  local copies, waits for them, and re-layouts  20.6 us (3%)
  between operations  13.9 us (2%)
  blocking collectives  11.9 us (2%)
    pallas_call x1, Pallas kernels, scatter_sums(): pl.pallas_call(functools.partial(scatter_kernel, chunks=chunks, copies=co...  140 us
    pallas_call x1, Pallas kernels, gather_project(): pl.pallas_call(functools.partial(gather_project_kernel, chunks=chunks, co...  123 us
    pallas_call x1, Pallas kernels, scan_backward(): pl.pallas_call(functools.partial(scan_backward_kernel, rank=rank, n=n), g...  121 us
    pallas_call x2, Pallas kernels, total_over_seq(): pl.pallas_call(functools.partial(total_kernel, chunks=chunks), in_specs=[...  98.1 us
    pallas_call x1, Pallas kernels, scan_forward(): pl.pallas_call(functools.partial(scan_forward_kernel, rank=rank, n=n), gr...  50.9 us
    all_gather x1, waiting for transfers between devices, local(): gm = lax.all_gather(behind, 'seq', axis=0).reshape(tokens, model)  27.3 us
    dot_general x3, matrix products, local(): lax.dot_general(a, b, (((0,), (0,)), ((), ())), preferred_element_type=F32)  24.8 us
    pallas_call x1, Pallas kernels, conv_backward(): pl.pallas_call(conv_backward_kernel, grid=(rows, chunks), in_specs=[tok(w...  17.1 us
  transfers between devices with their start and end apart: 3, of which 1 were waited for; matrix products, arithmetic and copies ran while one was open for 10% of the time, Pallas kernels for 63%

profile of v2, /device:TPU:0, one launch (start us, length us, event | category | flops | bytes accessed | tf_op | source)
XLA Modules:
  0.0 702.7 jit_solution(12503617159272456012)
XLA Ops:
  7.2 1.2 convert_element_type.53
  8.5 0.7 compare_convert_fusion
  9.2 2.4 fusion.10
  11.6 123.1 %gather_project.1 = (bf16[8,256,2048]{2,1,0:T(8,128)(2,1)}, bf16[8,256,512]{2,1,0:T(8,128)(2,1)}, f32[8,256,512]{2,1,0:T(8,128)}, bf16[2048,1024]{1,0:T(8,128)(2,1)}, f32[1,2048]{1,0:T(1,128)}) custom-call(bf16[256,2048]{1,0:T(8,128)(2,1)} %bitcast.47, bf16[256,8192]{1,0:T(8,128)(2,1)} %wq_ref.1, f32[1,256]{1,0:T(1,128)} %bitcast.59), custom_call_target="tpu_custom_call" | custom-call | tf_op jit(solution)/shard_map/gather_project/pallas_call | solution.py:617
  134.8 0.6 reshape.132.bias_ref
  135.4 0.6 reshape.134.bias_ref
  136.5 12.6 %conv_forward.1 = (bf16[8,2,128,512]{3,2,1,0:T(8,128)(2,1)}, bf16[8,2,160,128]{3,2,1,0:T(8,128)(2,1)}) custom-call(bf16[8,2,128,512]{3,2,1,0:T(8,128)(2,1)} %bitcast.41, bf16[4,512]{1,0:T(4,128)(2,1)} %taps_ref.3, bf16[1,512]{1,0:T(2,128)(2,1)} %reshape.132.bias_ref, bf16[160,512]{1,0:T(8,128)(2,1)} %selw_ref.3), custom_call_target="tpu_custom_call" | custom-call | tf_op jit(solution)/shard_map/conv_forward/pallas_call | solution.py:260
  149.2 53.9 %total_over_seq_1.1.sel_ref = bf16[8,2,160,128]{3,2,1,0:T(8,128)(2,1)} custom-call(bf16[8,2,160,128]{3,2,1,0:T(8,128)(2,1)} %get-tuple-element.39.part_ref), custom_call_target="tpu_custom_call" | custom-call | tf_op jit(solution)/shard_map/total_over_seq_1/pallas_call | solution.py:673
  203.0 50.9 %scan_forward.1 = (bf16[8,2,128,512]{3,2,1,0:T(8,128)(2,1)}, bf16[8,2,128,512]{3,2,1,0:T(8,128)(2,1)}, f32[8,2,16,512]{3,2,1,0:T(8,128)}) custom-call(bf16[8,2,160,128]{3,2,1,0:T(8,128)(2,1)} %total_over_seq_1.1.sel_ref, bf16[8,2,128,512]{3,2,1,0:T(8,128)(2,1)} %get-tuple-element.40.x_ref, f32[8,2,128,512]{3,2,1,0:T(8,128)} %bitcast.44, ...), custom_call_target="tpu_custom_call" | custom-call | tf_op jit(solution)/shard_map/scan_forward/pallas_call | solution.py:88
  254.0 8.5 %convolution_convert_fusion = bf16[2048,2048]{1,0:T(8,128)(2,1)} fusion(bf16[2048,512]{1,0:T(8,128)(2,1)} %bitcast.66, bf16[512,2048]{1,0:T(8,128)(2,1)S(1)} %copy-done.17), kind=kOutput, calls=%fused_computation.1 | convolution fusion | flops 4299161600 | bytes 12582912 | tf_op jit(solution)/shard_map/dot_general | solution.py:1034
  262.7 27.3 %all-gather.3.cloned.1.call-done = bf16[16,128,2048]{2,1,0:T(8,128)(2,1)} async-done(((bf16[2,128,2048]{2,1,0:T(8,128)(2,1)}), bf16[16,128,2048]{2,1,0:T(8,128)(2,1)}) %all-gather.3.cloned.1.call-update) | async-done | bytes 8388624 | tf_op jit(solution)/shard_map/all_gather | solution.py:1023
  290.1 9.5 %fusion.8.gg_ref = f32[8,2,128,512]{3,2,1,0:T(8,128)} fusion(bf16[8,2,128,2048]{3,2,1,0:T(8,128)(2,1)} %bitcast.64, bf16[512,2048]{1,0:T(8,128)(2,1)S(1)} %copy-done.17), kind=kOutput, calls=%fused_computation.19 | convolution fusion | flops 4294967296 | bytes 14680064 | tf_op jit(solution)/shard_map/dot_general | solution.py:1039
  299.6 121.0 %scan_backward.1 = (bf16[8,2,128,512]{3,2,1,0:T(8,128)(2,1)}, f32[8,2,128,512]{3,2,1,0:T(8,128)}, bf16[8,2,128,512]{3,2,1,0:T(8,128)(2,1)}, bf16[8,2,160,128]{3,...) custom-call(bf16[8,2,160,128]{3,2,1,0:T(8,128)(2,1)} %total_over_seq_1.1.sel_, ...), custom_call_target="tpu_custom_call" | custom-call | tf_op jit(solution)/shard_map/scan_backward/pallas_call | solution.py:217
  420.6 44.2 %total_over_seq_2.1.gsel_ref = bf16[8,2,160,128]{3,2,1,0:T(8,128)(2,1)} custom-call(bf16[8,2,160,128]{3,2,1,0:T(8,128)(2,1)} %get-tuple-element.48.part_ref), custom_call_target="tpu_custom_call" | custom-call | tf_op jit(solution)/shard_map/total_over_seq_2/pallas_call | solution.py:673
  464.8 17.1 %conv_backward.1 = (bf16[8,2,128,512]{3,2,1,0:T(8,128)(2,1)}, f32[4,512]{1,0:T(4,128)}, f32[1,512]{1,0:T(1,128)}, f32[160,512]{1,0:T(8,128)}) custom-call(bf16[8,2,128,512]{3,2,1,0:T(8,128)(2,1)} %bitcast.42, bf16[8,2,128,512]{3,2,1,0:T(8,128)(2,1)} %bitcast.43, f32[8,2,128,512]{3,2,1,0:T(8,128)} %get-tuple-element.47.gvals_ref, ...), custom_call_target="tpu_custom_call" | custom-call | tf_op jit(solution)/shard_map/conv_backward/pallas_call | solution.py:319
  482.0 9.6 %convolution_bitcast_fusion = f32[512,2048]{1,0:T(8,128)} fusion(bf16[8,2,128,512]{3,2,1,0:T(8,128)(2,1)S(1)} %copy-done.18, bf16[8,2,128,2048]{3,2,1,0:T(8,128)(2,1)} %bitcast.65), kind=kOutput, calls=%fused_computation.7 | convolution fusion | flops 4294967296 | bytes 14680064 | tf_op jit(solution)/shard_map/dot_general | solution.py:1043
  491.6 9.3 %convolution_convert_fusion.2 = bf16[2048,512]{0,1:T(8,128)(2,1)} fusion(bf16[2048,2048]{1,0:T(8,128)(2,1)} %bitcast.60, bf16[2048,512]{1,0:T(8,128)(2,1)S(1)} %bitcast.53), kind=kOutput, calls=%fused_computation.9 | convolution fusion | flops 4296015872 | bytes 12582912 | tf_op jit(solution)/shard_map/dot_general | solution.py:1043
  500.9 5.8 convolution_convert_fusion.1
  506.8 1.6 copy-done.5
  508.4 4.4 pad_maximum_fusion
  512.7 6.5 copy.27
  519.3 0.8 select_maximum_fusion.refs_3_
  520.0 140.2 %scatter_sums.1 = (bf16[256,2048]{1,0:T(8,128)(2,1)}, f32[168,512]{1,0:T(8,128)}, bf16[256,8192]{1,0:T(8,128)(2,1)}) custom-call(bf16[8,256,512]{2,1,0:T(8,128)(2,1)} %bitcast.52, bf16[8,256,512]{2,1,0:T(8,128)(2,1)} %bitcast.50, bf16[2048,1024]{1,0:T(8,128)(2,1)} %get-tuple-element.51.refs_2_, f32[168,512]{1,0:T(8,128)} %select_maximum_fusion.refs_3_, ...), custom_call_target="tpu_custom_call" | custom-call | tf_op jit(solution)/shard_map/scatter_sums/pallas_call | solution.py:991
  660.2 1.3 slice.10
  661.5 1.3 slice.9
  662.9 1.7 slice.11
  664.6 11.9 %all-reduce.1 = (f32[512]{0:T(512)}, f32[16,512]{1,0:T(8,128)}, f32[512]{0:T(512)}) all-reduce(f32[512]{0:T(512)S(1)} %bitcast.56, f32[16,512]{1,0:T(8,128)S(1)} %copy-done.7, f32[512]{0:T(512)S(1)} %bitcast.57), channel_id=1, replica_groups=mesh['dp'=4,'seq'=8] {'dp'}, use_global_device_ids=true, to_apply=%region_5.0 | all-reduce | flops 9216 | bytes 73728 | tf_op jit(solution)/shard_map/psum | solution.py:1045
  676.5 8.1 %multiply_reduce_fusion = (f32[256]{0:T(256)S(1)}, f32[256,8192]{1,0:T(8,128)}) fusion(bf16[256,8192]{1,0:T(8,128)(2,1)} %wq_ref.1, bf16[256,8192]{1,0:T(8,128)(2,1)} %get-tuple-element.58), kind=kLoop, calls=%fused_computation | loop fusion | flops 8388352 | bytes 16778240 | tf_op jit(solution)/shard_map/reduce_sum | solution.py:1064
  685.1 0.6 fusion.2
  685.8 4.0 fusion.5
  689.8 1.7 copy.34
  691.5 4.7 copy.35
  (54 shorter events, 1.6 us)
Async XLA Ops:
  7.2 282.9 %all-gather.3.cloned.1.call-start = ((), (), s32[]{:S(2)}) async-start(), calls=%async_computation.2 | async-start | bytes 9437184 | tf_op jit(solution)/shard_map/all_gather | solution.py:1023
  11.6 123.2 %copy-start.13 = (bf16[512]{0:T(512)(128)(2,1)S(1)}, bf16[512]{0:T(512)(128)(2,1)}, u32[]{:S(2)}) copy-start(bf16[512]{0:T(512)(128)(2,1)} %param.19) | copy-start | bytes 3076
  11.6 123.8 %copy-start.14 = (bf16[512]{0:T(512)(128)(2,1)S(1)}, bf16[512]{0:T(512)(128)(2,1)}, u32[]{:S(2)}) copy-start(bf16[512]{0:T(512)(128)(2,1)} %param.22) | copy-start | bytes 3076
  11.6 124.3 %copy-start.15 = (bf16[512]{0:T(512)(128)(2,1)S(1)}, bf16[512]{0:T(512)(128)(2,1)}, u32[]{:S(2)}) copy-start(bf16[512]{0:T(512)(128)(2,1)} %param.24) | copy-start | bytes 3076
  134.7 551.0 %reduce-scatter.2.cloned.1.call-start = ((), (), s32[]{:S(2)}) async-start(), calls=%async_computation.1 | async-start | bytes 9437184 | tf_op jit(solution)/shard_map/reduce_scatter | solution.py:1035
  203.0 51.0 %copy-start.17 = (bf16[512,2048]{1,0:T(8,128)(2,1)S(1)}, bf16[512,2048]{1,0:T(8,128)(2,1)}, u32[]{:S(2)}) copy-start(bf16[512,2048]{1,0:T(8,128)(2,1)} %param.25) | copy-start | bytes 6291460
  262.5 427.3 %all-reduce.5.cloned.1.call-start = ((), (), s32[]{:S(2)}) async-start(), calls=%async_computation.3 | async-start | bytes 8912896 | tf_op jit(solution)/shard_map/psum | solution.py:1045
  464.8 17.1 %copy-start.18 = (bf16[8,2,128,512]{3,2,1,0:T(8,128)(2,1)S(1)}, bf16[8,2,128,512]{3,2,1,0:T(8,128)(2,1)}, u32[]{:S(2)}) copy-start(bf16[8,2,128,512]{3,2,1,0:T(8,128)(2,1)} %get-tuple-element.42) | copy-start | bytes 6291460
  482.0 9.6 %copy-start.4 = (bf16[8,2,128,512]{3,2,1,0:T(8,128)(2,1)S(1)}, bf16[8,2,128,512]{3,2,1,0:T(8,128)(2,1)}, u32[]{:S(2)}) copy-start(bf16[8,2,128,512]{3,2,1,0:T(8,128)(2,1)} %get-tuple-element.49) | copy-start | bytes 6291460
  482.0 18.9 %slice-start = ((s8[8388608]{0:T(1024)(128)(4,1)}), s8[4194304]{0:T(1024)(128)(4,1)S(1)}, s32[]{:S(2)}) async-start(s8[8388608]{0:T(1024)(128)(4,1)} %bitcast.61), calls=%async_computation.4 | async-start | bytes 8388608
  491.6 9.3 %copy-start.3 = (bf16[8,2,128,512]{3,2,1,0:T(8,128)(2,1)S(1)}, bf16[8,2,128,512]{3,2,1,0:T(8,128)(2,1)}, u32[]{:S(2)}) copy-start(bf16[8,2,128,512]{3,2,1,0:T(8,128)(2,1)} %get-tuple-element.50) | copy-start | bytes 6291460
  491.6 9.3 %slice-start.1 = ((s8[8388608]{0:T(1024)(128)(4,1)}), s8[4194304]{0:T(1024)(128)(4,1)S(1)}, s32[]{:S(2)}) async-start(s8[8388608]{0:T(1024)(128)(4,1)} %bitcast.61), calls=%async_computation.5 | async-start | bytes 8388608
  506.8 1.6 copy-start.5
  512.7 6.5 copy-start.6
  512.7 6.5 copy-start.9
  512.7 6.5 copy-start.10
  520.0 144.6 %copy-start.7 = (f32[16,512]{1,0:T(8,128)S(1)}, f32[16,512]{1,0:T(8,128)}, u32[]{:S(2)}) copy-start(f32[16,512]{1,0:T(8,128)} %get-tuple-element.62) | copy-start | bytes 98308
  520.0 144.6 %copy-start.11 = (f32[1,512]{1,0:T(1,128)S(1)}, f32[1,512]{1,0:T(1,128)}, u32[]{:S(2)}) copy-start(f32[1,512]{1,0:T(1,128)} %get-tuple-element.61) | copy-start | bytes 6148
  520.0 144.6 %copy-start.12 = (f32[1,512]{1,0:T(1,128)S(1)}, f32[1,512]{1,0:T(1,128)}, u32[]{:S(2)}) copy-start(f32[1,512]{1,0:T(1,128)} %get-tuple-element.63) | copy-start | bytes 6148
  676.5 8.1 %copy-start.16 = (bf16[256]{0:T(256)(128)(2,1)S(1)}, bf16[256]{0:T(256)(128)(2,1)}, u32[]{:S(2)}) copy-start(bf16[256]{0:T(256)(128)(2,1)} %param.16) | copy-start | bytes 1540
  676.5 8.7 %copy-start = (bf16[2,128,2048]{2,1,0:T(8,128)(2,1)S(1)}, bf16[2,128,2048]{2,1,0:T(8,128)(2,1)}, u32[]{:S(2)}) copy-start(bf16[2,128,2048]{2,1,0:T(8,128)(2,1)} %param.13) | copy-start | bytes 3145732
  676.5 8.7 %copy-start.1 = (bf16[256,2048]{1,0:T(8,128)(2,1)S(1)}, bf16[256,2048]{1,0:T(8,128)(2,1)}, u32[]{:S(2)}) copy-start(bf16[256,2048]{1,0:T(8,128)(2,1)} %get-tuple-element.56) | copy-start | bytes 3145732
  676.5 8.7 %copy-start.8 = (f32[1,2048]{1,0:T(1,128)S(1)}, f32[1,2048]{1,0:T(1,128)}, u32[]{:S(2)}) copy-start(f32[1,2048]{1,0:T(1,128)} %get-tuple-element.57) | copy-start | bytes 24580
  684.5 1.2 copy-start.2
Sparse Core Ops, SparseCore 0:
  134.8 155.1 all-gather.2
  293.7 159.1 reduce-scatter.1
  506.9 118.8 all-reduce.4

commit v3 on v2

--- a/solution.py
+++ b/solution.py
@@ -12,16 +12,29 @@
 BF16 = jnp.bfloat16
 
 
-def softplus(v):
-    return jnp.maximum(v, 0.0) + jnp.log(1.0 + jnp.exp(-jnp.abs(v)))
+def inverse_of(whole):
+    guess = pl.reciprocal(whole, approx=True)
+    return guess * (2.0 - whole * guess)
+
+
+def gates_of(pre):
+    small = jnp.exp2(jnp.abs(pre) * -LOG2E)
+    whole = 1.0 + small
+    log_part = jnp.where(small < 1e-3, small * (1.0 - small * (0.5 - small * (1.0 / 3.0))), jnp.log(whole))
+    return jnp.maximum(pre, 0.0) + log_part, jnp.where(pre >= 0.0, 1.0, small) * inverse_of(whole)
 
 
 def sigmoid(v):
-    return 1.0 / (1.0 + jnp.exp(-v))
+    return 0.5 + 0.5 * jnp.tanh(0.5 * v)
 
 
 def nt_dot(a, b):
     return lax.dot_general(a, b, (((1,), (1,)), ((), ())), preferred_element_type=F32)
+
+
+def lane_tiles(width):
+    step = min(width, 512)
+    return [slice(k, k + step) for k in range(0, width, step)]
 
 
 def tile_matrix(n, wide):
@@ -36,77 +49,57 @@
     return col // n == row % BLOCK
 
 
-def scan_forward_kernel(sel_ref, x_ref, gate_ref, stepw_ref, bias_ref, decay_ref, skip_ref,
-                        gated_ref, ssm_ref, start_ref,
-                        dt_s, u_s, y_s, coef_s, bt_s, hist_s, state_s, *, rank, n):
-    chunk = pl.program_id(1)
-    length = x_ref.shape[-2]
+def scan_step(selected, x, gate, fresh, stepw_ref, bias_ref, skip_ref, gated_ref, gact_ref, tail_ref, dt_ref, slope_ref,
+              u_s, y_s, coef_s, bt_s, hist_a, hist_b, state_s, rate_s, rank, n):
+    length = x.shape[0]
     wide = BLOCK * n
-
-    @pl.when(chunk == 0)
-    def _():
-        state_s[...] = jnp.zeros_like(state_s)
-
-    start_ref[...] = state_s[...].reshape(start_ref.shape)
-    selected = sel_ref[...].reshape(sel_ref.shape[-2:]).astype(F32)
-    x = x_ref[...].reshape(x_ref.shape[-2:]).astype(F32)
+    state_s[...] = jnp.where(fresh, 0.0, state_s[...])
     low = selected[:rank].T.astype(BF16)
     pre = jnp.dot(low, stepw_ref[...], preferred_element_type=F32) + bias_ref[...]
-    dt = softplus(pre)
-    dt_s[...] = dt
+    dt, slope = gates_of(pre)
+    dt_ref[...] = dt
+    slope_ref[...] = slope
     u_s[...] = dt * x
     bt_s[...] = selected[rank:]
     spread = jnp.dot(selected[rank:].T[:, n:], tile_matrix(n, wide), preferred_element_type=F32)
     coef_s[...] = jnp.where(diagonal_mask(length, n, wide), spread, 0.0).astype(BF16)
-    rate = -jnp.exp(decay_ref[...].astype(F32)) * LOG2E
-
-    def block(k, state):
+    blocks = length // BLOCK
+
+    def finish(k, hist):
+        rows = pl.ds(pl.multiple_of(k * BLOCK, BLOCK), BLOCK)
+        y_s[rows, :] = jnp.dot(coef_s[rows, :], hist[...], preferred_element_type=F32)
+
+    def block(k, state, hist):
         at = pl.multiple_of(k * BLOCK, BLOCK)
-        dts = dt_s[pl.ds(at, BLOCK), :]
+        bs = pltpu.roll(bt_s[0:n, :], length - at, 1)
+        dts = dt_ref[pl.ds(at, BLOCK), :]
         us = u_s[pl.ds(at, BLOCK), :]
-        bs = pltpu.roll(bt_s[0:n, :], length - at, 1)
+        rate = rate_s[...]
         for i in range(BLOCK):
             factor = jnp.exp2(dts[i:i + 1, :] * rate)
             state = factor * state + us[i:i + 1, :] * bs[:, i:i + 1]
-            hist_s[i * n:(i + 1) * n, :] = state.astype(BF16)
-        y_s[pl.ds(at, BLOCK), :] = jnp.dot(coef_s[pl.ds(at, BLOCK), :], hist_s[...], preferred_element_type=F32)
+            hist[i * n:(i + 1) * n, :] = state.astype(BF16)
         return state
 
-    state_s[...] = lax.fori_loop(0, length // BLOCK, block, state_s[...])
-    gate = gate_ref[...].reshape(x.shape)
+    def pair(j, state):
+        finish(jnp.maximum(2 * j - 1, 0), hist_b)
+        state = block(2 * j, state, hist_a)
+        finish(2 * j, hist_a)
+        return block(2 * j + 1, state, hist_b)
+
+    state_s[...] = lax.fori_loop(0, blocks // 2, pair, state_s[...])
+    finish(blocks - 1, hist_b)
     ssm = y_s[...] + skip_ref[...] * x
-    ssm_ref[...] = ssm.astype(ssm_ref.dtype).reshape(ssm_ref.shape)
-    gated_ref[...] = (ssm * gate * sigmoid(gate)).astype(BF16).reshape(gated_ref.shape)
-
-
-def scan_forward(sel, x, gate, stepw, bias, decay, skip, n):
-    chunks, rows, length, width = x.shape
-    rank = stepw.shape[0]
-    wide = BLOCK * n
-    tok = lambda feat: pl.BlockSpec((1, 1, length, feat), lambda r, c: (c, r, 0, 0))
-    whole = lambda a: pl.BlockSpec(a.shape, lambda r, c: (0,) * a.ndim)
-    return pl.pallas_call(
-        functools.partial(scan_forward_kernel, rank=rank, n=n),
-        grid=(rows, chunks),
-        in_specs=[pl.BlockSpec((1, 1) + sel.shape[2:], lambda r, c: (c, r, 0, 0)), tok(width), tok(width), whole(stepw), whole(bias), whole(decay), whole(skip)],
-        out_specs=[tok(width), tok(width), pl.BlockSpec((1, 1, n, width), lambda r, c: (c, r, 0, 0))],
-        out_shape=[
-            jax.ShapeDtypeStruct((chunks, rows, length, width), BF16),
-            jax.ShapeDtypeStruct((chunks, rows, length, width), BF16),
-            jax.ShapeDtypeStruct((chunks, rows, n, width), F32),
-        ],
-        scratch_shapes=[
-            pltpu.VMEM((length, width), F32), pltpu.VMEM((length, width), F32), pltpu.VMEM((length, width), F32),
-            pltpu.VMEM((length, wide), BF16), pltpu.VMEM((2 * n, length), F32),
-            pltpu.VMEM((wide, width), BF16), pltpu.VMEM((n, width), F32),
-        ],
-        name="scan_forward",
-    )(sel, x, gate, stepw, bias, decay, skip)
-
-
-def scan_backward_kernel(sel_ref, x_ref, gate_ref, gg_ref, ssm_ref, start_ref, stepw_ref, bias_ref, decay_ref, skip_ref,
+    sg = sigmoid(gate)
+    gact = gate * sg
+    gact_ref[...] = gact
+    tail_ref[...] = (ssm * sg * (1.0 + gate * (1.0 - sg))).astype(BF16)
+    gated_ref[...] = (ssm * gact).astype(BF16)
+
+
+def scan_backward_kernel(sel_ref, x_ref, gact_ref, gg_ref, tail_ref, start_ref, dt_ref, slope_ref, stepw_ref, decay_ref, skip_ref,
                          ggate_ref, gvals_ref, gpre_ref, gsel_ref, gstepw_ref, gbias_ref, gdecay_ref, gskip_ref,
-                         dt_s, u_s, gy_s, gu_s, ah_s, bcoef_s, bt_s, hist_s, adj_s, harm_s, db_s, dc_s, carry_s, gd_s, *, rank, n):
+                         dt_s, u_s, gy_s, gu_s, ah_s, bcoef_s, bt_s, hist_s, adj_a, harm_a, adj_b, harm_b, db_s, dc_s, carry_s, gd_s, rate_s, factor_s, kept_s, *, rank, n):
     row, step = pl.program_id(0), pl.program_id(1)
     length = x_ref.shape[-2]
     wide = BLOCK * n
@@ -126,87 +119,111 @@
 
     selected = flat(sel_ref).astype(F32)
     x = flat(x_ref).astype(F32)
-    gate = flat(gate_ref)
     gg = flat(gg_ref)
-    ssm = flat(ssm_ref).astype(F32)
-    sg = sigmoid(gate)
-    gy = gg * gate * sg
-    ggate_ref[...] = (gg * ssm * sg * (1.0 + gate * (1.0 - sg))).astype(BF16).reshape(ggate_ref.shape)
+    gy = gg * flat(gact_ref)
+    ggate_ref[...] = (gg * flat(tail_ref).astype(F32)).astype(BF16).reshape(ggate_ref.shape)
     gskip_ref[...] += jnp.sum(gy * x, axis=0, keepdims=True)
     gy_s[...] = gy
-    low = selected[:rank].T.astype(BF16)
-    pre = jnp.dot(low, stepw_ref[...], preferred_element_type=F32) + bias_ref[...]
-    dt = softplus(pre)
+    dt = flat(dt_ref)
     dt_s[...] = dt
     u_s[...] = dt * x
     bt_s[...] = selected[rank:]
     tiles = tile_matrix(n, wide)
     spread = jnp.dot(selected[rank:].T[:, :n], tiles, preferred_element_type=F32)
     bcoef_s[...] = jnp.where(diagonal_mask(length, n, wide), spread, 0.0).astype(BF16)
-    decay = -jnp.exp(decay_ref[...].astype(F32))
-    rate = decay * LOG2E
+    rate_s[...] = -jnp.exp(decay_ref[...].astype(F32)) * LOG2E
     keep = diagonal_mask(BLOCK, n, wide)
     ones = keep.astype(BF16)
-    start = start_ref[...].reshape(carry_s.shape)
-
-    def again(k, state):
-        at = pl.multiple_of(k * BLOCK, BLOCK)
-        dts = dt_s[pl.ds(at, BLOCK), :]
-        us = u_s[pl.ds(at, BLOCK), :]
-        bs = pltpu.roll(bt_s[0:n, :], length - at, 1)
-        for i in range(BLOCK):
-            hist_s[pl.ds(pl.multiple_of((at + i) * n, n), n), :] = state.astype(BF16)
-            factor = jnp.exp2(dts[i:i + 1, :] * rate)
-            state = factor * state + us[i:i + 1, :] * bs[:, i:i + 1]
-        return state
-
-    last = lax.fori_loop(0, blocks, again, start)
-    hist_s[pl.ds(length * n, n), :] = last.astype(BF16)
-
-    def back(j, carried):
-        carry, gd = carried
-        k = blocks - 1 - j
-        at = pl.multiple_of(k * BLOCK, BLOCK)
-        dts = dt_s[pl.ds(at, BLOCK), :]
-        gys = gy_s[pl.ds(at, BLOCK), :]
-        cs = pltpu.roll(bt_s[n:2 * n, :], length - at, 1)
-        for i in range(BLOCK - 1, -1, -1):
-            dt_i = dts[i:i + 1, :]
-            g = cs[:, i:i + 1] * gys[i:i + 1, :] + carry
-            adj_s[i * n:(i + 1) * n, :] = g.astype(BF16)
-            carry = jnp.exp2(dt_i * rate) * g
-            h = carry * hist_s[pl.ds(pl.multiple_of((at + i) * n, n), n), :].astype(F32)
-            harm_s[i * n:(i + 1) * n, :] = (h * decay).astype(BF16)
-            gd = gd + dt_i * h
-        adj = adj_s[...]
-        rows = pl.ds(at, BLOCK)
-        gu_s[rows, :] = jnp.dot(bcoef_s[rows, :], adj, preferred_element_type=F32)
-        ah_s[rows, :] = jnp.dot(ones, harm_s[...], preferred_element_type=F32)
-        db_s[rows, :] = jnp.where(keep, nt_dot(u_s[rows, :].astype(BF16), adj), 0.0)
-        states = hist_s[pl.ds(pl.multiple_of((at + 1) * n, n), wide), :]
-        dc_s[rows, :] = jnp.where(keep, nt_dot(gys.astype(BF16), states), 0.0)
-        return carry, gd
-
-    carry, gd = lax.fori_loop(0, blocks, back, (carry_s[...], gd_s[...]))
-    carry_s[...] = carry
-    gd_s[...] = gd
+    lanes = lane_tiles(x.shape[1])
+    state_s = start_ref.at[0, 0]
+
+    def steps(lane):
+        def again(k, state):
+            at = pl.multiple_of(k * BLOCK, BLOCK)
+            bs = pltpu.roll(bt_s[0:n, :], length - at, 1)
+            dts = dt_s[pl.ds(at, BLOCK), lane]
+            us = u_s[pl.ds(at, BLOCK), lane]
+            rate = rate_s[:, lane]
+            for i in range(BLOCK):
+                here = pl.ds(pl.multiple_of((at + i) * n, n), n)
+                factor = jnp.exp2(dts[i:i + 1, :] * rate)
+                factor_s[here, lane] = factor
+                old = factor * state
+                kept_s[here, lane] = old
+                state = old + us[i:i + 1, :] * bs[:, i:i + 1]
+                hist_s[here, lane] = state.astype(BF16)
+            return state
+
+        lax.fori_loop(0, blocks, again, state_s[:, lane])
+
+        def products(k, adj_s, harm_s):
+            at = pl.multiple_of(k * BLOCK, BLOCK)
+            rows = pl.ds(at, BLOCK)
+            adj = adj_s[:, lane]
+            gu_s[rows, lane] = jnp.dot(bcoef_s[rows, :], adj, preferred_element_type=F32)
+            ah_s[rows, lane] = jnp.dot(ones, harm_s[:, lane], preferred_element_type=F32)
+            db = jnp.where(keep, nt_dot(u_s[rows, lane].astype(BF16), adj), 0.0)
+            states = hist_s[pl.ds(pl.multiple_of(at * n, n), wide), lane]
+            dc = jnp.where(keep, nt_dot(gy_s[rows, lane].astype(BF16), states), 0.0)
+            if lane.start == 0:
+                db_s[rows, :] = db
+                dc_s[rows, :] = dc
+            else:
+                db_s[rows, :] += db
+                dc_s[rows, :] += dc
+
+        def block(k, carry, adj_s, harm_s):
+            at = pl.multiple_of(k * BLOCK, BLOCK)
+            cs = pltpu.roll(bt_s[n:2 * n, :], length - at, 1)
+            dts = dt_s[pl.ds(at, BLOCK), lane]
+            gys = gy_s[pl.ds(at, BLOCK), lane]
+            rate = rate_s[:, lane]
+            gd = gd_s[:, lane]
+            for i in range(BLOCK - 1, -1, -1):
+                here = pl.ds(pl.multiple_of((at + i) * n, n), n)
+                g = cs[:, i:i + 1] * gys[i:i + 1, :] + carry
+                adj_s[i * n:(i + 1) * n, lane] = g.astype(BF16)
+                carry = factor_s[here, lane] * g
+                h = g * kept_s[here, lane]
+                harm_s[i * n:(i + 1) * n, lane] = (h * rate).astype(BF16)
+                gd = gd + dts[i:i + 1, :] * h
+            gd_s[:, lane] = gd
+            return carry
+
+        def pair(j, carry):
+            k = blocks - 1 - 2 * j
+            if lane.start == 0:
+                products(jnp.minimum(k + 1, blocks - 1), adj_b, harm_b)
+            else:
+                @pl.when(j > 0)
+                def _():
+                    products(k + 1, adj_b, harm_b)
+            carry = block(k, carry, adj_a, harm_a)
+            products(k, adj_a, harm_a)
+            return block(k - 1, carry, adj_b, harm_b)
+
+        carry_s[:, lane] = lax.fori_loop(0, blocks // 2, pair, carry_s[:, lane])
+        products(0, adj_b, harm_b)
+
+    for lane in lanes:
+        steps(lane)
     gu = gu_s[...]
-    gpre = ((x * gu + ah_s[...]) * sigmoid(pre)).astype(BF16)
+    gpre = ((x * gu + ah_s[...] * (1.0 / LOG2E)) * flat(slope_ref)).astype(BF16)
     gpre_ref[...] = gpre.reshape(gpre_ref.shape)
     gvals_ref[...] = (gy * skip_ref[...] + dt * gu).astype(gvals_ref.dtype).reshape(gvals_ref.shape)
     gbias_ref[...] += jnp.sum(gpre.astype(F32), axis=0, keepdims=True)
     gstepw_ref[...] += jnp.dot(selected[:rank].astype(BF16), gpre, preferred_element_type=F32)
-    fold = lambda ref: lax.dot_general(tiles, ref[...], (((1,), (1,)), ((), ())), preferred_element_type=F32, precision=lax.Precision.HIGHEST)
+    fold = lambda ref: nt_dot(tiles.astype(BF16), ref[...].astype(BF16))
     gsel_ref[0, 0, 0:rank, :] = nt_dot(stepw_ref[...], gpre).astype(BF16)
     gsel_ref[0, 0, rank:rank + n, :] = fold(db_s).astype(BF16)
     gsel_ref[0, 0, rank + n:rank + 2 * n, :] = fold(dc_s).astype(BF16)
 
     @pl.when((row == pl.num_programs(0) - 1) & (step == pl.num_programs(1) - 1))
     def _():
-        gdecay_ref[...] = gd * decay
-
-
-def scan_backward(sel, x, gate, gg, ssm, starts, stepw, bias, decay, skip, n):
+        gdecay_ref[...] = gd_s[...] * rate_s[...] * (1.0 / LOG2E)
+
+
+def scan_backward(sel, x, gact, gg, tail, starts, dt, slope, stepw, decay, skip, n):
     chunks, rows, length, width = x.shape
     rank = stepw.shape[0]
     wide = BLOCK * n
@@ -217,8 +234,8 @@
     return pl.pallas_call(
         functools.partial(scan_backward_kernel, rank=rank, n=n),
         grid=(rows, chunks),
-        in_specs=[pl.BlockSpec((1, 1) + sel.shape[2:], at), tok(width), tok(width), tok(width), tok(width), pl.BlockSpec((1, 1, n, width), at),
-                  whole(stepw.shape), whole(bias.shape), whole(decay.shape), whole(skip.shape)],
+        in_specs=[pl.BlockSpec((1, 1) + sel.shape[2:], at), tok(width), tok(width), tok(width), tok(width), pl.BlockSpec((1, 1, n, width), at), tok(width), tok(width),
+                  whole(stepw.shape), whole(decay.shape), whole(skip.shape)],
         out_specs=[tok(width), tok(width), tok(width), pl.BlockSpec((1, 1) + sel.shape[2:], at), whole((rank, width)), whole((1, width)), whole((n, width)), whole((1, width))],
         out_shape=[
             sds(x.shape, BF16), sds(x.shape, F32), sds(x.shape, BF16), sds(sel.shape, BF16),
@@ -228,44 +245,24 @@
             pltpu.VMEM((length, width), F32), pltpu.VMEM((length, width), F32), pltpu.VMEM((length, width), F32),
             pltpu.VMEM((length, width), F32), pltpu.VMEM((length, width), F32),
             pltpu.VMEM((length, wide), BF16), pltpu.VMEM((2 * n, length), F32),
-            pltpu.VMEM(((length + 1) * n, width), BF16), pltpu.VMEM((wide, width), BF16), pltpu.VMEM((wide, width), BF16),
+            pltpu.VMEM((length * n, width), BF16), pltpu.VMEM((wide, width), BF16), pltpu.VMEM((wide, width), BF16),
+            pltpu.VMEM((wide, width), BF16), pltpu.VMEM((wide, width), BF16),
             pltpu.VMEM((length, wide), F32), pltpu.VMEM((length, wide), F32),
-            pltpu.VMEM((n, width), F32), pltpu.VMEM((n, width), F32),
+            pltpu.VMEM((n, width), F32), pltpu.VMEM((n, width), F32), pltpu.VMEM((n, width), F32),
+            pltpu.VMEM((length * n, width), F32), pltpu.VMEM((length * n, width), F32),
         ],
         name="scan_backward",
-    )(sel, x, gate, gg, ssm, starts, stepw, bias, decay, skip)
-def conv_forward_kernel(ci_ref, taps_ref, bias_ref, selw_ref, x_ref, sel_ref, ext_s):
-    length = ci_ref.shape[-2]
+    )(sel, x, gact, gg, tail, starts, dt, slope, stepw, decay, skip)
+def conv_step(ci, fresh, taps_ref, bias_ref, selw_ref, ext_s):
+    length = ci.shape[0]
     tap_count = taps_ref.shape[0]
-
-    @pl.when(pl.program_id(1) == 0)
-    def _():
-        ext_s[0:8, :] = jnp.zeros((8, ext_s.shape[1]), F32)
-
-    ext_s[8:, :] = ci_ref[...].reshape(ci_ref.shape[-2:]).astype(F32)
+    ext_s[0:8, :] = jnp.where(fresh, 0.0, ext_s[length:length + 8, :])
+    ext_s[8:, :] = ci.astype(F32)
     total = bias_ref[...].astype(F32)
     for k in range(tap_count):
         total = total + taps_ref[k:k + 1, :].astype(F32) * ext_s[pl.ds(8 - tap_count + 1 + k, length), :]
-    ext_s[0:8, :] = ext_s[length:length + 8, :]
     x = (total * sigmoid(total)).astype(BF16)
-    x_ref[...] = x.reshape(x_ref.shape)
-    sel_ref[...] = nt_dot(selw_ref[...], x).astype(BF16).reshape(sel_ref.shape)
-
-
-def conv_forward(ci, taps, bias, selw):
-    chunks, rows, length, width = ci.shape
-    tok = lambda feat: pl.BlockSpec((1, 1, length, feat), lambda r, c: (c, r, 0, 0))
-    whole = lambda a: pl.BlockSpec(a.shape, lambda r, c: (0,) * a.ndim)
-    coef = (selw.shape[0], length)
-    return pl.pallas_call(
-        conv_forward_kernel,
-        grid=(rows, chunks),
-        in_specs=[tok(width), whole(taps), whole(bias), whole(selw)],
-        out_specs=[tok(width), pl.BlockSpec((1, 1) + coef, lambda r, c: (c, r, 0, 0))],
-        out_shape=[jax.ShapeDtypeStruct(ci.shape, BF16), jax.ShapeDtypeStruct((chunks, rows) + coef, BF16)],
-        scratch_shapes=[pltpu.VMEM((length + 8, width), F32)],
-        name="conv_forward",
-    )(ci, taps, bias, selw)
+    return x, nt_dot(selw_ref[...], x).astype(BF16)
 
 
 def conv_backward_kernel(ci_ref, prev_ref, gvals_ref, gsel_ref, taps_ref, bias_ref, selw_ref,
@@ -474,9 +471,9 @@
         if split:
             spread(s)
 
-    every_other(take_first)
     if zs > 1:
         relay(1)
+    every_other(take_first)
 
     def take_second(s, _):
         for j in range(1, xs):
@@ -491,10 +488,10 @@
             shared(s, d, w2send, 0, {"dp": d}).wait_recv()
         return 0
 
+    if zs > 2:
+        relay(2)
     if split:
         lax.fori_loop(0, chunks, take_second, 0)
-    if zs > 2:
-        relay(2)
     if split:
         lax.fori_loop(0, chunks, take_third, 0)
 
@@ -632,9 +629,16 @@
     )(hidden, wq, gain)
 
 
-def total_kernel(part_ref, out_ref, recv_v, send1, recv1, send2, recv2, own_sem, *, chunks):
-    me = lax.axis_index("seq")
-    meet(chunks, 1)
+def total_kernel(*refs, chunks, copies, extra):
+    part_ref, out_ref = refs[0], refs[1 + extra]
+    early, early_out = refs[1:1 + extra], refs[2 + extra:2 + 2 * extra]
+    refs = refs[2 + 2 * extra:]
+    recv_v, send1, recv1, send2, recv2 = refs[:5]
+    bufs, sems = refs[5:5 + 3 * extra], refs[5 + 3 * extra:]
+    me, mine = lax.axis_index("seq"), lax.axis_index("dp")
+    x, c = mine // 2, mine % 2
+    xs = copies // 2
+    meet(chunks, copies if extra else 1)
 
     def first(s):
         return remote(part_ref.at[s], recv_v.at[me], send1.at[s], recv1.at[me], {"seq": s})
@@ -654,39 +658,304 @@
             return 0
         lax.fori_loop(1, chunks, one, 0)
 
+    def part_of(e, core):
+        rows = early[e].shape[0] // 2
+        return pl.ds(pl.multiple_of(core * rows, rows), rows)
+
+    def to_core(e):
+        return remote(early[e].at[part_of(e, 1 - c)], bufs[3 * e], sems[0].at[e], sems[1].at[e], {"dp": x * 2 + 1 - c})
+
+    def across(e, j):
+        return remote(bufs[3 * e + 1], bufs[3 * e + 2].at[x], sems[2].at[e, j], sems[3].at[e, x], {"dp": lax.rem(x + j, xs) * 2 + c})
+
+    def from_across(e, j):
+        q = lax.rem(x + j, xs)
+        return remote(bufs[3 * e + 2].at[q], bufs[3 * e + 2].at[q], sems[2].at[e, j], sems[3].at[e, q], {"dp": q * 2 + c})
+
+    def back(e):
+        return remote(early_out[e].at[part_of(e, c)], early_out[e].at[part_of(e, c)], sems[4].at[e], sems[5].at[e], {"dp": x * 2 + 1 - c})
+
+    def from_back(e):
+        return remote(early_out[e].at[part_of(e, 1 - c)], early_out[e].at[part_of(e, 1 - c)], sems[4].at[e], sems[5].at[e], {"dp": x * 2 + 1 - c})
+
+    def by_rows(e, fn):
+        count = early[e].shape[0] // 2
+        step = 16
+
+        def one(i, _):
+            fn(pl.multiple_of(i * step, step), step, pl.multiple_of(c * count, count) + i * step)
+            return 0
+        lax.fori_loop(0, count // step, one, 0)
+
     every_other(lambda s: first(s).start())
+    for e in range(extra):
+        to_core(e).start()
     recv_v[me] = part_ref[me]
+    for e in range(extra):
+        to_core(e).wait_recv()
+
+        def fold(at, step, full):
+            mine_rows = early[e][pl.ds(pl.multiple_of(full, step), step), :].astype(F32)
+            bufs[3 * e + 1][pl.ds(at, step), :] = (mine_rows + bufs[3 * e][pl.ds(at, step), :].astype(F32)).astype(BF16)
+
+        by_rows(e, fold)
+        for j in range(1, xs):
+            across(e, j).start()
     every_other(lambda s: landed_first(s).wait_recv())
     total = recv_v[0].astype(F32)
     for s in range(1, chunks):
         total = total + recv_v[s].astype(F32)
     out_ref[me] = total.astype(BF16)
     every_other(lambda s: second(s).start())
+    for e in range(extra):
+        for j in range(1, xs):
+            from_across(e, j).wait_recv()
+
+        def finish(at, step, full):
+            total = bufs[3 * e + 1][pl.ds(at, step), :].astype(F32)
+            for j in range(1, xs):
+                total = total + bufs[3 * e + 2][lax.rem(x + j, xs), pl.ds(at, step), :].astype(F32)
+            early_out[e][pl.ds(pl.multiple_of(full, step), step), :] = total.astype(BF16)
+
+        by_rows(e, finish)
+        back(e).start()
     every_other(lambda s: landed_second(s).wait_recv())
     every_other(lambda s: first(s).wait_send())
     every_other(lambda s: second(s).wait_send())
-
-
-def total_over_seq(part, chunks, key):
+    for e in range(extra):
+        from_back(e).wait_recv()
+        to_core(e).wait_send()
+        for j in range(1, xs):
+            across(e, j).wait_send()
+        back(e).wait_send()
+
+
+def total_over_seq(part, chunks, copies, key, early=()):
     vmem = pl.BlockSpec(memory_space=pltpu.VMEM)
     dma = pltpu.SemaphoreType.DMA
-    return pl.pallas_call(
-        functools.partial(total_kernel, chunks=chunks),
-        in_specs=[vmem],
-        out_specs=vmem,
-        out_shape=jax.ShapeDtypeStruct(part.shape, BF16),
-        scratch_shapes=[pltpu.VMEM(part.shape, BF16),
-                        dma((chunks,)), dma((chunks,)), dma((chunks,)), dma((chunks,)), dma(())],
+    extra = len(early)
+    xs = max(1, copies // 2)
+    scratch = [pltpu.VMEM(part.shape, BF16), dma((chunks,)), dma((chunks,)), dma((chunks,)), dma((chunks,))]
+    for a in early:
+        rows = a.shape[0] // 2
+        scratch += [pltpu.VMEM((rows, a.shape[1]), BF16), pltpu.VMEM((rows, a.shape[1]), BF16), pltpu.VMEM((xs, rows, a.shape[1]), BF16)]
+    if extra:
+        scratch += [dma((extra,)), dma((extra,)), dma((extra, xs)), dma((extra, xs)), dma((extra,)), dma((extra,))]
+    sds = jax.ShapeDtypeStruct
+    got = pl.pallas_call(
+        functools.partial(total_kernel, chunks=chunks, copies=copies, extra=extra),
+        in_specs=[vmem] * (1 + extra),
+        out_specs=[vmem] * (1 + extra),
+        out_shape=[sds(part.shape, BF16)] + [sds(a.shape, BF16) for a in early],
+        scratch_shapes=scratch,
         compiler_params=pltpu.CompilerParams(collective_id=key, has_side_effects=True, vmem_limit_bytes=60 * 1024 * 1024),
         name=f"total_over_seq_{key}",
-    )(part)
+    )(part, *early)
+    return got if extra else got[0]
+def forward_kernel(ci_ref, gate_ref, gm_ref, taps_ref, cbias_ref, selw_ref, stepw_ref, sbias_ref, decay_ref, skip_ref,
+                   gmall_ref, sel_ref, x_ref, gated_ref, gact_ref, tail_ref, dt_ref, slope_ref, start_ref,
+                   gate_v, part_v, recv_v, x_v, gated_v, gact_v, tail_v, dt_v, slope_v, start_v,
+                   ext_s, u_s, y_s, coef_s, bt_s, hist_a, hist_b, state_s, rate_s,
+                   load_sem, own_sem, out_sem, grecv, gside, gup, gdown, send1, recv1, send2, recv2, *, chunks, copies, n):
+    zs, ys = grid_of(chunks, copies)
+    me = lax.axis_index("seq")
+    z, y = me // ys, me % ys
+    tokens, model = gm_ref.shape
+    rows, length, width = ci_ref.shape[1:]
+    rank = stepw_ref.shape[0]
+    half = tokens // 2
+    load = pltpu.make_async_copy(gate_ref, gate_v, load_sem)
+    load.start()
+    own = pltpu.make_async_copy(gm_ref, gmall_ref.at[me], own_sem)
+    own.start()
+    meet(chunks, 1)
+
+    def block(o, yy, h):
+        return gmall_ref.at[o * ys + yy, pl.ds(h * half, half)]
+
+    def source(o, h, k):
+        return gm_ref.at[pl.ds(h * half, half)] if k is None else block(o, y, h)
+
+    def up(o, h, k=0):
+        return remote(source(o, h, k), block(o, y, h), gup.at[o, h], grecv.at[o * ys + y, h], {"seq": (z + 1) * ys + y})
+
+    def down(o, h, k=0):
+        return remote(source(o, h, k), block(o, y, h), gdown.at[o, h], grecv.at[o * ys + y, h], {"seq": (z - 1) * ys + y})
+
+    def side(o, j, h, k=0):
+        return remote(source(o, h, k), block(o, y, h), gside.at[o, j - 1, h], grecv.at[o * ys + y, h], {"seq": z * ys + lax.rem(y + j, ys)})
+
+    def landed(o, yy, h):
+        return remote(block(o, yy, h), block(o, yy, h), gside.at[o, 0, h], grecv.at[o * ys + yy, h], {"seq": lax.rem(me + 1, chunks)})
+
+    def when(cond, fn):
+        pl.when(cond)(fn)
+
+    for h in range(2):
+        when(z + 1 < zs, lambda: up(z, h, None).start())
+        when(z > 0, lambda: down(z, h, None).start())
+        for j in range(1, ys):
+            side(z, j, h, None).start()
+
+    def relay(k):
+        for h in range(2):
+            @pl.when(z - k >= 0)
+            def _():
+                landed(z - k, y, h).wait_recv()
+                when(z + 1 < zs, lambda: up(z - k, h).start())
+                for j in range(1, ys):
+                    side(z - k, j, h).start()
+
+            @pl.when(z + k < zs)
+            def _():
+                landed(z + k, y, h).wait_recv()
+                when(z > 0, lambda: down(z + k, h).start())
+                for j in range(1, ys):
+                    side(z + k, j, h).start()
+
+    rate_s[...] = -jnp.exp(decay_ref[...].astype(F32)) * LOG2E
+
+    def conv(i, _):
+        r, c = i // chunks, i % chunks
+        x, part = conv_step(ci_ref[c, r], c == 0, taps_ref, cbias_ref, selw_ref, ext_s)
+        x_v[c, r] = x
+        part_v[c, r] = part
+        return 0
+
+    lax.fori_loop(0, rows * chunks, conv, 0)
+    x_out = pltpu.make_async_copy(x_v, x_ref, out_sem.at[0, 0])
+    x_out.start()
+
+    def first(s):
+        return remote(part_v.at[s], recv_v.at[me], send1.at[s], recv1.at[me], {"seq": s})
+
+    def landed_first(s):
+        return remote(part_v.at[s], recv_v.at[s], send1.at[s], recv1.at[s], {"seq": s})
+
+    def second(s):
+        return remote(sel_ref.at[me], sel_ref.at[me], send2.at[s], recv2.at[me], {"seq": s})
+
+    def landed_second(s):
+        return remote(sel_ref.at[s], sel_ref.at[s], send2.at[s], recv2.at[s], {"seq": s})
+
+    def every_other(fn):
+        def one(k, _):
+            fn(lax.rem(me + k, chunks))
+            return 0
+        lax.fori_loop(1, chunks, one, 0)
+
+    every_other(lambda s: first(s).start())
+    recv_v[me] = part_v[me]
+    every_other(lambda s: landed_first(s).wait_recv())
+    total = recv_v[0].astype(F32)
+    for s in range(1, chunks):
+        total = total + recv_v[s].astype(F32)
+    sel_ref[me] = total.astype(BF16)
+    every_other(lambda s: second(s).start())
+    if zs > 1:
+        relay(1)
+    every_other(lambda s: landed_second(s).wait_recv())
+    load.wait()
+    pairs = ((gated_v, gated_ref), (gact_v, gact_ref), (tail_v, tail_ref), (dt_v, dt_ref), (slope_v, slope_ref), (start_v, start_ref))
+
+    def outs(c, r):
+        return [pltpu.make_async_copy(src.at[c, r], dst.at[c, r], out_sem.at[1 + k, c * rows + r]) for k, (src, dst) in enumerate(pairs)]
+
+    def scan(i, _):
+        r, c = i // chunks, i % chunks
+        start_v[c, r] = jnp.where(c == 0, 0.0, state_s[...])
+        scan_step(sel_ref[c, r].astype(F32), x_v[c, r].astype(F32), gate_v[c, r], c == 0, stepw_ref, sbias_ref, skip_ref,
+                  gated_v.at[c, r], gact_v.at[c, r], tail_v.at[c, r], dt_v.at[c, r], slope_v.at[c, r],
+                  u_s, y_s, coef_s, bt_s, hist_a, hist_b, state_s, rate_s, rank, n)
+        for one in outs(c, r):
+            one.start()
+        return 0
+
+    count = rows * chunks
+    parts = max(1, zs - 2)
+    for k in range(parts):
+        lax.fori_loop(count * k // parts, count * (k + 1) // parts, scan, 0)
+        if 2 + k < zs:
+            relay(2 + k)
+
+    def others(o, _):
+        for j in range(1, ys):
+            for h in range(2):
+                landed(o, lax.rem(y + j, ys), h).wait_recv()
+        return 0
+
+    lax.fori_loop(0, zs, others, 0)
+    own.wait()
+    x_out.wait()
+
+    def settle(i, _):
+        for one in outs(i // rows, i % rows):
+            one.wait()
+        return 0
+
+    lax.fori_loop(0, count, settle, 0)
+    every_other(lambda s: first(s).wait_send())
+    every_other(lambda s: second(s).wait_send())
+
+    def drain(k, _):
+        for h in range(2):
+            @pl.when(z - k >= 0)
+            def _():
+                when(z + 1 < zs, lambda: up(z - k, h).wait_send())
+                for j in range(1, ys):
+                    side(z - k, j, h).wait_send()
+
+            @pl.when((z + k < zs) & (k > 0))
+            def _():
+                when(z > 0, lambda: down(z + k, h).wait_send())
+                for j in range(1, ys):
+                    side(z + k, j, h).wait_send()
+        return 0
+
+    lax.fori_loop(0, zs, drain, 0)
+    for h in range(2):
+        when(z > 0, lambda: down(z, h).wait_send())
+
+
+def forward(ci, gate, gm, taps, cbias, selw, stepw, sbias, decay, skip, copies, n):
+    chunks, rows, length, width = ci.shape
+    tokens, model = gm.shape
+    zs, ys = grid_of(chunks, copies)
+    wide = BLOCK * n
+    sds = jax.ShapeDtypeStruct
+    dma = pltpu.SemaphoreType.DMA
+    vmem = pl.BlockSpec(memory_space=pltpu.VMEM)
+    hbm = pl.BlockSpec(memory_space=pl.ANY)
+    coef = (chunks, rows, selw.shape[0], length)
+    starts = (chunks, rows, n, width)
+    full = ci.shape
+    return pl.pallas_call(
+        functools.partial(forward_kernel, chunks=chunks, copies=copies, n=n),
+        in_specs=[vmem, hbm] + [vmem] * 8,
+        out_specs=[hbm, vmem] + [hbm] * 7,
+        out_shape=[sds((chunks, tokens, model), BF16), sds(coef, BF16), sds(full, BF16), sds(full, BF16), sds(full, F32), sds(full, BF16),
+                   sds(full, F32), sds(full, F32), sds(starts, F32)],
+        scratch_shapes=[
+            pltpu.VMEM(full, F32), pltpu.VMEM(coef, BF16), pltpu.VMEM(coef, BF16), pltpu.VMEM(full, BF16), pltpu.VMEM(full, BF16),
+            pltpu.VMEM(full, F32), pltpu.VMEM(full, BF16), pltpu.VMEM(full, F32), pltpu.VMEM(full, F32), pltpu.VMEM(starts, F32),
+            pltpu.VMEM((length + 8, width), F32), pltpu.VMEM((length, width), F32), pltpu.VMEM((length, width), F32),
+            pltpu.VMEM((length, wide), BF16), pltpu.VMEM((2 * n, length), F32), pltpu.VMEM((wide, width), BF16), pltpu.VMEM((wide, width), BF16),
+            pltpu.VMEM((n, width), F32), pltpu.VMEM((n, width), F32),
+            dma(()), dma(()), dma((7, rows * chunks)), dma((chunks, 2)), dma((zs, max(1, ys - 1), 2)), dma((zs, 2)), dma((zs, 2)),
+            dma((chunks,)), dma((chunks,)), dma((chunks,)), dma((chunks,)),
+        ],
+        compiler_params=pltpu.CompilerParams(collective_id=1, has_side_effects=True, vmem_limit_bytes=60 * 1024 * 1024),
+        name="forward",
+    )(ci, gate, gm, taps, cbias, selw, stepw, sbias, decay, skip)
+
+
 def order_of(zs):
     return [sorted(range(zs), key=lambda t: (-abs(t - z), t)) for z in range(zs)]
 
 
 def scatter_kernel(*refs, chunks, copies, split):
     if split:
-        (gc_ref, gg_ref, w_ref, late_ref, gin_ref, red_ref, sum_ref, all_ref,
+        (gc_ref, gg_ref, w_ref, late_ref, ginc_ref, ging_ref, red_ref, sum_ref, all_ref,
          ysend_v, yrecv_v, own_v, zrecv_v, late_v, w_v, g1_v, mine_v, g2_v, t_v, fin_v, load_sem,
          ysend, yrecv, zup, zdown, zrecv, lsend, lrecv,
          g1send, g1recv, g2send, g2recv, g3send, g3recv, g4send, g4recv) = refs
@@ -716,9 +985,13 @@
     if split:
         piece, inner2 = fin_v.shape
         inner = inner2 // 2
-        loads = [pltpu.make_async_copy(gin_ref.at[:, q * 2 + c], mine_v.at[q], load_sem.at[1 + q]) for q in range(xs)]
-        for one in loads:
-            one.start()
+        sides = (ginc_ref, ging_ref)
+        cols = [pl.ds(part * width, width) for part in range(2)]
+        loads = [[pltpu.make_async_copy(sides[part].at[:, q * 2 + c], mine_v.at[q, :, :, cols[part]], load_sem.at[1 + q * 2 + part]) for part in range(2)]
+                 for q in range(xs)]
+        for q in range(xs):
+            for part in range(2):
+                loads[q][part].start()
     meet(chunks, copies)
 
     def late_to(d):
@@ -734,11 +1007,12 @@
         lax.fori_loop(1, copies, one, 0)
 
     if split:
-        def g1(q):
-            return remote(gin_ref.at[:, q * 2 + 1 - c], g1_v.at[q], g1send.at[q], g1recv.at[q], {"dp": x * 2 + 1 - c})
+        def g1(q, part):
+            return remote(sides[part].at[:, q * 2 + 1 - c], g1_v.at[q, :, :, cols[part]], g1send.at[q, part], g1recv.at[q, part], {"dp": x * 2 + 1 - c})
 
         for q in range(xs):
-            g1(q).start()
+            for part in range(2):
+                g1(q, part).start()
     every_copy(lambda d: late_to(d).start())
     w_in.wait()
 
@@ -756,6 +1030,7 @@
         return remote(ysend_v.at[k % ysend_v.shape[0], rows], yrecv_v.at[k, rows], ysend.at[k, h], yrecv.at[k, h], {"seq": z * ys + lax.rem(y + j, ys)})
 
     slots = ysend_v.shape[0]
+    ahead = 2 if slots == zs * (ys - 1) else zs
     for i in range(zs):
         for j in range(1, ys):
             k = i * (ys - 1) + j - 1
@@ -763,8 +1038,9 @@
                 for h in range(2):
                     to_side((k - slots) // (ys - 1), (k - slots) % (ys - 1) + 1, h).wait_send()
             partial(dest(i) * ys + lax.rem(y + j, ys), ysend_v, k % slots)
-            for h in range(2):
-                to_side(i, j, h).start()
+            if i < ahead:
+                for h in range(2):
+                    to_side(i, j, h).start()
 
     def add_into(total, terms):
         def one(r, _):
@@ -781,8 +1057,9 @@
             return remote(g2_v.at[q], g2_v.at[q], g2send.at[q], g2recv.at[q], {"dp": q * 2 + c})
 
         for q in range(xs):
-            loads[q].wait()
-            g1(q).wait_recv()
+            for part in range(2):
+                loads[q][part].wait()
+                g1(q, part).wait_recv()
 
             def fold(s, _):
                 mine_v[q, s] = (mine_v[q, s].astype(F32) + g1_v[q, s].astype(F32)).astype(BF16)
@@ -884,6 +1161,10 @@
                     total = total + yrecv_v[i * (ys - 1) + j - 1, sl, :].astype(F32)
                 return total
 
+            if h == 0 and i + ahead < zs:
+                for j in range(1, ys):
+                    for g in range(2):
+                        to_side(i + ahead, j, g).start()
             if ys > 1:
                 accumulate(t, h, side_sum)
 
@@ -946,7 +1227,8 @@
                 sink(t, h).wait_send()
     if split:
         for q in range(xs):
-            g1(q).wait_send()
+            for part in range(2):
+                g1(q, part).wait_send()
 
             @pl.when(q != x)
             def _():
@@ -959,7 +1241,7 @@
             g4(lax.rem(x + j, xs) * 2 + c, xs - 1 + j, mine).wait_send()
 
 
-def scatter_sums(gc, gg, w_all, late, gin, chunks, copies, split):
+def scatter_sums(gc, gg, w_all, late, ginc, ging, chunks, copies, split):
     tokens, width = gc.shape[1:]
     model = w_all.shape[0]
     zs, ys = grid_of(chunks, copies)
@@ -977,17 +1259,17 @@
     scratch = [pltpu.VMEM((slots, tokens, model), BF16), pltpu.VMEM((others, tokens, model), BF16),
                pltpu.VMEM((zs, tokens, model), BF16), pltpu.VMEM((zs + 1, tokens, model), BF16),
                pltpu.VMEM((copies,) + late.shape, F32), pltpu.VMEM(w_all.shape, BF16)]
-    sems = [dma((1 + xs,)), dma((others, 2)), dma((others, 2)), dma((zs, 2)), dma((zs, 2)), dma((zs + 1, 2)), dma((copies,)), dma((copies,))]
+    sems = [dma((1 + 2 * xs,)), dma((others, 2)), dma((others, 2)), dma((zs, 2)), dma((zs, 2)), dma((zs + 1, 2)), dma((copies,)), dma((copies,))]
     if split:
-        piece = gin.shape[2]
+        piece = ginc.shape[2]
         slab = (xs, chunks, piece, 2 * width)
-        args.append(gin)
-        in_specs.append(any_spec)
+        args += [ginc, ging]
+        in_specs += [any_spec] * 2
         out_specs.append(any_spec)
         out_shape.append(sds((copies * piece, 2 * chunks * width), BF16))
         scratch += [pltpu.VMEM(slab, BF16), pltpu.VMEM(slab, BF16), pltpu.VMEM(slab, BF16), pltpu.VMEM(slab[1:], BF16),
                     pltpu.VMEM((piece, 2 * chunks * width), BF16)]
-        sems += [dma((xs,)), dma((xs,)), dma((xs,)), dma((xs,)), dma((chunks, 2)), dma((chunks, 2)), dma((2 * xs,)), dma((copies,))]
+        sems += [dma((xs, 2)), dma((xs, 2)), dma((xs,)), dma((xs,)), dma((chunks, 2)), dma((chunks, 2)), dma((2 * xs,)), dma((copies,))]
     return pl.pallas_call(
         functools.partial(scatter_kernel, chunks=chunks, copies=copies, split=split),
         in_specs=in_specs,
@@ -1019,17 +1301,15 @@
     slots = here * length + lax.broadcasted_iota(jnp.int32, (rows, length), 1)
     valid = (slots < lengths[:, None]).astype(F32)[..., None]
     cotangent = grad_out.astype(F32) * valid
-    behind, gain_row = lax.optimization_barrier((cotangent.astype(BF16), gain_row))
-    gm = lax.all_gather(behind, "seq", axis=0).reshape(tokens, model)
-
     shaped = lambda a: a.reshape(chunks, rows, length, a.shape[-1])
     ci, gate = shaped(ci), shaped(gate)
     bias_row = conv_bias.reshape(1, width)
-    x, partial = conv_forward(ci, conv_weight, bias_row, select_weight)
-    sel = total_over_seq(partial, chunks, 1)
     step_row = step_bias.reshape(1, width)
     skip_row = skip_weight.reshape(1, width)
-    gated, ssm, starts = scan_forward(sel, x, gate, step_weight, step_row, decay_log, skip_row, n)
+    gm, sel, x, gated, gact, tail, dt, slope, starts = forward(
+        ci, gate, cotangent.astype(BF16).reshape(rows * length, model), conv_weight, bias_row, select_weight,
+        step_weight, step_row, decay_log, skip_row, copies, n)
+    gm = gm.reshape(tokens, model)
     gated2 = gated.reshape(tokens, width)
     mixed = jnp.dot(gated2, output_weight, preferred_element_type=F32).astype(BF16)
     mixed = lax.psum_scatter(shaped(mixed), "seq", scatter_dimension=0, tiled=False)
@@ -1038,26 +1318,28 @@
 
     gg = shaped(lax.dot_general(gm, output_weight, (((1,), (1,)), ((), ())), preferred_element_type=F32))
     ggate, gvals, gpre, gpart, gstepw, gstepb, gdecay, gskip = scan_backward(
-        sel, x, gate, gg, ssm, starts, step_weight, step_row, decay_log, skip_row, n)
-    gsel = total_over_seq(gpart, chunks, 2)
+        sel, x, gact, gg, tail, starts, dt, slope, step_weight, decay_log, skip_row, n)
     tn = lambda a, b: lax.dot_general(a, b, (((0,), (0,)), ((), ())), preferred_element_type=F32)
-    gout = tn(gated2, gm)
-    gstepw, gstepb, gdecay, gskip, gout = lax.psum((gstepw, gstepb, gdecay, gskip, gout), "dp")
+    gout = tn(gated2, gm).astype(BF16)
+    small = jnp.concatenate([gstepw, gdecay, gstepb, gskip], axis=0).astype(BF16)
+    small = jnp.pad(small, ((0, -small.shape[0] % 32), (0, 0)))
+    gsel, gout, small = total_over_seq(gpart, chunks, copies, 2, (gout, small))
+    gout, small = gout.astype(F32), small.astype(F32)
+    gstepw, gdecay, gstepb, gskip = small[:rank], small[rank:rank + n], small[rank + n], small[rank + n + 1]
     gci, gtaps, gconvb, gselw = conv_backward(ci, gvals, gsel, conv_weight, bias_row, select_weight)
     tap_count = gtaps.shape[0]
     gci2 = gci.reshape(tokens, width)
     ggate2 = ggate.reshape(tokens, width)
-    gin = jnp.concatenate([tn(normed, gci2).astype(BF16), tn(normed, ggate2).astype(BF16)], axis=1)
-    gin = gin.reshape(chunks, copies, share // copies, 2 * width)
+    ginc, ging = (tn(normed, g).astype(BF16).reshape(chunks, copies, share // copies, width) for g in (gci2, ggate2))
     late = jnp.concatenate([gselw, gtaps, gconvb], axis=0)
     late = jnp.pad(late, ((0, -late.shape[0] % 8), (0, 0)))
     flat = lambda a: a.reshape(chunks, rows * length, width)
-    got = scatter_sums(flat(gci), flat(ggate), w_all, late, gin, chunks, copies, split)
+    got = scatter_sums(flat(gci), flat(ggate), w_all, late, ginc, ging, chunks, copies, split)
     scaled, late = got[:2]
     if split:
         gin = got[2].astype(F32)
     else:
-        gin = gin.reshape(chunks, copies, share // copies, 2, width)
+        gin = jnp.stack([ginc, ging], axis=3)
         gin = lax.psum_scatter(gin, "dp", scatter_dimension=1, tiled=False)
         gin = lax.all_to_all(gin, "seq", split_axis=0, concat_axis=2, tiled=False)
         gin = lax.all_gather(gin.reshape(share // copies, 2 * chunks * width), "dp", axis=0, tiled=True).astype(F32)
@@ -1067,8 +1349,8 @@
     ghidden = inverse * scaled - source * inverse ** 3 * jnp.mean(scaled * source, axis=-1, keepdims=True) + cotangent
     picked = gselw.shape[0]
     gselw, gtaps, gconvb = late[:picked], late[picked:picked + tap_count], late[picked + tap_count]
-    return (output, ghidden, ggain, gin, gtaps, gconvb, gselw, gstepw, gstepb.reshape(width),
-            gdecay, gskip.reshape(width), gout)
+    return (output, ghidden, ggain, gin, gtaps, gconvb, gselw, gstepw, gstepb,
+            gdecay, gskip, gout)
 
 
 def solution(mesh):

time: 707 us -> 633 us (0.90)
  Pallas kernels: 563 us -> 532 us
  waiting for transfers between devices: 27.4 us -> 0.02 us
  blocking collectives: 11.9 us -> 0 us
  local copies, waits for them, and re-layouts: 20.6 us -> 12.5 us
    pallas_call x1, Pallas kernels: 121 us -> 92.2 us  [scan_backward(): pl.pallas_call(functools.partial(scan_backward_kernel, rank=rank, n=n), g...]
    all_gather x1 -> x0, waiting for transfers between devices: 27.3 us -> none  [local(): gm = lax.all_gather(behind, 'seq', axis=0).reshape(tokens, model)]
    pallas_call x4 -> x2, Pallas kernels: 162 us -> 181 us  [the longest x1 122 us: forward(): pl.pallas_call(functools.partial(forward_kernel, chunks=chunks, copies=co...]
    pallas_call x1, Pallas kernels: 140 us -> 124 us  [scatter_sums(): pl.pallas_call(functools.partial(scatter_kernel, chunks=chunks, copies=co...]
    psum x1 -> x0, blocking collectives: 11.9 us -> none  [local(): lax.psum((gstepw, gstepb, gdecay, gskip, gout), 'dp')]
    unnamed x44 -> x18, local copies, waits for them, and re-layouts: 8.02 us -> 0.04 us
  transfers between devices with their start and end apart: 3 -> 1, of which waited for: 1 -> 0; matrix products, arithmetic and copies ran while one was open for 10% -> 10% of each run, Pallas kernels for 63% -> 46%
where the time goes in v3:
time: 633 us; the launch traced here: 632 us
  Pallas kernels  532 us (84%)
  matrix products  46.5 us (7%)
  other arithmetic  26.2 us (4%)
  between operations  14.1 us (2%)
  local copies, waits for them, and re-layouts  12.5 us (2%)
    pallas_call x1, Pallas kernels, scatter_sums(): pl.pallas_call(functools.partial(scatter_kernel, chunks=chunks, copies=co...  124 us
    pallas_call x1, Pallas kernels, forward(): pl.pallas_call(functools.partial(forward_kernel, chunks=chunks, copies=co...  122 us
    pallas_call x1, Pallas kernels, gather_project(): pl.pallas_call(functools.partial(gather_project_kernel, chunks=chunks, co...  119 us
    pallas_call x1, Pallas kernels, scan_backward(): pl.pallas_call(functools.partial(scan_backward_kernel, rank=rank, n=n), g...  92.2 us
    pallas_call x1, Pallas kernels, total_over_seq(): pl.pallas_call(functools.partial(total_kernel, chunks=chunks, copies=copi...  58.3 us
    dot_general x3, matrix products, local(): lax.dot_general(a, b, (((0,), (0,)), ((), ())), preferred_element_type=F32)  28.6 us
    pallas_call x1, Pallas kernels, conv_backward(): pl.pallas_call(conv_backward_kernel, grid=(rows, chunks), in_specs=[tok(w...  16.9 us
  transfers between devices with their start and end apart: 1, of which 0 were waited for; matrix products, arithmetic and copies ran while one was open for 10% of the time, Pallas kernels for 46%

profile of v3, /device:TPU:0, one launch (start us, length us, event | category | flops | bytes accessed | tf_op | source)
XLA Modules:
  0.0 631.8 jit_solution(5873002745751681134)
XLA Ops:
  7.2 1.2 convert_element_type.65
  8.5 1.3 reshape.136.cbias_ref.bias_ref
  9.7 1.3 reshape.138.skip_ref
  11.0 1.3 reshape.137.sbias_ref
  12.2 0.7 compare_convert_fusion
  13.0 2.4 fusion.10
  15.4 118.5 %gather_project.1 = (bf16[8,256,2048]{2,1,0:T(8,128)(2,1)}, bf16[8,256,512]{2,1,0:T(8,128)(2,1)}, f32[8,256,512]{2,1,0:T(8,128)}, bf16[2048,1024]{1,0:T(8,128)(2,1)}, f32[1,2048]{1,0:T(1,128)}) custom-call(bf16[256,2048]{1,0:T(8,128)(2,1)} %bitcast.43, bf16[256,8192]{1,0:T(8,128)(2,1)} %wq_ref.1, f32[1,256]{1,0:T(1,128)} %bitcast.59), custom_call_target="tpu_custom_call" | custom-call | tf_op jit(solution)/shard_map/gather_project/pallas_call | solution.py:614
  133.9 122.4 %forward.1 = (bf16[8,256,2048]{2,1,0:T(8,128)(2,1)}, bf16[8,2,160,128]{3,2,1,0:T(8,128)(2,1)}, bf16[8,2,128,512]{3,2,1,0:T(8,128)(2,1)}, bf16[8,2,128,512]{3,2,1...) custom-call(bf16[8,2,128,512]{3,2,1,0:T(8,128)(2,1)} %bitcast.40, ...), custom_call_target="tpu_custom_call" | custom-call | tf_op jit(solution)/shard_map/forward/pallas_call | solution.py:932
  256.3 8.3 %convolution_convert_fusion = bf16[2048,2048]{1,0:T(8,128)(2,1)} fusion(bf16[2048,512]{1,0:T(8,128)(2,1)} %bitcast.64, bf16[512,2048]{1,0:T(8,128)(2,1)S(1)} %copy-done.7), kind=kOutput, calls=%fused_computation.1 | convolution fusion | flops 4299161600 | bytes 12582912 | tf_op jit(solution)/shard_map/dot_general | solution.py:1314
  264.7 9.5 %fusion.8.gg_ref = f32[8,2,128,512]{3,2,1,0:T(8,128)} fusion(bf16[8,2,128,2048]{3,2,1,0:T(8,128)(2,1)} %bitcast.62, bf16[512,2048]{1,0:T(8,128)(2,1)S(1)} %copy-done.7), kind=kOutput, calls=%fused_computation.18 | convolution fusion | flops 4294967296 | bytes 14680064 | tf_op jit(solution)/shard_map/dot_general | solution.py:1319
  274.2 92.2 %scan_backward.1 = (bf16[8,2,128,512]{3,2,1,0:T(8,128)(2,1)}, f32[8,2,128,512]{3,2,1,0:T(8,128)}, bf16[8,2,128,512]{3,2,1,0:T(8,128)(2,1)}, bf16[8,2,160,128]{3,...) custom-call(bf16[8,2,160,128]{3,2,1,0:T(8,128)(2,1)} %get-tuple-element.46.se, ...), custom_call_target="tpu_custom_call" | custom-call | tf_op jit(solution)/shard_map/scan_backward/pallas_call | solution.py:234
  366.4 0.7 convert.16
  367.1 0.7 convert.17
  367.8 0.8 convert.15
  368.5 1.0 convert.14
  369.5 0.7 fusion.17.refs_2_
  370.2 9.1 %convolution_convert_fusion.3.refs_1_ = bf16[512,2048]{1,0:T(8,128)(2,1)} fusion(bf16[2048,512]{1,0:T(8,128)(2,1)S(1)} %bitcast.65, bf16[2048,2048]{1,0:T(8,128)(2,1)} %bitcast.63), kind=kOutput, calls=%fused_computation.8 | convolution fusion | flops 4296015872 | bytes 12582912 | tf_op jit(solution)/shard_map/dot_general | solution.py:1322
  379.3 58.3 %total_over_seq_2.1 = (bf16[8,2,160,128]{3,2,1,0:T(8,128)(2,1)}, bf16[512,2048]{1,0:T(8,128)(2,1)}, bf16[160,512]{1,0:T(8,128)(2,1)}) custom-call(bf16[8,2,160,128]{3,2,1,0:T(8,128)(2,1)} %get-tuple-element.55.refs_0_, bf16[512,2048]{1,0:T(8,128)(2,1)} %convolution_convert_fusion.3.refs_1_, bf16[160,512]{1,0:T(8,128)(2,1)} %fusion.17.refs_2_), custom_call_target="tpu_custom_call" | custom-call | tf_op jit(solution)/shard_map/total_over_seq_2/pallas_call | solution.py:745
  437.6 1.3 slice.30
  438.9 1.6 slice.28
  440.6 16.9 %conv_backward.1 = (bf16[8,2,128,512]{3,2,1,0:T(8,128)(2,1)}, f32[4,512]{1,0:T(4,128)}, f32[1,512]{1,0:T(1,128)}, f32[160,512]{1,0:T(8,128)}) custom-call(bf16[8,2,128,512]{3,2,1,0:T(8,128)(2,1)} %bitcast.41, bf16[8,2,128,512]{3,2,1,0:T(8,128)(2,1)} %bitcast.42, f32[8,2,128,512]{3,2,1,0:T(8,128)} %get-tuple-element.54.gvals_ref, ...), custom_call_target="tpu_custom_call" | custom-call | tf_op jit(solution)/shard_map/conv_backward/pallas_call | solution.py:316
  457.5 1.8 select_maximum_fusion.refs_3_
  459.2 10.0 %convolution_convert_fusion.2 = bf16[2048,512]{1,0:T(8,128)(2,1)} fusion(bf16[2048,2048]{1,0:T(8,128)(2,1)} %bitcast.60, bf16[2048,512]{1,0:T(8,128)(2,1)} %bitcast.50), kind=kOutput, calls=%fused_computation.7 | convolution fusion | flops 4296015872 | bytes 12582912 | tf_op jit(solution)/shard_map/dot_general | solution.py:1322
  469.3 9.5 %convolution_convert_fusion.1 = bf16[2048,512]{1,0:T(8,128)(2,1)} fusion(bf16[2048,2048]{1,0:T(8,128)(2,1)} %bitcast.61, bf16[2048,512]{1,0:T(8,128)(2,1)S(1)} %bitcast.49), kind=kOutput, calls=%fused_computation.6 | convolution fusion | flops 4296015872 | bytes 12582912 | tf_op jit(solution)/shard_map/dot_general | solution.py:1322
  478.7 124.1 %scatter_sums.1 = (bf16[256,2048]{1,0:T(8,128)(2,1)}, f32[168,512]{1,0:T(8,128)}, bf16[256,8192]{1,0:T(8,128)(2,1)}) custom-call(bf16[8,256,512]{2,1,0:T(8,128)(2,1)} %bitcast.51, bf16[8,256,512]{2,1,0:T(8,128)(2,1)} %bitcast.48, bf16[2048,1024]{1,0:T(8,128)(2,1)} %get-tuple-element.63.refs_2_, f32[168,512]{1,0:T(8,128)} %select_maximum_fusion.refs_3_, ...), custom_call_target="tpu_custom_call" | custom-call | tf_op jit(solution)/shard_map/scatter_sums/pallas_call | solution.py:1273
  602.9 1.3 slice.22
  604.2 1.3 slice.21
  605.5 1.7 slice.23
  607.2 4.3 convert_element_type.81
  611.5 6.8 %multiply_reduce_fusion = (f32[256]{0:T(256)S(1)}, f32[256,8192]{1,0:T(8,128)}) fusion(bf16[256,8192]{1,0:T(8,128)(2,1)S(1)} %copy-done, bf16[256,8192]{1,0:T(8,128)(2,1)} %get-tuple-element.70), kind=kLoop, calls=%fused_computation | loop fusion | flops 8388352 | bytes 16778240 | tf_op jit(solution)/shard_map/reduce_sum | solution.py:1346
  619.5 1.4 fusion.18
  620.9 4.0 fusion.5
  (25 shorter events, 1.3 us)
Async XLA Ops:
  7.2 613.7 %reduce-scatter.2.cloned.1.call-start = ((), (), s32[]{:S(2)}) async-start(), calls=%async_computation.1 | async-start | bytes 9437184 | tf_op jit(solution)/shard_map/reduce_scatter | solution.py:1315
  133.9 122.4 %copy-start.7 = (bf16[512,2048]{1,0:T(8,128)(2,1)S(1)}, bf16[512,2048]{1,0:T(8,128)(2,1)}, u32[]{:S(2)}) copy-start(bf16[512,2048]{1,0:T(8,128)(2,1)} %param.25) | copy-start | bytes 6291460
  274.2 96.0 %copy-start.8 = (bf16[8,2,128,512]{3,2,1,0:T(8,128)(2,1)S(1)}, bf16[8,2,128,512]{3,2,1,0:T(8,128)(2,1)}, u32[]{:S(2)}) copy-start(bf16[8,2,128,512]{3,2,1,0:T(8,128)(2,1)} %get-tuple-element.45) | copy-start | bytes 6291460
  459.2 10.0 %copy-start.4 = (bf16[8,2,128,512]{3,2,1,0:T(8,128)(2,1)S(1)}, bf16[8,2,128,512]{3,2,1,0:T(8,128)(2,1)}, u32[]{:S(2)}) copy-start(bf16[8,2,128,512]{3,2,1,0:T(8,128)(2,1)} %get-tuple-element.62) | copy-start | bytes 6291460
  607.2 4.3 copy-start
  611.5 6.8 %copy-start.6 = (bf16[256]{0:T(256)(128)(2,1)S(1)}, bf16[256]{0:T(256)(128)(2,1)}, u32[]{:S(2)}) copy-start(bf16[256]{0:T(256)(128)(2,1)} %param.16) | copy-start | bytes 1540
  611.5 7.4 %copy-start.1 = (bf16[2,128,2048]{2,1,0:T(8,128)(2,1)S(1)}, bf16[2,128,2048]{2,1,0:T(8,128)(2,1)}, u32[]{:S(2)}) copy-start(bf16[2,128,2048]{2,1,0:T(8,128)(2,1)} %param.13) | copy-start | bytes 3145732
  611.5 7.4 %copy-start.2 = (bf16[256,2048]{1,0:T(8,128)(2,1)S(1)}, bf16[256,2048]{1,0:T(8,128)(2,1)}, u32[]{:S(2)}) copy-start(bf16[256,2048]{1,0:T(8,128)(2,1)} %get-tuple-element.68) | copy-start | bytes 3145732
  611.5 7.4 %copy-start.5 = (f32[1,2048]{1,0:T(1,128)S(1)}, f32[1,2048]{1,0:T(1,128)}, u32[]{:S(2)}) copy-start(f32[1,2048]{1,0:T(1,128)} %get-tuple-element.69) | copy-start | bytes 24580
  618.3 2.6 copy-start.3
Sparse Core Ops, SparseCore 0:
  264.8 178.9 reduce-scatter.1

commit v4 on v3

--- a/solution.py
+++ b/solution.py
@@ -97,51 +97,34 @@
     gated_ref[...] = (ssm * gact).astype(BF16)
 
 
-def scan_backward_kernel(sel_ref, x_ref, gact_ref, gg_ref, tail_ref, start_ref, dt_ref, slope_ref, stepw_ref, decay_ref, skip_ref,
-                         ggate_ref, gvals_ref, gpre_ref, gsel_ref, gstepw_ref, gbias_ref, gdecay_ref, gskip_ref,
-                         dt_s, u_s, gy_s, gu_s, ah_s, bcoef_s, bt_s, hist_s, adj_a, harm_a, adj_b, harm_b, db_s, dc_s, carry_s, gd_s, rate_s, factor_s, kept_s, *, rank, n):
-    row, step = pl.program_id(0), pl.program_id(1)
-    length = x_ref.shape[-2]
+def back_step(selected, x, fresh, gact_ref, gg_ref, tail_ref, start_ref, dt_ref, slope_ref, stepw_ref, skip_ref,
+              ggate_ref, gvals_ref, gsel_ref, gstepw_ref, gbias_ref, gskip_ref,
+              u_s, gy_s, gu_s, ah_s, bcoef_s, bt_s, hist_s, adj_a, harm_a, adj_b, harm_b, db_s, dc_s, carry_s, gd_s, rate_s, factor_s, kept_s, rank, n):
+    length = x.shape[0]
     wide = BLOCK * n
     blocks = length // BLOCK
-    flat = lambda ref: ref[...].reshape(ref.shape[-2:])
-
-    @pl.when(step == 0)
-    def _():
-        carry_s[...] = jnp.zeros_like(carry_s)
-
-    @pl.when((step == 0) & (row == 0))
-    def _():
-        gstepw_ref[...] = jnp.zeros_like(gstepw_ref)
-        gbias_ref[...] = jnp.zeros_like(gbias_ref)
-        gskip_ref[...] = jnp.zeros_like(gskip_ref)
-        gd_s[...] = jnp.zeros_like(gd_s)
-
-    selected = flat(sel_ref).astype(F32)
-    x = flat(x_ref).astype(F32)
-    gg = flat(gg_ref)
-    gy = gg * flat(gact_ref)
-    ggate_ref[...] = (gg * flat(tail_ref).astype(F32)).astype(BF16).reshape(ggate_ref.shape)
+    carry_s[...] = jnp.where(fresh, 0.0, carry_s[...])
+    gg = gg_ref[...]
+    gy = gg * gact_ref[...]
+    ggate_ref[...] = (gg * tail_ref[...].astype(F32)).astype(BF16)
     gskip_ref[...] += jnp.sum(gy * x, axis=0, keepdims=True)
     gy_s[...] = gy
-    dt = flat(dt_ref)
-    dt_s[...] = dt
+    dt = dt_ref[...]
     u_s[...] = dt * x
     bt_s[...] = selected[rank:]
     tiles = tile_matrix(n, wide)
     spread = jnp.dot(selected[rank:].T[:, :n], tiles, preferred_element_type=F32)
     bcoef_s[...] = jnp.where(diagonal_mask(length, n, wide), spread, 0.0).astype(BF16)
-    rate_s[...] = -jnp.exp(decay_ref[...].astype(F32)) * LOG2E
     keep = diagonal_mask(BLOCK, n, wide)
     ones = keep.astype(BF16)
     lanes = lane_tiles(x.shape[1])
-    state_s = start_ref.at[0, 0]
+    state_s = start_ref
 
     def steps(lane):
         def again(k, state):
             at = pl.multiple_of(k * BLOCK, BLOCK)
             bs = pltpu.roll(bt_s[0:n, :], length - at, 1)
-            dts = dt_s[pl.ds(at, BLOCK), lane]
+            dts = dt_ref[pl.ds(at, BLOCK), lane]
             us = u_s[pl.ds(at, BLOCK), lane]
             rate = rate_s[:, lane]
             for i in range(BLOCK):
@@ -175,7 +158,7 @@
         def block(k, carry, adj_s, harm_s):
             at = pl.multiple_of(k * BLOCK, BLOCK)
             cs = pltpu.roll(bt_s[n:2 * n, :], length - at, 1)
-            dts = dt_s[pl.ds(at, BLOCK), lane]
+            dts = dt_ref[pl.ds(at, BLOCK), lane]
             gys = gy_s[pl.ds(at, BLOCK), lane]
             rate = rate_s[:, lane]
             gd = gd_s[:, lane]
@@ -208,51 +191,16 @@
     for lane in lanes:
         steps(lane)
     gu = gu_s[...]
-    gpre = ((x * gu + ah_s[...] * (1.0 / LOG2E)) * flat(slope_ref)).astype(BF16)
-    gpre_ref[...] = gpre.reshape(gpre_ref.shape)
-    gvals_ref[...] = (gy * skip_ref[...] + dt * gu).astype(gvals_ref.dtype).reshape(gvals_ref.shape)
+    gpre = ((x * gu + ah_s[...] * (1.0 / LOG2E)) * slope_ref[...]).astype(BF16)
+    gvals_ref[...] = (gy * skip_ref[...] + dt * gu).astype(gvals_ref.dtype)
     gbias_ref[...] += jnp.sum(gpre.astype(F32), axis=0, keepdims=True)
     gstepw_ref[...] += jnp.dot(selected[:rank].astype(BF16), gpre, preferred_element_type=F32)
     fold = lambda ref: nt_dot(tiles.astype(BF16), ref[...].astype(BF16))
-    gsel_ref[0, 0, 0:rank, :] = nt_dot(stepw_ref[...], gpre).astype(BF16)
-    gsel_ref[0, 0, rank:rank + n, :] = fold(db_s).astype(BF16)
-    gsel_ref[0, 0, rank + n:rank + 2 * n, :] = fold(dc_s).astype(BF16)
-
-    @pl.when((row == pl.num_programs(0) - 1) & (step == pl.num_programs(1) - 1))
-    def _():
-        gdecay_ref[...] = gd_s[...] * rate_s[...] * (1.0 / LOG2E)
-
-
-def scan_backward(sel, x, gact, gg, tail, starts, dt, slope, stepw, decay, skip, n):
-    chunks, rows, length, width = x.shape
-    rank = stepw.shape[0]
-    wide = BLOCK * n
-    at = lambda r, c: (chunks - 1 - c, r, 0, 0)
-    tok = lambda feat: pl.BlockSpec((1, 1, length, feat), at)
-    whole = lambda shape: pl.BlockSpec(shape, lambda r, c: (0,) * len(shape))
-    sds = jax.ShapeDtypeStruct
-    return pl.pallas_call(
-        functools.partial(scan_backward_kernel, rank=rank, n=n),
-        grid=(rows, chunks),
-        in_specs=[pl.BlockSpec((1, 1) + sel.shape[2:], at), tok(width), tok(width), tok(width), tok(width), pl.BlockSpec((1, 1, n, width), at), tok(width), tok(width),
-                  whole(stepw.shape), whole(decay.shape), whole(skip.shape)],
-        out_specs=[tok(width), tok(width), tok(width), pl.BlockSpec((1, 1) + sel.shape[2:], at), whole((rank, width)), whole((1, width)), whole((n, width)), whole((1, width))],
-        out_shape=[
-            sds(x.shape, BF16), sds(x.shape, F32), sds(x.shape, BF16), sds(sel.shape, BF16),
-            sds((rank, width), F32), sds((1, width), F32), sds((n, width), F32), sds((1, width), F32),
-        ],
-        scratch_shapes=[
-            pltpu.VMEM((length, width), F32), pltpu.VMEM((length, width), F32), pltpu.VMEM((length, width), F32),
-            pltpu.VMEM((length, width), F32), pltpu.VMEM((length, width), F32),
-            pltpu.VMEM((length, wide), BF16), pltpu.VMEM((2 * n, length), F32),
-            pltpu.VMEM((length * n, width), BF16), pltpu.VMEM((wide, width), BF16), pltpu.VMEM((wide, width), BF16),
-            pltpu.VMEM((wide, width), BF16), pltpu.VMEM((wide, width), BF16),
-            pltpu.VMEM((length, wide), F32), pltpu.VMEM((length, wide), F32),
-            pltpu.VMEM((n, width), F32), pltpu.VMEM((n, width), F32), pltpu.VMEM((n, width), F32),
-            pltpu.VMEM((length * n, width), F32), pltpu.VMEM((length * n, width), F32),
-        ],
-        name="scan_backward",
-    )(sel, x, gact, gg, tail, starts, dt, slope, stepw, decay, skip)
+    gsel_ref[0:rank, :] = nt_dot(stepw_ref[...], gpre).astype(BF16)
+    gsel_ref[rank:rank + n, :] = fold(db_s).astype(BF16)
+    gsel_ref[rank + n:rank + 2 * n, :] = fold(dc_s).astype(BF16)
+
+
 def conv_step(ci, fresh, taps_ref, bias_ref, selw_ref, ext_s):
     length = ci.shape[0]
     tap_count = taps_ref.shape[0]
@@ -265,34 +213,21 @@
     return x, nt_dot(selw_ref[...], x).astype(BF16)
 
 
-def conv_backward_kernel(ci_ref, prev_ref, gvals_ref, gsel_ref, taps_ref, bias_ref, selw_ref,
-                         gci_ref, gtaps_ref, gbias_ref, gselw_ref, ext_s, gext_s):
-    row, step = pl.program_id(0), pl.program_id(1)
-    length = ci_ref.shape[-2]
+def conv_back_step(ci_ref, prev_ref, first, fresh, gvals_ref, gsel_ref, taps_ref, bias_ref, selw_ref,
+                   gci_ref, gtaps_ref, gbias_ref, gselw_ref, ext_s, gext_s):
+    length = ci_ref.shape[0]
     tap_count = taps_ref.shape[0]
-    flat = lambda ref: ref[...].reshape(ref.shape[-2:])
-
-    @pl.when(step == 0)
-    def _():
-        gext_s[length:, :] = jnp.zeros((8, gext_s.shape[1]), F32)
-
-    @pl.when((step == 0) & (row == 0))
-    def _():
-        gtaps_ref[...] = jnp.zeros_like(gtaps_ref)
-        gbias_ref[...] = jnp.zeros_like(gbias_ref)
-        gselw_ref[...] = jnp.zeros_like(gselw_ref)
-
-    first = step == pl.num_programs(1) - 1
-    ext_s[8:, :] = flat(ci_ref).astype(F32)
-    before = flat(prev_ref)[length - 16:, :].astype(F32)[8:, :]
+    gext_s[length:, :] = jnp.where(fresh, 0.0, gext_s[length:, :])
+    ext_s[8:, :] = ci_ref[...].astype(F32)
+    before = prev_ref[...][length - 16:, :].astype(F32)[8:, :]
     ext_s[0:8, :] = jnp.where(first, 0.0, before)
     total = bias_ref[...].astype(F32)
     for k in range(tap_count):
         total = total + taps_ref[k:k + 1, :].astype(F32) * ext_s[pl.ds(8 - tap_count + 1 + k, length), :]
     sg = sigmoid(total)
     x = (total * sg).astype(BF16)
-    gsel = flat(gsel_ref)
-    gvals = flat(gvals_ref) + jnp.dot(gsel.astype(F32).T.astype(BF16), selw_ref[...], preferred_element_type=F32)
+    gsel = gsel_ref[...]
+    gvals = gvals_ref[...] + jnp.dot(gsel.astype(F32).T.astype(BF16), selw_ref[...], preferred_element_type=F32)
     gconv = gvals * sg * (1.0 + total * (1.0 - sg))
     gbias_ref[...] += jnp.sum(gconv, axis=0, keepdims=True)
     for k in range(tap_count):
@@ -302,26 +237,10 @@
     gci = jnp.zeros_like(gconv)
     for k in range(tap_count):
         gci = gci + taps_ref[k:k + 1, :].astype(F32) * gext_s[pl.ds(tap_count - 1 - k, length), :]
-    gci_ref[...] = gci.astype(BF16).reshape(gci_ref.shape)
+    gci_ref[...] = gci.astype(BF16)
     gext_s[length:, :] = gconv[0:8, :]
 
 
-def conv_backward(ci, gvals, gsel, taps, bias, selw):
-    chunks, rows, length, width = ci.shape
-    at = lambda r, c: (chunks - 1 - c, r, 0, 0)
-    before = lambda r, c: (jnp.maximum(chunks - 2 - c, 0), r, 0, 0)
-    tok = lambda feat, where: pl.BlockSpec((1, 1, length, feat), where)
-    whole = lambda shape: pl.BlockSpec(shape, lambda r, c: (0,) * len(shape))
-    sds = jax.ShapeDtypeStruct
-    return pl.pallas_call(
-        conv_backward_kernel,
-        grid=(rows, chunks),
-        in_specs=[tok(width, at), tok(width, before), tok(width, at), pl.BlockSpec((1, 1) + gsel.shape[2:], at), whole(taps.shape), whole(bias.shape), whole(selw.shape)],
-        out_specs=[tok(width, at), whole(taps.shape), whole(bias.shape), whole(selw.shape)],
-        out_shape=[sds(ci.shape, BF16), sds(taps.shape, F32), sds(bias.shape, F32), sds(selw.shape, F32)],
-        scratch_shapes=[pltpu.VMEM((length + 8, width), F32), pltpu.VMEM((length + 8, width), F32)],
-        name="conv_backward",
-    )(ci, ci, gvals, gsel, taps, bias, selw)
 MESH = pl.DeviceIdType.MESH
 
 
@@ -354,7 +273,7 @@
 
 def gather_project_kernel(hid_ref, wq_ref, gain_ref, n_ref, ci_ref, gate_ref, w_ref, row_ref,
                           hid_v, gain_v, w_v, n_v, ci_v, gate_v,
-                          load_sem, out_sem, hrecv, hside, hup, hdown,
+                          load_sem, out_sem, hrecv, hside, hup, hdown, hlend,
                           w1send, w1recv, w2recv, w2send, w3send, gsend, grecv, *, chunks, copies, share, split):
     zs, ys = grid_of(chunks, copies)
     xs = copies // 2
@@ -365,6 +284,7 @@
     width = ci_v.shape[1]
     inner = chunks * width
     half = tokens // 2
+    even = ys == 2 and zs % 2 == 0
     piece = share // (copies if split else 1)
     spot = mine if split else 0
     load = pltpu.make_async_copy(hid_ref, hid_v.at[me], load_sem)
@@ -434,21 +354,36 @@
             side(z, j, h).start()
     every_other(send_first)
 
+    partner = z + 1 - 2 * (z % 2)
+
+    def sides(o, h, act):
+        if even and h == 1:
+            when(o != partner, lambda: act(side(o, 1, h)))
+        else:
+            for j in range(1, ys):
+                act(side(o, j, h))
+
+    def lend():
+        return remote(block(z, 1 - y, 1), block(z, 1 - y, 1), hlend, hrecv.at[z * ys + 1 - y, 1], {"seq": partner * ys + y})
+
+    def lend_on():
+        if even:
+            landed(z, 1 - y, 1).wait_recv()
+            lend().start()
+
     def relay(k):
         for h in range(2):
             @pl.when(z - k >= 0)
             def _():
                 landed(z - k, y, h).wait_recv()
                 when(z + 1 < zs, lambda: up(z - k, h).start())
-                for j in range(1, ys):
-                    side(z - k, j, h).start()
+                sides(z - k, h, lambda one: one.start())
 
             @pl.when(z + k < zs)
             def _():
                 landed(z + k, y, h).wait_recv()
                 when(z > 0, lambda: down(z + k, h).start())
-                for j in range(1, ys):
-                    side(z + k, j, h).start()
+                sides(z + k, h, lambda one: one.start())
 
     def shared(s, d, sems, k, device):
         return remote(w_v.at[w_rows(s, d)], w_v.at[w_rows(s, d)], sems.at[s, k], w2recv.at[s, d], device)
@@ -490,6 +425,7 @@
 
     if zs > 2:
         relay(2)
+    lend_on()
     if split:
         lax.fori_loop(0, chunks, take_second, 0)
     if split:
@@ -547,8 +483,11 @@
 
             @pl.when(ok & jnp.logical_not(own))
             def _():
-                for h in range(2):
-                    landed(o, yy, h).wait_recv()
+                landed(o, yy, 0).wait_recv()
+                if even:
+                    when(o != z, lambda: landed(o, yy, 1).wait_recv())
+                else:
+                    landed(o, yy, 1).wait_recv()
 
             @pl.when(ok)
             def _():
@@ -589,19 +528,19 @@
             @pl.when(z - k >= 0)
             def _():
                 when(z + 1 < zs, lambda: up(z - k, h).wait_send())
-                for j in range(1, ys):
-                    side(z - k, j, h).wait_send()
+                sides(z - k, h, lambda one: one.wait_send())
 
             @pl.when((z + k < zs) & (k > 0))
             def _():
                 when(z > 0, lambda: down(z + k, h).wait_send())
-                for j in range(1, ys):
-                    side(z + k, j, h).wait_send()
+                sides(z + k, h, lambda one: one.wait_send())
         return 0
 
     lax.fori_loop(0, zs, drain, 0)
     for h in range(2):
         when(z > 0, lambda: down(z, h).wait_send())
+    if even:
+        lend().wait_send()
 
 
 def gather_project(hidden, wq, gain, chunks, copies, share, split):
@@ -620,7 +559,7 @@
         scratch_shapes=[
             pltpu.VMEM((chunks, tokens, model), BF16), pltpu.VMEM((chunks, 1, share), F32), pltpu.VMEM((model, 2 * width), BF16),
             pltpu.VMEM((tokens, model), BF16), pltpu.VMEM((tokens, width), BF16), pltpu.VMEM((tokens, width), F32),
-            dma(()), dma((3,)), dma((chunks, 2)), dma((zs, max(1, ys - 1), 2)), dma((zs, 2)), dma((zs, 2)),
+            dma(()), dma((3,)), dma((chunks, 2)), dma((zs, max(1, ys - 1), 2)), dma((zs, 2)), dma((zs, 2)), dma(()),
             dma((chunks, 2)), dma((chunks, 2)), dma((chunks, copies)), dma((chunks, max(1, copies // 2))), dma((chunks, max(1, copies // 2))),
             dma((chunks,)), dma((chunks,)),
         ],
@@ -629,134 +568,11 @@
     )(hidden, wq, gain)
 
 
-def total_kernel(*refs, chunks, copies, extra):
-    part_ref, out_ref = refs[0], refs[1 + extra]
-    early, early_out = refs[1:1 + extra], refs[2 + extra:2 + 2 * extra]
-    refs = refs[2 + 2 * extra:]
-    recv_v, send1, recv1, send2, recv2 = refs[:5]
-    bufs, sems = refs[5:5 + 3 * extra], refs[5 + 3 * extra:]
-    me, mine = lax.axis_index("seq"), lax.axis_index("dp")
-    x, c = mine // 2, mine % 2
-    xs = copies // 2
-    meet(chunks, copies if extra else 1)
-
-    def first(s):
-        return remote(part_ref.at[s], recv_v.at[me], send1.at[s], recv1.at[me], {"seq": s})
-
-    def landed_first(s):
-        return remote(part_ref.at[s], recv_v.at[s], send1.at[s], recv1.at[s], {"seq": s})
-
-    def second(s):
-        return remote(out_ref.at[me], out_ref.at[me], send2.at[s], recv2.at[me], {"seq": s})
-
-    def landed_second(s):
-        return remote(out_ref.at[s], out_ref.at[s], send2.at[s], recv2.at[s], {"seq": s})
-
-    def every_other(fn):
-        def one(k, _):
-            fn(lax.rem(me + k, chunks))
-            return 0
-        lax.fori_loop(1, chunks, one, 0)
-
-    def part_of(e, core):
-        rows = early[e].shape[0] // 2
-        return pl.ds(pl.multiple_of(core * rows, rows), rows)
-
-    def to_core(e):
-        return remote(early[e].at[part_of(e, 1 - c)], bufs[3 * e], sems[0].at[e], sems[1].at[e], {"dp": x * 2 + 1 - c})
-
-    def across(e, j):
-        return remote(bufs[3 * e + 1], bufs[3 * e + 2].at[x], sems[2].at[e, j], sems[3].at[e, x], {"dp": lax.rem(x + j, xs) * 2 + c})
-
-    def from_across(e, j):
-        q = lax.rem(x + j, xs)
-        return remote(bufs[3 * e + 2].at[q], bufs[3 * e + 2].at[q], sems[2].at[e, j], sems[3].at[e, q], {"dp": q * 2 + c})
-
-    def back(e):
-        return remote(early_out[e].at[part_of(e, c)], early_out[e].at[part_of(e, c)], sems[4].at[e], sems[5].at[e], {"dp": x * 2 + 1 - c})
-
-    def from_back(e):
-        return remote(early_out[e].at[part_of(e, 1 - c)], early_out[e].at[part_of(e, 1 - c)], sems[4].at[e], sems[5].at[e], {"dp": x * 2 + 1 - c})
-
-    def by_rows(e, fn):
-        count = early[e].shape[0] // 2
-        step = 16
-
-        def one(i, _):
-            fn(pl.multiple_of(i * step, step), step, pl.multiple_of(c * count, count) + i * step)
-            return 0
-        lax.fori_loop(0, count // step, one, 0)
-
-    every_other(lambda s: first(s).start())
-    for e in range(extra):
-        to_core(e).start()
-    recv_v[me] = part_ref[me]
-    for e in range(extra):
-        to_core(e).wait_recv()
-
-        def fold(at, step, full):
-            mine_rows = early[e][pl.ds(pl.multiple_of(full, step), step), :].astype(F32)
-            bufs[3 * e + 1][pl.ds(at, step), :] = (mine_rows + bufs[3 * e][pl.ds(at, step), :].astype(F32)).astype(BF16)
-
-        by_rows(e, fold)
-        for j in range(1, xs):
-            across(e, j).start()
-    every_other(lambda s: landed_first(s).wait_recv())
-    total = recv_v[0].astype(F32)
-    for s in range(1, chunks):
-        total = total + recv_v[s].astype(F32)
-    out_ref[me] = total.astype(BF16)
-    every_other(lambda s: second(s).start())
-    for e in range(extra):
-        for j in range(1, xs):
-            from_across(e, j).wait_recv()
-
-        def finish(at, step, full):
-            total = bufs[3 * e + 1][pl.ds(at, step), :].astype(F32)
-            for j in range(1, xs):
-                total = total + bufs[3 * e + 2][lax.rem(x + j, xs), pl.ds(at, step), :].astype(F32)
-            early_out[e][pl.ds(pl.multiple_of(full, step), step), :] = total.astype(BF16)
-
-        by_rows(e, finish)
-        back(e).start()
-    every_other(lambda s: landed_second(s).wait_recv())
-    every_other(lambda s: first(s).wait_send())
-    every_other(lambda s: second(s).wait_send())
-    for e in range(extra):
-        from_back(e).wait_recv()
-        to_core(e).wait_send()
-        for j in range(1, xs):
-            across(e, j).wait_send()
-        back(e).wait_send()
-
-
-def total_over_seq(part, chunks, copies, key, early=()):
-    vmem = pl.BlockSpec(memory_space=pltpu.VMEM)
-    dma = pltpu.SemaphoreType.DMA
-    extra = len(early)
-    xs = max(1, copies // 2)
-    scratch = [pltpu.VMEM(part.shape, BF16), dma((chunks,)), dma((chunks,)), dma((chunks,)), dma((chunks,))]
-    for a in early:
-        rows = a.shape[0] // 2
-        scratch += [pltpu.VMEM((rows, a.shape[1]), BF16), pltpu.VMEM((rows, a.shape[1]), BF16), pltpu.VMEM((xs, rows, a.shape[1]), BF16)]
-    if extra:
-        scratch += [dma((extra,)), dma((extra,)), dma((extra, xs)), dma((extra, xs)), dma((extra,)), dma((extra,))]
-    sds = jax.ShapeDtypeStruct
-    got = pl.pallas_call(
-        functools.partial(total_kernel, chunks=chunks, copies=copies, extra=extra),
-        in_specs=[vmem] * (1 + extra),
-        out_specs=[vmem] * (1 + extra),
-        out_shape=[sds(part.shape, BF16)] + [sds(a.shape, BF16) for a in early],
-        scratch_shapes=scratch,
-        compiler_params=pltpu.CompilerParams(collective_id=key, has_side_effects=True, vmem_limit_bytes=60 * 1024 * 1024),
-        name=f"total_over_seq_{key}",
-    )(part, *early)
-    return got if extra else got[0]
 def forward_kernel(ci_ref, gate_ref, gm_ref, taps_ref, cbias_ref, selw_ref, stepw_ref, sbias_ref, decay_ref, skip_ref,
                    gmall_ref, sel_ref, x_ref, gated_ref, gact_ref, tail_ref, dt_ref, slope_ref, start_ref,
                    gate_v, part_v, recv_v, x_v, gated_v, gact_v, tail_v, dt_v, slope_v, start_v,
                    ext_s, u_s, y_s, coef_s, bt_s, hist_a, hist_b, state_s, rate_s,
-                   load_sem, own_sem, out_sem, grecv, gside, gup, gdown, send1, recv1, send2, recv2, *, chunks, copies, n):
+                   load_sem, own_sem, out_sem, grecv, gside, gup, gdown, glend, send1, recv1, send2, recv2, *, chunks, copies, n):
     zs, ys = grid_of(chunks, copies)
     me = lax.axis_index("seq")
     z, y = me // ys, me % ys
@@ -764,6 +580,7 @@
     rows, length, width = ci_ref.shape[1:]
     rank = stepw_ref.shape[0]
     half = tokens // 2
+    even = ys == 2 and zs % 2 == 0
     load = pltpu.make_async_copy(gate_ref, gate_v, load_sem)
     load.start()
     own = pltpu.make_async_copy(gm_ref, gmall_ref.at[me], own_sem)
@@ -797,21 +614,36 @@
         for j in range(1, ys):
             side(z, j, h, None).start()
 
+    partner = z + 1 - 2 * (z % 2)
+
+    def sides(o, h, act):
+        if even and h == 1:
+            when(o != partner, lambda: act(side(o, 1, h)))
+        else:
+            for j in range(1, ys):
+                act(side(o, j, h))
+
+    def lend():
+        return remote(block(z, 1 - y, 1), block(z, 1 - y, 1), glend, grecv.at[z * ys + 1 - y, 1], {"seq": partner * ys + y})
+
+    def lend_on():
+        if even:
+            landed(z, 1 - y, 1).wait_recv()
+            lend().start()
+
     def relay(k):
         for h in range(2):
             @pl.when(z - k >= 0)
             def _():
                 landed(z - k, y, h).wait_recv()
                 when(z + 1 < zs, lambda: up(z - k, h).start())
-                for j in range(1, ys):
-                    side(z - k, j, h).start()
+                sides(z - k, h, lambda one: one.start())
 
             @pl.when(z + k < zs)
             def _():
                 landed(z + k, y, h).wait_recv()
                 when(z > 0, lambda: down(z + k, h).start())
-                for j in range(1, ys):
-                    side(z + k, j, h).start()
+                sides(z + k, h, lambda one: one.start())
 
     rate_s[...] = -jnp.exp(decay_ref[...].astype(F32)) * LOG2E
 
@@ -854,6 +686,8 @@
     every_other(lambda s: second(s).start())
     if zs > 1:
         relay(1)
+    if zs <= 2:
+        lend_on()
     every_other(lambda s: landed_second(s).wait_recv())
     load.wait()
     pairs = ((gated_v, gated_ref), (gact_v, gact_ref), (tail_v, tail_ref), (dt_v, dt_ref), (slope_v, slope_ref), (start_v, start_ref))
@@ -877,11 +711,16 @@
         lax.fori_loop(count * k // parts, count * (k + 1) // parts, scan, 0)
         if 2 + k < zs:
             relay(2 + k)
+        if k == 0 and zs > 2:
+            lend_on()
 
     def others(o, _):
         for j in range(1, ys):
-            for h in range(2):
-                landed(o, lax.rem(y + j, ys), h).wait_recv()
+            landed(o, lax.rem(y + j, ys), 0).wait_recv()
+            if even:
+                when(o != z, lambda: landed(o, 1 - y, 1).wait_recv())
+            else:
+                landed(o, lax.rem(y + j, ys), 1).wait_recv()
         return 0
 
     lax.fori_loop(0, zs, others, 0)
@@ -902,19 +741,19 @@
             @pl.when(z - k >= 0)
             def _():
                 when(z + 1 < zs, lambda: up(z - k, h).wait_send())
-                for j in range(1, ys):
-                    side(z - k, j, h).wait_send()
+                sides(z - k, h, lambda one: one.wait_send())
 
             @pl.when((z + k < zs) & (k > 0))
             def _():
                 when(z > 0, lambda: down(z + k, h).wait_send())
-                for j in range(1, ys):
-                    side(z + k, j, h).wait_send()
+                sides(z + k, h, lambda one: one.wait_send())
         return 0
 
     lax.fori_loop(0, zs, drain, 0)
     for h in range(2):
         when(z > 0, lambda: down(z, h).wait_send())
+    if even:
+        lend().wait_send()
 
 
 def forward(ci, gate, gm, taps, cbias, selw, stepw, sbias, decay, skip, copies, n):
@@ -941,7 +780,7 @@
             pltpu.VMEM((length + 8, width), F32), pltpu.VMEM((length, width), F32), pltpu.VMEM((length, width), F32),
             pltpu.VMEM((length, wide), BF16), pltpu.VMEM((2 * n, length), F32), pltpu.VMEM((wide, width), BF16), pltpu.VMEM((wide, width), BF16),
             pltpu.VMEM((n, width), F32), pltpu.VMEM((n, width), F32),
-            dma(()), dma(()), dma((7, rows * chunks)), dma((chunks, 2)), dma((zs, max(1, ys - 1), 2)), dma((zs, 2)), dma((zs, 2)),
+            dma(()), dma(()), dma((7, rows * chunks)), dma((chunks, 2)), dma((zs, max(1, ys - 1), 2)), dma((zs, 2)), dma((zs, 2)), dma(()),
             dma((chunks,)), dma((chunks,)), dma((chunks,)), dma((chunks,)),
         ],
         compiler_params=pltpu.CompilerParams(collective_id=1, has_side_effects=True, vmem_limit_bytes=60 * 1024 * 1024),
@@ -956,13 +795,13 @@
 def scatter_kernel(*refs, chunks, copies, split):
     if split:
         (gc_ref, gg_ref, w_ref, late_ref, ginc_ref, ging_ref, red_ref, sum_ref, all_ref,
-         ysend_v, yrecv_v, own_v, zrecv_v, late_v, w_v, g1_v, mine_v, g2_v, t_v, fin_v, load_sem,
-         ysend, yrecv, zup, zdown, zrecv, lsend, lrecv,
+         ysend_v, yrecv_v, own_v, zrecv_v, lend_v, late_v, w_v, g1_v, mine_v, g2_v, t_v, fin_v, load_sem,
+         ysend, yrecv, zup, zdown, zrecv, lend_sem, lsend, lrecv,
          g1send, g1recv, g2send, g2recv, g3send, g3recv, g4send, g4recv) = refs
     else:
         (gc_ref, gg_ref, w_ref, late_ref, red_ref, sum_ref,
-         ysend_v, yrecv_v, own_v, zrecv_v, late_v, w_v, load_sem,
-         ysend, yrecv, zup, zdown, zrecv, lsend, lrecv) = refs
+         ysend_v, yrecv_v, own_v, zrecv_v, lend_v, late_v, w_v, load_sem,
+         ysend, yrecv, zup, zdown, zrecv, lend_sem, lsend, lrecv) = refs
     zs, ys = grid_of(chunks, copies)
     xs = copies // 2
     me, mine = lax.axis_index("seq"), lax.axis_index("dp")
@@ -973,6 +812,7 @@
     half = tokens // 2
     tile = min(256, model)
     tables = order_of(zs)
+    partner = z + 1 - 2 * (z % 2)
 
     def dest(i):
         got = 0
@@ -1013,7 +853,6 @@
         for q in range(xs):
             for part in range(2):
                 g1(q, part).start()
-    every_copy(lambda d: late_to(d).start())
     w_in.wait()
 
     def partial(s, out, at):
@@ -1030,8 +869,36 @@
         return remote(ysend_v.at[k % ysend_v.shape[0], rows], yrecv_v.at[k, rows], ysend.at[k, h], yrecv.at[k, h], {"seq": z * ys + lax.rem(y + j, ys)})
 
     slots = ysend_v.shape[0]
+    even = ys == 2 and zs % 2 == 0 and slots == zs
+
+    def lend(i):
+        return remote(ysend_v.at[i, pl.ds(half, half)], lend_v, lend_sem.at[0], lend_sem.at[1], {"seq": partner * ys + y})
+
+    def send_side(i, j, h):
+        if not even or h == 0:
+            to_side(i, j, h).start()
+            return
+
+        @pl.when(dest(i) != partner)
+        def _():
+            if i == zs - 1:
+                lend(i).wait_recv()
+
+                def one(r, _):
+                    sl = pl.ds(pl.multiple_of(half + r * 32, 32), 32)
+                    ysend_v[i, sl, :] = (ysend_v[i, sl, :].astype(F32) + lend_v[pl.ds(pl.multiple_of(r * 32, 32), 32), :].astype(F32)).astype(BF16)
+                    return 0
+                lax.fori_loop(0, half // 32, one, 0)
+            to_side(i, j, h).start()
+
+    def if_sent(i, h, fn):
+        if even and h == 1:
+            pl.when(dest(i) != partner)(fn)
+        else:
+            fn()
+
     ahead = 2 if slots == zs * (ys - 1) else zs
-    for i in range(zs):
+    def outgoing(i):
         for j in range(1, ys):
             k = i * (ys - 1) + j - 1
             if k >= slots:
@@ -1040,41 +907,38 @@
             partial(dest(i) * ys + lax.rem(y + j, ys), ysend_v, k % slots)
             if i < ahead:
                 for h in range(2):
-                    to_side(i, j, h).start()
-
-    def add_into(total, terms):
-        def one(r, _):
-            sl = pl.ds(pl.multiple_of(r * 32, 32), 32)
-            total(sl, terms)
-            return 0
-        return one
+                    send_side(i, j, h)
+            if even:
+                pl.when(dest(i) == partner)(lambda: lend(i).start())
 
     if split:
-        def g2(q):
-            return remote(mine_v.at[q], g2_v.at[x], g2send.at[q], g2recv.at[x], {"dp": q * 2 + c})
-
-        def g2_from(q):
-            return remote(g2_v.at[q], g2_v.at[q], g2send.at[q], g2recv.at[q], {"dp": q * 2 + c})
-
-        for q in range(xs):
-            for part in range(2):
+        def g2(q, part):
+            return remote(mine_v.at[q, :, :, cols[part]], g2_v.at[x, :, :, cols[part]], g2send.at[q, part], g2recv.at[x, part], {"dp": q * 2 + c})
+
+        def g2_from(q, part):
+            return remote(g2_v.at[q, :, :, cols[part]], g2_v.at[q, :, :, cols[part]], g2send.at[q, part], g2recv.at[q, part], {"dp": q * 2 + c})
+
+        for i in range(min(2, zs)):
+            outgoing(i)
+        for part in range(2):
+            for q in range(xs):
                 loads[q][part].wait()
                 g1(q, part).wait_recv()
 
-            def fold(s, _):
-                mine_v[q, s] = (mine_v[q, s].astype(F32) + g1_v[q, s].astype(F32)).astype(BF16)
-                return 0
-            lax.fori_loop(0, chunks, fold, 0)
-
-            @pl.when(q != x)
-            def _():
-                g2(q).start()
+                def fold(s, _):
+                    mine_v[q, s, :, cols[part]] = (mine_v[q, s, :, cols[part]].astype(F32) + g1_v[q, s, :, cols[part]].astype(F32)).astype(BF16)
+                    return 0
+                lax.fori_loop(0, chunks, fold, 0)
+
+                @pl.when(q != x)
+                def _():
+                    g2(q, part).start()
 
         def columns(part, s):
             return pl.ds(pl.multiple_of(part * inner + s * width, width), width)
 
         def g3(s, part):
-            return remote(t_v.at[s, :, pl.ds(part * width, width)], fin_v.at[:, columns(part, me)], g3send.at[s, part], g3recv.at[me, part], {"seq": s})
+            return remote(t_v.at[s, :, cols[part]], fin_v.at[:, columns(part, me)], g3send.at[s, part], g3recv.at[me, part], {"seq": s})
 
         def g3_from(s, part):
             return remote(fin_v.at[:, columns(part, s)], fin_v.at[:, columns(part, s)], g3send.at[s, part], g3recv.at[s, part], {"seq": s})
@@ -1085,43 +949,48 @@
                 return 0
             lax.fori_loop(1, chunks, one, 0)
 
-        def third():
+        def third(part):
             for q in range(xs):
                 @pl.when(q != x)
                 def _():
-                    g2_from(q).wait_recv()
+                    g2_from(q, part).wait_recv()
 
             def fold(s, _):
-                total = mine_v[x, s].astype(F32)
+                total = mine_v[x, s, :, cols[part]].astype(F32)
                 for q in range(1, xs):
-                    total = total + g2_v[lax.rem(x + q, xs), s].astype(F32)
-                t_v[s] = total.astype(BF16)
+                    total = total + g2_v[lax.rem(x + q, xs), s, :, cols[part]].astype(F32)
+                t_v[s, :, cols[part]] = total.astype(BF16)
                 return 0
             lax.fori_loop(0, chunks, fold, 0)
-            for part in range(2):
-                every_other(lambda s: g3(s, part).start())
-                fin_v[:, columns(part, me)] = t_v[me, :, part * width:(part + 1) * width]
+            every_other(lambda s: g3(s, part).start())
+            fin_v[:, columns(part, me)] = t_v[me, :, cols[part]]
 
         def rows_of(d):
             return pl.ds(pl.multiple_of(d * piece, piece), piece)
 
-        def g4(d_src, k, d):
-            src = fin_v if d_src is None else all_ref.at[rows_of(d_src)]
+        sides_of = [pl.ds(part * inner, inner) for part in range(2)]
+
+        def g4(d_src, k, d, part):
+            src = fin_v.at[:, sides_of[part]] if d_src is None else all_ref.at[rows_of(d_src), sides_of[part]]
             row = mine if d_src is None else d_src
-            return remote(src, all_ref.at[rows_of(row)], g4send.at[k], g4recv.at[row], {"dp": d})
-
-        def g4_from(d):
-            return remote(all_ref.at[rows_of(d)], all_ref.at[rows_of(d)], g4send.at[0], g4recv.at[d], {"dp": d})
-
-        keep = pltpu.make_async_copy(fin_v, all_ref.at[rows_of(mine)], load_sem.at[0])
-
-        def fourth():
-            for part in range(2):
-                every_other(lambda s: g3_from(s, part).wait_recv())
+            return remote(src, all_ref.at[rows_of(row), sides_of[part]], g4send.at[k, part], g4recv.at[row, part], {"dp": d})
+
+        def g4_from(d, part):
+            to = all_ref.at[rows_of(d), sides_of[part]]
+            return remote(to, to, g4send.at[0, part], g4recv.at[d, part], {"dp": d})
+
+        keep = [pltpu.make_async_copy(fin_v.at[:, sides_of[part]], all_ref.at[rows_of(mine), sides_of[part]], load_sem.at[part]) for part in range(2)]
+
+        def fourth(part):
+            every_other(lambda s: g3_from(s, part).wait_recv())
             for j in range(1, xs):
-                g4(None, j, lax.rem(x + j, xs) * 2 + c).start()
-            g4(None, 0, x * 2 + 1 - c).start()
-            keep.start()
+                g4(None, j, lax.rem(x + j, xs) * 2 + c, part).start()
+            g4(None, 0, x * 2 + 1 - c, part).start()
+            keep[part].start()
+
+    for i in range(min(2, zs) if split else 0, zs):
+        outgoing(i)
+    every_copy(lambda d: late_to(d).start())
 
     def arrived(i, j, h):
         rows = pl.ds(h * half, half)
@@ -1153,7 +1022,7 @@
         partial(t * ys + y, own_v, t)
         for h in range(2):
             for j in range(1, ys):
-                arrived(i, ys - j, h).wait_recv()
+                if_sent(i, h, lambda: arrived(i, ys - j, h).wait_recv())
 
             def side_sum(sl):
                 total = yrecv_v[i * (ys - 1), sl, :].astype(F32)
@@ -1161,12 +1030,8 @@
                     total = total + yrecv_v[i * (ys - 1) + j - 1, sl, :].astype(F32)
                 return total
 
-            if h == 0 and i + ahead < zs:
-                for j in range(1, ys):
-                    for g in range(2):
-                        to_side(i + ahead, j, g).start()
             if ys > 1:
-                accumulate(t, h, side_sum)
+                if_sent(i, h, lambda: accumulate(t, h, side_sum))
 
             @pl.when(((t > z) & (z > 0)) | ((t == z) & (z > 0)))
             def _():
@@ -1191,30 +1056,40 @@
             def _():
                 sink(t, h).start()
         if split and i == 0:
-            third()
-        if split and i == max(0, zs - 2):
-            fourth()
+            third(0)
+            third(1)
+        if split and i == min(1, zs - 1):
+            fourth(0)
+            fourth(1)
+        if i + ahead < zs:
+            for j in range(1, ys):
+                for h in range(2):
+                    send_side(i + ahead, j, h)
 
     red_ref[...] = own_v[z]
     every_copy(lambda d: late_from(d).wait_recv())
-    total = late_ref[...]
+    total = late_ref[...].astype(F32)
     for k in range(1, copies):
-        total = total + late_v[lax.rem(mine + k, copies)]
+        total = total + late_v[lax.rem(mine + k, copies)].astype(F32)
     sum_ref[...] = total
     if split:
-        for j in range(1, xs):
-            d = lax.rem(x + j, xs) * 2 + c
-            g4_from(d).wait_recv()
-            g4(d, xs - 1 + j, x * 2 + 1 - c).start()
-        keep.wait()
-        for j in range(xs):
-            g4_from(lax.rem(x + j, xs) * 2 + 1 - c).wait_recv()
+        for part in range(2):
+            for j in range(1, xs):
+                d = lax.rem(x + j, xs) * 2 + c
+                g4_from(d, part).wait_recv()
+                g4(d, xs - 1 + j, x * 2 + 1 - c, part).start()
+        for part in range(2):
+            keep[part].wait()
+            for j in range(xs):
+                g4_from(lax.rem(x + j, xs) * 2 + 1 - c, part).wait_recv()
 
     every_copy(lambda d: late_to(d).wait_send())
     count = zs * (ys - 1)
     for k in range(max(0, count - slots), count):
         for h in range(2):
-            to_side(k // (ys - 1), k % (ys - 1) + 1, h).wait_send()
+            if_sent(k // (ys - 1), h, lambda: to_side(k // (ys - 1), k % (ys - 1) + 1, h).wait_send())
+    if even:
+        lend(0).wait_send()
     for i in range(zs):
         t = dest(i)
         for h in range(2):
@@ -1226,19 +1101,18 @@
             def _():
                 sink(t, h).wait_send()
     if split:
-        for q in range(xs):
-            for part in range(2):
+        for part in range(2):
+            for q in range(xs):
                 g1(q, part).wait_send()
 
-            @pl.when(q != x)
-            def _():
-                g2(q).wait_send()
-        for part in range(2):
+                @pl.when(q != x)
+                def _():
+                    g2(q, part).wait_send()
             every_other(lambda s: g3(s, part).wait_send())
-        for j in range(xs):
-            g4(None, j, mine).wait_send()
-        for j in range(1, xs):
-            g4(lax.rem(x + j, xs) * 2 + c, xs - 1 + j, mine).wait_send()
+            for j in range(xs):
+                g4(None, j, mine, part).wait_send()
+            for j in range(1, xs):
+                g4(lax.rem(x + j, xs) * 2 + c, xs - 1 + j, mine, part).wait_send()
 
 
 def scatter_sums(gc, gg, w_all, late, ginc, ging, chunks, copies, split):
@@ -1257,9 +1131,9 @@
     out_specs = [vmem, vmem]
     out_shape = [sds((tokens, model), BF16), sds(late.shape, F32)]
     scratch = [pltpu.VMEM((slots, tokens, model), BF16), pltpu.VMEM((others, tokens, model), BF16),
-               pltpu.VMEM((zs, tokens, model), BF16), pltpu.VMEM((zs + 1, tokens, model), BF16),
-               pltpu.VMEM((copies,) + late.shape, F32), pltpu.VMEM(w_all.shape, BF16)]
-    sems = [dma((1 + 2 * xs,)), dma((others, 2)), dma((others, 2)), dma((zs, 2)), dma((zs, 2)), dma((zs + 1, 2)), dma((copies,)), dma((copies,))]
+               pltpu.VMEM((zs, tokens, model), BF16), pltpu.VMEM((zs + 1, tokens, model), BF16), pltpu.VMEM((tokens // 2, model), BF16),
+               pltpu.VMEM((copies,) + late.shape, BF16), pltpu.VMEM(w_all.shape, BF16)]
+    sems = [dma((1 + 2 * xs,)), dma((others, 2)), dma((others, 2)), dma((zs, 2)), dma((zs, 2)), dma((zs + 1, 2)), dma((2,)), dma((copies,)), dma((copies,))]
     if split:
         piece = ginc.shape[2]
         slab = (xs, chunks, piece, 2 * width)
@@ -1269,7 +1143,7 @@
         out_shape.append(sds((copies * piece, 2 * chunks * width), BF16))
         scratch += [pltpu.VMEM(slab, BF16), pltpu.VMEM(slab, BF16), pltpu.VMEM(slab, BF16), pltpu.VMEM(slab[1:], BF16),
                     pltpu.VMEM((piece, 2 * chunks * width), BF16)]
-        sems += [dma((xs, 2)), dma((xs, 2)), dma((xs,)), dma((xs,)), dma((chunks, 2)), dma((chunks, 2)), dma((2 * xs,)), dma((copies,))]
+        sems += [dma((xs, 2)), dma((xs, 2)), dma((xs, 2)), dma((xs, 2)), dma((chunks, 2)), dma((chunks, 2)), dma((2 * xs, 2)), dma((copies, 2))]
     return pl.pallas_call(
         functools.partial(scatter_kernel, chunks=chunks, copies=copies, split=split),
         in_specs=in_specs,
@@ -1279,6 +1153,375 @@
         compiler_params=pltpu.CompilerParams(collective_id=3, has_side_effects=True, vmem_limit_bytes=62 * 1024 * 1024),
         name="scatter_sums",
     )(*args)
+def backward_kernel(*refs, chunks, copies, n, inside, extra):
+    ins = 15 + (1 if inside else 0) + (1 if extra else 0)
+    (gg_ref, gact_ref, tail_ref, x_ref, dt_ref, slope_ref, start_ref, sel_ref, ci_ref, stepw_ref, decay_ref, skip_ref,
+     taps_ref, cbias_ref, selw_ref) = refs[:15]
+    mixed_ref = refs[15] if inside else None
+    gout_ref = refs[ins - 1] if extra else None
+    outs = 9 + (1 if inside else 0) + (1 if extra else 0)
+    (ggate_ref, gci_ref, gstepw_ref, gsbias_ref, gdecay_ref, gskip_ref, gtaps_ref, gcbias_ref, gselw_ref) = refs[ins:ins + 9]
+    red_ref = refs[ins + 9] if inside else None
+    gsum_ref = refs[ins + outs - 1] if extra else None
+    refs = refs[ins + outs:]
+    (gg_v, gact_v, tail_v, x_v, dt_v, slope_v, start_v, ggate_v, gci_v, gvals_v, part_v, recv_v, sel2_v,
+     u_s, gy_s, gu_s, ah_s, bcoef_s, bt_s, hist_s, adj_a, harm_a, adj_b, harm_b, db_s, dc_s, carry_s, gd_s, rate_s, factor_s, kept_s,
+     ext_s, gext_s, in_sem, ggate_sem, gci_sem, send1, recv1, send2, recv2) = refs[:40]
+    refs = refs[40:]
+    if inside:
+        own_v, yrecv_v, zrecv_v, own_sem, ysend, yrecv, zup, zdown, zrecv = refs[:9]
+        refs = refs[9:]
+    if extra:
+        core_v, half_v, far_v, esend, erecv, asend, arecv, bsend, brecv = refs
+    zs, ys = grid_of(chunks, copies)
+    xs = copies // 2
+    me, mine = lax.axis_index("seq"), lax.axis_index("dp")
+    z, y = me // ys, me % ys
+    xd, cd = mine // 2, mine % 2
+    rows = sel_ref.shape[1]
+    rank = stepw_ref.shape[0]
+    count = rows * chunks
+
+    def where_of(i):
+        return chunks - 1 - i % chunks, i // chunks
+
+    streams = ((gg_ref, gg_v), (gact_ref, gact_v), (tail_ref, tail_v), (x_ref, x_v), (dt_ref, dt_v), (slope_ref, slope_v), (start_ref, start_v))
+
+    def fetch(i):
+        c, r = where_of(i)
+        return [pltpu.make_async_copy(src.at[c, r], dst.at[i % 2], in_sem.at[k, i % 2]) for k, (src, dst) in enumerate(streams)]
+
+    for one in fetch(0):
+        one.start()
+    if inside:
+        tokens, model = red_ref.shape
+        half = tokens // 2
+        own_loads = [pltpu.make_async_copy(mixed_ref.at[t * ys + y], own_v.at[t], own_sem.at[t]) for t in range(zs)]
+        for one in own_loads:
+            one.start()
+    meet(chunks, copies if extra else 1)
+
+    if inside:
+        tables = order_of(zs)
+
+        def dest(i):
+            got = 0
+            for k in range(zs):
+                for q in range(zs):
+                    got = got + jnp.where((z == k) & (i == q), tables[k][q], 0)
+            return got
+
+        def part_rows(h):
+            return pl.ds(h * half, half)
+
+        def to_side(i, h):
+            return remote(mixed_ref.at[dest(i) * ys + 1 - y, part_rows(h)], yrecv_v.at[i, part_rows(h)], ysend.at[i, h], yrecv.at[i, h], {"seq": z * ys + 1 - y})
+
+        def arrived(i, h):
+            return remote(yrecv_v.at[i, part_rows(h)], yrecv_v.at[i, part_rows(h)], ysend.at[i, h], yrecv.at[i, h], {"seq": z * ys + 1 - y})
+
+        def climb(t, h):
+            return remote(own_v.at[t, part_rows(h)], zrecv_v.at[t, part_rows(h)], zup.at[t, h], zrecv.at[t, h], {"seq": (z + 1) * ys + y})
+
+        def sink(t, h):
+            slot = jnp.where(t == z - 1, zs, t)
+            return remote(own_v.at[t, part_rows(h)], zrecv_v.at[slot, part_rows(h)], zdown.at[t, h], zrecv.at[slot, h], {"seq": (z - 1) * ys + y})
+
+        def from_z(slot, h):
+            return remote(zrecv_v.at[slot, part_rows(h)], zrecv_v.at[slot, part_rows(h)], zup.at[0, h], zrecv.at[slot, h], {"seq": lax.rem(me + 1, chunks)})
+
+        def accumulate(t, h, buf, slot):
+            def one(r, _):
+                sl = pl.ds(pl.multiple_of(h * half + r * 32, 32), 32)
+                own_v[t, sl, :] = own_v[t, sl, :] + buf[slot, sl, :]
+                return 0
+            lax.fori_loop(0, half // 32, one, 0)
+
+        def settle(i):
+            t = dest(i)
+            for h in range(2):
+                arrived(i, h).wait_recv()
+                accumulate(t, h, yrecv_v, i)
+
+                @pl.when((t >= z) & (z > 0))
+                def _():
+                    from_z(t, h).wait_recv()
+                    accumulate(t, h, zrecv_v, t)
+
+                @pl.when((t < z) & (z + 1 < zs))
+                def _():
+                    from_z(t, h).wait_recv()
+                    accumulate(t, h, zrecv_v, t)
+
+                @pl.when((t == z) & (z + 1 < zs))
+                def _():
+                    from_z(zs, h).wait_recv()
+                    accumulate(t, h, zrecv_v, zs)
+
+                @pl.when(t > z)
+                def _():
+                    climb(t, h).start()
+
+                @pl.when(t < z)
+                def _():
+                    sink(t, h).start()
+
+            @pl.when(i + 2 < zs)
+            def _():
+                for h in range(2):
+                    to_side(i + 2, h).start()
+
+        for i in range(2):
+            for h in range(2):
+                to_side(i, h).start()
+        edge = (z == 0) | (z == zs - 1)
+
+    if extra:
+        grows = gout_ref.shape[0] // 2
+
+        def part_of(core):
+            return pl.ds(pl.multiple_of(core * grows, grows), grows)
+
+        to_core = remote(gout_ref.at[part_of(1 - cd)], core_v, esend, erecv, {"dp": xd * 2 + 1 - cd})
+
+        def across(j):
+            return remote(half_v, far_v.at[xd], asend.at[j], arecv.at[xd], {"dp": lax.rem(xd + j, xs) * 2 + cd})
+
+        def from_across(j):
+            q = lax.rem(xd + j, xs)
+            return remote(far_v.at[q], far_v.at[q], asend.at[j], arecv.at[q], {"dp": q * 2 + cd})
+
+        back_out = remote(gsum_ref.at[part_of(cd)], gsum_ref.at[part_of(cd)], bsend, brecv, {"dp": xd * 2 + 1 - cd})
+        back_in = remote(gsum_ref.at[part_of(1 - cd)], gsum_ref.at[part_of(1 - cd)], bsend, brecv, {"dp": xd * 2 + 1 - cd})
+        to_core.start()
+
+        def by_rows(fn):
+            def one(i, _):
+                fn(pl.ds(pl.multiple_of(i * 16, 16), 16), pl.ds(pl.multiple_of(cd * grows + i * 16, 16), 16))
+                return 0
+            lax.fori_loop(0, grows // 16, one, 0)
+
+        def chip_sum():
+            to_core.wait_recv()
+
+            def fold(at, full):
+                half_v[at, :] = (gout_ref[full, :].astype(F32) + core_v[at, :].astype(F32)).astype(BF16)
+            by_rows(fold)
+            for j in range(1, xs):
+                across(j).start()
+
+        def whole_sum():
+            for j in range(1, xs):
+                from_across(j).wait_recv()
+
+            def fold(at, full):
+                total = half_v[at, :].astype(F32)
+                for j in range(1, xs):
+                    total = total + far_v[lax.rem(xd + j, xs), at, :].astype(F32)
+                gsum_ref[full, :] = total.astype(BF16)
+            by_rows(fold)
+            back_out.start()
+
+    def first(s, r):
+        return remote(part_v.at[s, r], recv_v.at[me, r], send1.at[s, r], recv1.at[me, r], {"seq": s})
+
+    def landed_first(s, r):
+        return remote(part_v.at[s, r], recv_v.at[s, r], send1.at[s, r], recv1.at[s, r], {"seq": s})
+
+    def second(s, r):
+        return remote(sel2_v.at[me, r], sel2_v.at[me, r], send2.at[s, r], recv2.at[me, r], {"seq": s})
+
+    def landed_second(s, r):
+        return remote(sel2_v.at[s, r], sel2_v.at[s, r], send2.at[s, r], recv2.at[s, r], {"seq": s})
+
+    def every_other(fn):
+        def one(k, _):
+            fn(lax.rem(me + k, chunks))
+            return 0
+        lax.fori_loop(1, chunks, one, 0)
+
+    def send_row(r):
+        every_other(lambda s: first(s, r).start())
+        recv_v[me, r] = part_v[me, r]
+
+    def sum_row(r):
+        every_other(lambda s: landed_first(s, r).wait_recv())
+        total = recv_v[0, r].astype(F32)
+        for s in range(1, chunks):
+            total = total + recv_v[s, r].astype(F32)
+        sel2_v[me, r] = total.astype(BF16)
+        every_other(lambda s: second(s, r).start())
+
+    for ref in (gstepw_ref, gsbias_ref, gskip_ref, gd_s, gtaps_ref, gcbias_ref, gselw_ref):
+        ref[...] = jnp.zeros_like(ref)
+    rate_s[...] = -jnp.exp(decay_ref[...].astype(F32)) * LOG2E
+
+    def ggate_out(i):
+        c, r = where_of(i)
+        return pltpu.make_async_copy(ggate_v.at[i % 2], ggate_ref.at[c, r], ggate_sem.at[i % 2])
+
+    def gci_out(i):
+        c, r = where_of(i)
+        return pltpu.make_async_copy(gci_v.at[i % 2], gci_ref.at[c, r], gci_sem.at[i % 2])
+
+    def scan(i, _):
+        c, r = where_of(i)
+        slot = i % 2
+
+        @pl.when(i + 1 < count)
+        def _():
+            for one in fetch(i + 1):
+                one.start()
+
+        @pl.when(i >= 2)
+        def _():
+            ggate_out(i - 2).wait()
+
+        for one in fetch(i):
+            one.wait()
+        back_step(sel_ref[c, r].astype(F32), x_v[slot].astype(F32), i % chunks == 0, gact_v.at[slot], gg_v.at[slot], tail_v.at[slot],
+                  start_v.at[slot], dt_v.at[slot], slope_v.at[slot], stepw_ref, skip_ref,
+                  ggate_v.at[slot], gvals_v.at[c, r], part_v.at[c, r], gstepw_ref, gsbias_ref, gskip_ref,
+                  u_s, gy_s, gu_s, ah_s, bcoef_s, bt_s, hist_s, adj_a, harm_a, adj_b, harm_b, db_s, dc_s, carry_s, gd_s, rate_s, factor_s, kept_s, rank, n)
+        ggate_out(i).start()
+        late = min(3, chunks - 1)
+
+        @pl.when((i % chunks == chunks - 1) & (r + 1 < rows))
+        def _():
+            send_row(r)
+
+        @pl.when((i % chunks == late) & (r > 0))
+        def _():
+            sum_row(r - 1)
+
+        if extra:
+            pl.when(i == 2)(chip_sum)
+            pl.when(i == 8)(whole_sum)
+        if inside:
+            lo = jnp.where(edge, jnp.where(i == 4, 0, jnp.where(i == 9, 1, 2)), jnp.where(i == 9, 0, 1))
+            hi = jnp.where(edge, lo + 1, jnp.where(i == 9, 1, jnp.where(i == 13, 3, 0)))
+
+            @pl.when((i == 4) | (i == 9) | (i == 13))
+            def _():
+                for k in range(own_v.shape[0]):
+                    pl.when(i == 4)(own_loads[k].wait)
+
+                def one(k, _):
+                    settle(k)
+                    return 0
+                lax.fori_loop(lo, hi, one, 0)
+        return 0
+
+    lax.fori_loop(0, count, scan, 0)
+    send_row(rows - 1)
+    gdecay_ref[...] = gd_s[...] * rate_s[...] * (1.0 / LOG2E)
+    for i in range(max(0, count - 2), count):
+        ggate_out(i).wait()
+
+    def conv(i, _):
+        c, r = where_of(i)
+
+        @pl.when(i >= 2)
+        def _():
+            gci_out(i - 2).wait()
+
+        conv_back_step(ci_ref.at[c, r], ci_ref.at[jnp.maximum(c - 1, 0), r], c == 0, i % chunks == 0, gvals_v.at[c, r], sel2_v.at[c, r],
+                       taps_ref, cbias_ref, selw_ref, gci_v.at[i % 2], gtaps_ref, gcbias_ref, gselw_ref, ext_s, gext_s)
+        gci_out(i).start()
+        return 0
+
+    for r in range(rows - 1):
+        every_other(lambda s: landed_second(s, r).wait_recv())
+    lax.fori_loop(0, count - chunks, conv, 0)
+    sum_row(rows - 1)
+    if inside:
+        settle(zs - 1)
+        red_ref[...] = own_v[z]
+    every_other(lambda s: landed_second(s, rows - 1).wait_recv())
+    lax.fori_loop(count - chunks, count, conv, 0)
+    for i in range(max(0, count - 2), count):
+        gci_out(i).wait()
+    for r in range(rows):
+        every_other(lambda s: first(s, r).wait_send())
+        every_other(lambda s: second(s, r).wait_send())
+    if extra:
+        to_core.wait_send()
+        for j in range(1, xs):
+            across(j).wait_send()
+        back_in.wait_recv()
+        back_out.wait_send()
+    if inside:
+        for i in range(zs):
+            t = dest(i)
+            for h in range(2):
+                to_side(i, h).wait_send()
+
+                @pl.when(t > z)
+                def _():
+                    climb(t, h).wait_send()
+
+                @pl.when(t < z)
+                def _():
+                    sink(t, h).wait_send()
+
+
+def backward(gg, gact, tail, x, dt, slope, starts, sel, ci, stepw, decay, skip, taps, cbias, selw, mixed, gout, copies, n):
+    chunks, rows, length, width = ci.shape
+    rank = stepw.shape[0]
+    zs, ys = grid_of(chunks, copies)
+    xs = max(1, copies // 2)
+    wide = BLOCK * n
+    inside = mixed is not None
+    extra = copies % 2 == 0
+    sds = jax.ShapeDtypeStruct
+    dma = pltpu.SemaphoreType.DMA
+    vmem = pl.BlockSpec(memory_space=pltpu.VMEM)
+    hbm = pl.BlockSpec(memory_space=pl.ANY)
+    args = [gg, gact, tail, x, dt, slope, starts, sel, ci, stepw, decay, skip, taps, cbias, selw]
+    in_specs = [hbm] * 7 + [vmem] * 8
+    out_specs = [hbm] * 2 + [vmem] * 7
+    out_shape = [sds(ci.shape, BF16), sds(ci.shape, BF16), sds((rank, width), F32), sds((1, width), F32), sds((n, width), F32), sds((1, width), F32),
+                 sds(taps.shape, F32), sds((1, width), F32), sds(selw.shape, F32)]
+    tile, coef = (length, width), sel.shape
+    scratch = [pltpu.VMEM((2,) + tile, F32), pltpu.VMEM((2,) + tile, F32), pltpu.VMEM((2,) + tile, BF16), pltpu.VMEM((2,) + tile, BF16),
+               pltpu.VMEM((2,) + tile, F32), pltpu.VMEM((2,) + tile, F32), pltpu.VMEM((2, n, width), F32),
+               pltpu.VMEM((2,) + tile, BF16), pltpu.VMEM((2,) + tile, BF16), pltpu.VMEM(ci.shape, F32),
+               pltpu.VMEM(coef, BF16), pltpu.VMEM(coef, BF16), pltpu.VMEM(coef, BF16),
+               pltpu.VMEM(tile, F32), pltpu.VMEM(tile, F32), pltpu.VMEM(tile, F32), pltpu.VMEM(tile, F32),
+               pltpu.VMEM((length, wide), BF16), pltpu.VMEM((2 * n, length), F32), pltpu.VMEM((length * n, width), BF16),
+               pltpu.VMEM((wide, width), BF16), pltpu.VMEM((wide, width), BF16), pltpu.VMEM((wide, width), BF16), pltpu.VMEM((wide, width), BF16),
+               pltpu.VMEM((length, wide), F32), pltpu.VMEM((length, wide), F32),
+               pltpu.VMEM((n, width), F32), pltpu.VMEM((n, width), F32), pltpu.VMEM((n, width), F32),
+               pltpu.VMEM((length * n, width), F32), pltpu.VMEM((length * n, width), F32),
+               pltpu.VMEM((length + 8, width), F32), pltpu.VMEM((length + 8, width), F32),
+               dma((7, 2)), dma((2,)), dma((2,)), dma((chunks, rows)), dma((chunks, rows)), dma((chunks, rows)), dma((chunks, rows))]
+    if inside:
+        tokens, model = mixed.shape[1:]
+        args.append(mixed)
+        in_specs.append(hbm)
+        out_specs.append(vmem)
+        out_shape.append(sds((tokens, model), BF16))
+        scratch += [pltpu.VMEM((zs, tokens, model), BF16), pltpu.VMEM((zs, tokens, model), BF16), pltpu.VMEM((zs + 1, tokens, model), BF16),
+                    dma((zs,)), dma((zs, 2)), dma((zs, 2)), dma((zs, 2)), dma((zs, 2)), dma((zs + 1, 2))]
+    if extra:
+        args.append(gout)
+        in_specs.append(vmem)
+        out_specs.append(vmem)
+        out_shape.append(sds(gout.shape, BF16))
+        part = (gout.shape[0] // 2, gout.shape[1])
+        scratch += [pltpu.VMEM(part, BF16), pltpu.VMEM(part, BF16), pltpu.VMEM((xs,) + part, BF16),
+                    dma(()), dma(()), dma((xs,)), dma((xs,)), dma(()), dma(())]
+    return pl.pallas_call(
+        functools.partial(backward_kernel, chunks=chunks, copies=copies, n=n, inside=inside, extra=extra),
+        in_specs=in_specs,
+        out_specs=out_specs,
+        out_shape=out_shape,
+        scratch_shapes=scratch,
+        compiler_params=pltpu.CompilerParams(collective_id=2, has_side_effects=True, vmem_limit_bytes=63 * 1024 * 1024),
+        name="backward",
+    )(*args)
+
+
 from jax.sharding import PartitionSpec as P
 
 
@@ -1311,29 +1554,26 @@
         step_weight, step_row, decay_log, skip_row, copies, n)
     gm = gm.reshape(tokens, model)
     gated2 = gated.reshape(tokens, width)
-    mixed = jnp.dot(gated2, output_weight, preferred_element_type=F32).astype(BF16)
-    mixed = lax.psum_scatter(shaped(mixed), "seq", scatter_dimension=0, tiled=False)
+    mixed = shaped(jnp.dot(gated2, output_weight, preferred_element_type=F32).astype(BF16))
+    zs, ys = grid_of(chunks, copies)
+    inside = ys == 2 and zs == 4
     source = hidden.astype(F32)
-    output = ((source + mixed.astype(F32)) * valid).astype(BF16)
-
     gg = shaped(lax.dot_general(gm, output_weight, (((1,), (1,)), ((), ())), preferred_element_type=F32))
-    ggate, gvals, gpre, gpart, gstepw, gstepb, gdecay, gskip = scan_backward(
-        sel, x, gact, gg, tail, starts, dt, slope, step_weight, decay_log, skip_row, n)
     tn = lambda a, b: lax.dot_general(a, b, (((0,), (0,)), ((), ())), preferred_element_type=F32)
     gout = tn(gated2, gm).astype(BF16)
-    small = jnp.concatenate([gstepw, gdecay, gstepb, gskip], axis=0).astype(BF16)
-    small = jnp.pad(small, ((0, -small.shape[0] % 32), (0, 0)))
-    gsel, gout, small = total_over_seq(gpart, chunks, copies, 2, (gout, small))
-    gout, small = gout.astype(F32), small.astype(F32)
-    gstepw, gdecay, gstepb, gskip = small[:rank], small[rank:rank + n], small[rank + n], small[rank + n + 1]
-    gci, gtaps, gconvb, gselw = conv_backward(ci, gvals, gsel, conv_weight, bias_row, select_weight)
+    flat = lambda a: a.reshape(chunks, rows * length, a.shape[-1])
+    got = backward(gg, gact, tail, x, dt, slope, starts, sel, ci, step_weight, decay_log, skip_row, conv_weight, bias_row, select_weight,
+                   flat(mixed) if inside else None, gout, copies, n)
+    ggate, gci, gstepw, gstepb, gdecay, gskip, gtaps, gconvb, gselw = got[:9]
+    mixed = got[9].reshape(rows, length, model) if inside else lax.psum_scatter(mixed, "seq", scatter_dimension=0, tiled=False)
+    gout = got[-1].astype(F32)
+    output = ((source + mixed.astype(F32)) * valid).astype(BF16)
     tap_count = gtaps.shape[0]
     gci2 = gci.reshape(tokens, width)
     ggate2 = ggate.reshape(tokens, width)
     ginc, ging = (tn(normed, g).astype(BF16).reshape(chunks, copies, share // copies, width) for g in (gci2, ggate2))
-    late = jnp.concatenate([gselw, gtaps, gconvb], axis=0)
-    late = jnp.pad(late, ((0, -late.shape[0] % 8), (0, 0)))
-    flat = lambda a: a.reshape(chunks, rows * length, width)
+    late = jnp.concatenate([gselw, gstepw, gdecay, gtaps, gstepb, gskip, gconvb], axis=0).astype(BF16)
+    late = jnp.pad(late, ((0, -late.shape[0] % 16), (0, 0)))
     got = scatter_sums(flat(gci), flat(ggate), w_all, late, ginc, ging, chunks, copies, split)
     scaled, late = got[:2]
     if split:
@@ -1347,8 +1587,10 @@
     scaled = scaled.reshape(rows, length, model).astype(F32) * gain_row
     inverse = lax.rsqrt(jnp.mean(source * source, axis=-1, keepdims=True) + EPSILON)
     ghidden = inverse * scaled - source * inverse ** 3 * jnp.mean(scaled * source, axis=-1, keepdims=True) + cotangent
-    picked = gselw.shape[0]
-    gselw, gtaps, gconvb = late[:picked], late[picked:picked + tap_count], late[picked + tap_count]
+    sizes = (gselw.shape[0], rank, n, tap_count)
+    ends = [sum(sizes[:k + 1]) for k in range(len(sizes))]
+    gselw, gstepw, gdecay, gtaps = (late[e - k:e] for e, k in zip(ends, sizes))
+    gstepb, gskip, gconvb = (late[ends[-1] + k] for k in range(3))
     return (output, ghidden, ggain, gin, gtaps, gconvb, gselw, gstepw, gstepb,
             gdecay, gskip, gout)
 

time: 633 us -> 598 us (0.945); the launches traced: 632 us -> 590 us
  Pallas kernels: 532 us -> 511 us
  between operations: 14.1 us -> 0.8 us
    pallas_call x3 -> x1, Pallas kernels: 167 us -> 142 us  [backward(): pl.pallas_call(functools.partial(backward_kernel, chunks=chunks, copies=c...]
    pallas_call x1, Pallas kernels: 119 us -> 139 us  [gather_project(): pl.pallas_call(functools.partial(gather_project_kernel, chunks=chunks, co...]
    pallas_call x1, Pallas kernels: 124 us -> 113 us  [scatter_sums(): pl.pallas_call(functools.partial(scatter_kernel, chunks=chunks, copies=co...]
  transfers between devices with their start and end apart: 1 -> 0, of which waited for: 0 -> 0; matrix products, arithmetic and copies ran while one was open for 10% -> 0% of each run, Pallas kernels for 46% -> 0%
where the time goes in v4:
time: 598 us; the launch traced here: 590 us
  Pallas kernels  511 us (85%)
  matrix products  42 us (7%)
  other arithmetic  22.5 us (4%)
  local copies, waits for them, and re-layouts  13.6 us (2%)
    pallas_call x1, Pallas kernels, backward(): pl.pallas_call(functools.partial(backward_kernel, chunks=chunks, copies=c...  142 us
    pallas_call x1, Pallas kernels, gather_project(): pl.pallas_call(functools.partial(gather_project_kernel, chunks=chunks, co...  139 us
    pallas_call x1, Pallas kernels, forward(): pl.pallas_call(functools.partial(forward_kernel, chunks=chunks, copies=co...  116 us
    pallas_call x1, Pallas kernels, scatter_sums(): pl.pallas_call(functools.partial(scatter_kernel, chunks=chunks, copies=co...  113 us
    dot_general x3, matrix products, local(): lax.dot_general(a, b, (((0,), (0,)), ((), ())), preferred_element_type=F32)  29.1 us

profile of v4, /device:TPU:0, one launch (start us, length us, event | category | flops | bytes accessed | tf_op | source)
XLA Modules:
  0.0 589.8 jit_solution(1694974477462519368)
XLA Ops:
  0.7 0.7 compare_convert_fusion
  1.4 1.2 convert_element_type.60
  2.6 1.3 reshape.134.cbias_ref.refs_13_
  3.9 1.3 reshape.136.skip_ref.refs_11_
  5.1 1.3 reshape.135.sbias_ref
  6.4 2.4 fusion.10
  8.8 139.3 %gather_project.1 = (bf16[8,256,2048]{2,1,0:T(8,128)(2,1)}, bf16[8,256,512]{2,1,0:T(8,128)(2,1)}, f32[8,256,512]{2,1,0:T(8,128)}, bf16[2048,1024]{1,0:T(8,128)(2,1)}, f32[1,2048]{1,0:T(1,128)}) custom-call(bf16[256,2048]{1,0:T(8,128)(2,1)} %bitcast.39, bf16[256,8192]{1,0:T(8,128)(2,1)} %wq_ref.1, f32[1,256]{1,0:T(1,128)} %bitcast.58), custom_call_target="tpu_custom_call" | custom-call | tf_op jit(solution)/shard_map/gather_project/pallas_call | solution.py:553
  148.1 116.5 %forward.1 = (bf16[8,256,2048]{2,1,0:T(8,128)(2,1)}, bf16[8,2,160,128]{3,2,1,0:T(8,128)(2,1)}, bf16[8,2,128,512]{3,2,1,0:T(8,128)(2,1)}, bf16[8,2,128,512]{3,2,1...) custom-call(bf16[8,2,128,512]{3,2,1,0:T(8,128)(2,1)} %bitcast.41, ...), custom_call_target="tpu_custom_call" | custom-call | tf_op jit(solution)/shard_map/forward/pallas_call | solution.py:771
  264.6 10.0 %convolution_convert_fusion.3.refs_16_ = bf16[512,2048]{1,0:T(8,128)(2,1)} fusion(bf16[2048,512]{1,0:T(8,128)(2,1)} %bitcast.63, bf16[2048,2048]{1,0:T(8,128)(2,1)} %bitcast.61), kind=kOutput, calls=%fused_computation.8 | convolution fusion | flops 4296015872 | bytes 12582912 | tf_op jit(solution)/shard_map/dot_general | solution.py:1562
  274.6 6.1 %fusion.8.refs_0_ = f32[8,2,128,512]{3,2,1,0:T(8,128)} fusion(bf16[8,2,128,2048]{3,2,1,0:T(8,128)(2,1)S(1)} %bitcast.62, bf16[512,2048]{1,0:T(8,128)(2,1)S(1)} %copy-done.12), kind=kOutput, calls=%fused_computation.18 | convolution fusion | flops 4294967296 | bytes 14680064 | tf_op jit(solution)/shard_map/dot_general | solution.py:1561
  280.8 6.7 %convolution_convert_fusion = bf16[2048,2048]{1,0:T(8,128)(2,1)} fusion(bf16[2048,512]{1,0:T(8,128)(2,1)S(1)} %bitcast.64, bf16[512,2048]{1,0:T(8,128)(2,1)S(1)} %copy-done.12), kind=kOutput, calls=%fused_computation.1 | convolution fusion | flops 4299161600 | bytes 12582912 | tf_op jit(solution)/shard_map/dot_general | solution.py:1557
  287.5 141.9 %backward.1 = (bf16[8,2,128,512]{3,2,1,0:T(8,128)(2,1)}, bf16[8,2,128,512]{3,2,1,0:T(8,128)(2,1)}, f32[128,512]{1,0:T(8,128)}, f32[1,512]{1,0:T(1,128)}, f32[16,...) custom-call(f32[8,2,128,512]{3,2,1,0:T(8,128)} %fusion.8.refs_0_, ...), custom_call_target="tpu_custom_call" | custom-call | tf_op jit(solution)/shard_map/backward/pallas_call | solution.py:1514
  429.4 0.8 convert.27
  430.2 0.7 convert.28
  431.6 0.7 convert.26
  432.3 0.8 convert.25
  433.0 1.0 convert.24
  434.0 1.0 convert.23
  435.1 0.7 pad.4.refs_3_
  435.9 9.6 %convolution_convert_fusion.1 = bf16[2048,512]{1,0:T(8,128)(2,1)} fusion(bf16[2048,2048]{1,0:T(8,128)(2,1)} %bitcast.59, bf16[2048,512]{1,0:T(8,128)(2,1)S(1)} %bitcast.47), kind=kOutput, calls=%fused_computation.6 | convolution fusion | flops 4296015872 | bytes 12582912 | tf_op jit(solution)/shard_map/dot_general | solution.py:1562
  445.5 9.4 %convolution_convert_fusion.2 = bf16[2048,512]{1,0:T(8,128)(2,1)} fusion(bf16[2048,2048]{1,0:T(8,128)(2,1)} %bitcast.60, bf16[2048,512]{1,0:T(8,128)(2,1)S(1)} %bitcast.49), kind=kOutput, calls=%fused_computation.7 | convolution fusion | flops 4296015872 | bytes 12582912 | tf_op jit(solution)/shard_map/dot_general | solution.py:1562
  454.9 113.3 %scatter_sums.1 = (bf16[256,2048]{1,0:T(8,128)(2,1)}, f32[320,512]{1,0:T(8,128)}, bf16[256,8192]{1,0:T(8,128)(2,1)}) custom-call(bf16[8,256,512]{2,1,0:T(8,128)(2,1)} %bitcast.48, bf16[8,256,512]{2,1,0:T(8,128)(2,1)} %bitcast.46, bf16[2048,1024]{1,0:T(8,128)(2,1)} %get-tuple-element.54.refs_2_, bf16[320,512]{1,0:T(8,128)(2,1)} %pad.4.refs_3_, ...), custom_call_target="tpu_custom_call" | custom-call | tf_op jit(solution)/shard_map/scatter_sums/pallas_call | solution.py:1147
  568.3 1.9 fusion.2
  570.3 1.4 fusion.11
  571.7 1.3 slice.21
  573.0 1.4 slice.26
  574.4 1.7 slice.24
  576.0 1.7 slice.23
  577.8 2.8 fusion.5
  580.6 2.7 convert_element_type.75
  583.3 1.4 copy-done
  584.7 4.5 multiply_reduce_fusion
  (32 shorter events, 1.4 us)
Async XLA Ops:
  264.6 10.1 %copy-start.11 = (bf16[8,256,2048]{2,1,0:T(8,128)(2,1)S(1)}, bf16[8,256,2048]{2,1,0:T(8,128)(2,1)}, u32[]{:S(2)}) copy-start(bf16[8,256,2048]{2,1,0:T(8,128)(2,1)} %get-tuple-element.42) | copy-start | bytes 25165828
  264.6 10.1 %copy-start.12 = (bf16[512,2048]{1,0:T(8,128)(2,1)S(1)}, bf16[512,2048]{1,0:T(8,128)(2,1)}, u32[]{:S(2)}) copy-start(bf16[512,2048]{1,0:T(8,128)(2,1)} %param.25) | copy-start | bytes 6291460
  274.6 6.1 %copy-start.13 = (bf16[8,2,128,512]{3,2,1,0:T(8,128)(2,1)S(1)}, bf16[8,2,128,512]{3,2,1,0:T(8,128)(2,1)}, u32[]{:S(2)}) copy-start(bf16[8,2,128,512]{3,2,1,0:T(8,128)(2,1)} %get-tuple-element.50) | copy-start | bytes 6291460
  429.4 6.5 %copy-start.6 = (bf16[8,2,128,512]{3,2,1,0:T(8,128)(2,1)S(1)}, bf16[8,2,128,512]{3,2,1,0:T(8,128)(2,1)}, u32[]{:S(2)}) copy-start(bf16[8,2,128,512]{3,2,1,0:T(8,128)(2,1)} %get-tuple-element.53) | copy-start | bytes 6291460
  435.9 9.6 %copy-start.7 = (bf16[8,2,128,512]{3,2,1,0:T(8,128)(2,1)S(1)}, bf16[8,2,128,512]{3,2,1,0:T(8,128)(2,1)}, u32[]{:S(2)}) copy-start(bf16[8,2,128,512]{3,2,1,0:T(8,128)(2,1)} %get-tuple-element.52) | copy-start | bytes 6291460
  454.9 113.4 %copy-start.1 = (bf16[2,128,2048]{2,1,0:T(8,128)(2,1)S(1)}, bf16[2,128,2048]{2,1,0:T(8,128)(2,1)}, u32[]{:S(2)}) copy-start(bf16[2,128,2048]{2,1,0:T(8,128)(2,1)} %param.13) | copy-start | bytes 3145732
  454.9 113.4 %copy-start.9 = (f32[1,2048]{1,0:T(1,128)S(1)}, f32[1,2048]{1,0:T(1,128)}, u32[]{:S(2)}) copy-start(f32[1,2048]{1,0:T(1,128)} %get-tuple-element.64) | copy-start | bytes 24580
  568.3 9.5 %copy-start.2 = (bf16[256,2048]{1,0:T(8,128)(2,1)S(1)}, bf16[256,2048]{1,0:T(8,128)(2,1)}, u32[]{:S(2)}) copy-start(bf16[256,2048]{1,0:T(8,128)(2,1)} %get-tuple-element.63) | copy-start | bytes 3145732
  568.3 9.5 %copy-start.3 = (bf16[2,128,2048]{2,1,0:T(8,128)(2,1)S(1)}, bf16[2,128,2048]{2,1,0:T(8,128)(2,1)}, u32[]{:S(2)}) copy-start(bf16[2,128,2048]{2,1,0:T(8,128)(2,1)} %param.14) | copy-start | bytes 3145732
  568.3 9.5 %copy-start.8 = (bf16[256,2048]{1,0:T(8,128)(2,1)S(1)}, bf16[256,2048]{1,0:T(8,128)(2,1)}, u32[]{:S(2)}) copy-start(bf16[256,2048]{1,0:T(8,128)(2,1)} %get-tuple-element.51) | copy-start | bytes 3145732
  577.8 2.8 copy-start.5
  577.8 5.5 copy-start.4
  580.6 4.1 copy-start
  584.7 4.5 copy-start.10

commit v5 on v4

--- a/solution.py
+++ b/solution.py
@@ -97,8 +97,8 @@
     gated_ref[...] = (ssm * gact).astype(BF16)
 
 
-def back_step(selected, x, fresh, gact_ref, gg_ref, tail_ref, start_ref, dt_ref, slope_ref, stepw_ref, skip_ref,
-              ggate_ref, gvals_ref, gsel_ref, gstepw_ref, gbias_ref, gskip_ref,
+def back_step(selected, x, fresh, gact_ref, gg_ref, start_ref, dt_ref, slope_ref, stepw_ref, skip_ref,
+              gvals_ref, gsel_ref, gstepw_ref, gbias_ref, gskip_ref,
               u_s, gy_s, gu_s, ah_s, bcoef_s, bt_s, hist_s, adj_a, harm_a, adj_b, harm_b, db_s, dc_s, carry_s, gd_s, rate_s, factor_s, kept_s, rank, n):
     length = x.shape[0]
     wide = BLOCK * n
@@ -106,7 +106,6 @@
     carry_s[...] = jnp.where(fresh, 0.0, carry_s[...])
     gg = gg_ref[...]
     gy = gg * gact_ref[...]
-    ggate_ref[...] = (gg * tail_ref[...].astype(F32)).astype(BF16)
     gskip_ref[...] += jnp.sum(gy * x, axis=0, keepdims=True)
     gy_s[...] = gy
     dt = dt_ref[...]
@@ -480,6 +479,8 @@
             k = k0 - jnp.where(own, 0, 1)
             o = z + k * (2 * lower - 1)
             ok = (k >= 0) & (k < zs) & (o >= 0) & (o < zs) & ((lower == 0) | (k > 0))
+            if even:
+                ok = ok & (own | (o != partner))
 
             @pl.when(ok & jnp.logical_not(own))
             def _():
@@ -495,15 +496,20 @@
             return 0
         lax.fori_loop(first * 2 * ys, last * 2 * ys, one, 0)
 
-    work(0, min(3, zs))
+    work(0, min(2, zs))
 
     def later(k, _):
         relay(k)
-        work(k, k + 1)
+        work(k - 1, k)
         return 0
 
     lax.fori_loop(3, zs, later, 0)
+    work(max(2, zs - 1), zs)
     work(zs, zs + 1)
+    if even:
+        for h in range(2):
+            landed(partner, 1 - y, h).wait_recv()
+        project(partner * ys + 1 - y)
     w_out.wait()
 
     def drain_first(s):
@@ -568,11 +574,15 @@
     )(hidden, wq, gain)
 
 
-def forward_kernel(ci_ref, gate_ref, gm_ref, taps_ref, cbias_ref, selw_ref, stepw_ref, sbias_ref, decay_ref, skip_ref,
-                   gmall_ref, sel_ref, x_ref, gated_ref, gact_ref, tail_ref, dt_ref, slope_ref, start_ref,
+SPLIT = 9
+
+
+def forward_kernel(ci_ref, gate_ref, gm_ref, taps_ref, cbias_ref, selw_ref, stepw_ref, sbias_ref, decay_ref, skip_ref, wout_ref,
+                   gmall_ref, sel_ref, x_ref, gated_ref, gact_ref, dt_ref, slope_ref, start_ref, mixed_ref, gg_ref, ggate_ref,
                    gate_v, part_v, recv_v, x_v, gated_v, gact_v, tail_v, dt_v, slope_v, start_v,
+                   gm_v, mixed_v, gg_v, ggate_v,
                    ext_s, u_s, y_s, coef_s, bt_s, hist_a, hist_b, state_s, rate_s,
-                   load_sem, own_sem, out_sem, grecv, gside, gup, gdown, glend, send1, recv1, send2, recv2, *, chunks, copies, n):
+                   load_sem, own_sem, out_sem, gm_sem, mixed_sem, gg_sem, grecv, gside, gup, gdown, glend, send1, recv1, send2, recv2, *, chunks, copies, n):
     zs, ys = grid_of(chunks, copies)
     me = lax.axis_index("seq")
     z, y = me // ys, me % ys
@@ -608,11 +618,13 @@
     def when(cond, fn):
         pl.when(cond)(fn)
 
-    for h in range(2):
+    def first_sends(h):
         when(z + 1 < zs, lambda: up(z, h, None).start())
         when(z > 0, lambda: down(z, h, None).start())
         for j in range(1, ys):
             side(z, j, h, None).start()
+
+    first_sends(0)
 
     partner = z + 1 - 2 * (z % 2)
 
@@ -677,6 +689,7 @@
         lax.fori_loop(1, chunks, one, 0)
 
     every_other(lambda s: first(s).start())
+    first_sends(1)
     recv_v[me] = part_v[me]
     every_other(lambda s: landed_first(s).wait_recv())
     total = recv_v[0].astype(F32)
@@ -690,7 +703,7 @@
         lend_on()
     every_other(lambda s: landed_second(s).wait_recv())
     load.wait()
-    pairs = ((gated_v, gated_ref), (gact_v, gact_ref), (tail_v, tail_ref), (dt_v, dt_ref), (slope_v, slope_ref), (start_v, start_ref))
+    pairs = ((gated_v, gated_ref), (gact_v, gact_ref), (dt_v, dt_ref), (slope_v, slope_ref), (start_v, start_ref))
 
     def outs(c, r):
         return [pltpu.make_async_copy(src.at[c, r], dst.at[c, r], out_sem.at[1 + k, c * rows + r]) for k, (src, dst) in enumerate(pairs)]
@@ -706,25 +719,79 @@
         return 0
 
     count = rows * chunks
-    parts = max(1, zs - 2)
-    for k in range(parts):
-        lax.fori_loop(count * k // parts, count * (k + 1) // parts, scan, 0)
-        if 2 + k < zs:
-            relay(2 + k)
-        if k == 0 and zs > 2:
-            lend_on()
-
-    def others(o, _):
-        for j in range(1, ys):
-            landed(o, lax.rem(y + j, ys), 0).wait_recv()
+    if zs > 2:
+        relay(2)
+        lend_on()
+    cuts = [count * SPLIT // 16 + (count - count * SPLIT // 16) * k // max(1, zs - 3) for k in range(zs - 2)] if zs > 3 else []
+    at = 0
+    for k, cut in enumerate(cuts[:-1]):
+        lax.fori_loop(at, cut, scan, 0)
+        relay(3 + k)
+        at = cut
+    lax.fori_loop(at, count, scan, 0)
+
+    tile = min(512, model)
+
+    def mixed_out(s):
+        return pltpu.make_async_copy(mixed_v.at[s % 2], mixed_ref.at[s], mixed_sem.at[s % 2])
+
+    def mix(s, _):
+        @pl.when(s >= 2)
+        def _():
+            mixed_out(s - 2).wait()
+
+        lhs = gated_v[s].reshape(tokens, width)
+
+        def one(i, _):
+            sl = pl.ds(pl.multiple_of(i * tile, tile), tile)
+            mixed_v[s % 2, :, sl] = jnp.dot(lhs, wout_ref[:, sl], preferred_element_type=F32).astype(BF16)
+            return 0
+        lax.fori_loop(0, model // tile, one, 0)
+        mixed_out(s).start()
+        return 0
+
+    lax.fori_loop(0, chunks, mix, 0)
+    for s in range(chunks - 2, chunks):
+        mixed_out(s).wait()
+
+    own.wait()
+
+    def bring(s):
+        return pltpu.make_async_copy(gmall_ref.at[s], gm_v, gm_sem)
+
+    def back(s):
+        bring(s).start()
+        bring(s).wait()
+        got = nt_dot(gm_v[...], wout_ref[...])
+        gg_v[...] = got.reshape(gg_v.shape)
+        ggate_v[...] = (got * tail_v[s].reshape(tokens, width).astype(F32)).astype(BF16).reshape(ggate_v.shape)
+        one, two = pltpu.make_async_copy(gg_v, gg_ref.at[s], gg_sem.at[0]), pltpu.make_async_copy(ggate_v, ggate_ref.at[s], gg_sem.at[1])
+        one.start()
+        two.start()
+        one.wait()
+        two.wait()
+
+    last = [[k] + [q for q in range(zs) if q not in (k, k + 1 - 2 * (k % 2))] + [k + 1 - 2 * (k % 2)] for k in range(zs)] if even else [list(range(zs))] * zs
+
+    def others(i, _):
+        lower, k = i // zs, i % zs
+        o = 0
+        for p in range(zs):
+            for q in range(zs):
+                o = o + jnp.where((z == p) & (k == q), last[p][q], 0)
+
+        @pl.when(lower > 0)
+        def _():
+            landed(o, lax.rem(y + lower, ys), 0).wait_recv()
             if even:
                 when(o != z, lambda: landed(o, 1 - y, 1).wait_recv())
             else:
-                landed(o, lax.rem(y + j, ys), 1).wait_recv()
+                landed(o, lax.rem(y + lower, ys), 1).wait_recv()
+
+        back(o * ys + lax.rem(y + lower, ys))
         return 0
 
-    lax.fori_loop(0, zs, others, 0)
-    own.wait()
+    lax.fori_loop(0, ys * zs, others, 0)
     x_out.wait()
 
     def settle(i, _):
@@ -756,7 +823,7 @@
         lend().wait_send()
 
 
-def forward(ci, gate, gm, taps, cbias, selw, stepw, sbias, decay, skip, copies, n):
+def forward(ci, gate, gm, taps, cbias, selw, stepw, sbias, decay, skip, wout, copies, n):
     chunks, rows, length, width = ci.shape
     tokens, model = gm.shape
     zs, ys = grid_of(chunks, copies)
@@ -770,22 +837,143 @@
     full = ci.shape
     return pl.pallas_call(
         functools.partial(forward_kernel, chunks=chunks, copies=copies, n=n),
-        in_specs=[vmem, hbm] + [vmem] * 8,
-        out_specs=[hbm, vmem] + [hbm] * 7,
-        out_shape=[sds((chunks, tokens, model), BF16), sds(coef, BF16), sds(full, BF16), sds(full, BF16), sds(full, F32), sds(full, BF16),
-                   sds(full, F32), sds(full, F32), sds(starts, F32)],
+        in_specs=[vmem, hbm] + [vmem] * 9,
+        out_specs=[hbm, vmem] + [hbm] * 9,
+        out_shape=[sds((chunks, tokens, model), BF16), sds(coef, BF16), sds(full, BF16), sds(full, BF16), sds(full, F32),
+                   sds(full, F32), sds(full, F32), sds(starts, F32), sds((chunks, tokens, model), BF16), sds(full, F32), sds(full, BF16)],
         scratch_shapes=[
             pltpu.VMEM(full, F32), pltpu.VMEM(coef, BF16), pltpu.VMEM(coef, BF16), pltpu.VMEM(full, BF16), pltpu.VMEM(full, BF16),
             pltpu.VMEM(full, F32), pltpu.VMEM(full, BF16), pltpu.VMEM(full, F32), pltpu.VMEM(full, F32), pltpu.VMEM(starts, F32),
+            pltpu.VMEM((tokens, model), BF16), pltpu.VMEM((2, tokens, model), BF16), pltpu.VMEM(full[1:], F32), pltpu.VMEM(full[1:], BF16),
             pltpu.VMEM((length + 8, width), F32), pltpu.VMEM((length, width), F32), pltpu.VMEM((length, width), F32),
             pltpu.VMEM((length, wide), BF16), pltpu.VMEM((2 * n, length), F32), pltpu.VMEM((wide, width), BF16), pltpu.VMEM((wide, width), BF16),
             pltpu.VMEM((n, width), F32), pltpu.VMEM((n, width), F32),
-            dma(()), dma(()), dma((7, rows * chunks)), dma((chunks, 2)), dma((zs, max(1, ys - 1), 2)), dma((zs, 2)), dma((zs, 2)), dma(()),
+            dma(()), dma(()), dma((7, rows * chunks)), dma(()), dma((2,)), dma((2,)), dma((chunks, 2)), dma((zs, max(1, ys - 1), 2)), dma((zs, 2)), dma((zs, 2)), dma(()),
             dma((chunks,)), dma((chunks,)), dma((chunks,)), dma((chunks,)),
         ],
         compiler_params=pltpu.CompilerParams(collective_id=1, has_side_effects=True, vmem_limit_bytes=60 * 1024 * 1024),
         name="forward",
-    )(ci, gate, gm, taps, cbias, selw, stepw, sbias, decay, skip)
+    )(ci, gate, gm, taps, cbias, selw, stepw, sbias, decay, skip, wout)
+
+
+class Exchange:
+    def __init__(self, gin, out, bufs, sems, chunks, copies):
+        self.gin, self.out = gin, out
+        self.g1, self.mine_v, self.g2, self.t_v, self.fin = bufs
+        self.load, self.s1, self.r1, self.s2, self.r2, self.s3, self.r3, self.s4, self.r4 = sems
+        self.chunks, self.xs = chunks, copies // 2
+        self.me, self.mine = lax.axis_index("seq"), lax.axis_index("dp")
+        self.x, self.c = self.mine // 2, self.mine % 2
+        self.piece, self.width = self.t_v.shape[1:]
+
+    def own(self, q):
+        return pltpu.make_async_copy(self.gin.at[:, q * 2 + self.c], self.mine_v.at[q], self.load.at[q])
+
+    def to_core(self, q):
+        return remote(self.gin.at[:, q * 2 + 1 - self.c], self.g1.at[q], self.s1.at[q], self.r1.at[q], {"dp": self.x * 2 + 1 - self.c})
+
+    def across(self, q):
+        return remote(self.mine_v.at[q], self.g2.at[self.x], self.s2.at[q], self.r2.at[self.x], {"dp": q * 2 + self.c})
+
+    def from_across(self, q):
+        return remote(self.g2.at[q], self.g2.at[q], self.s2.at[q], self.r2.at[q], {"dp": q * 2 + self.c})
+
+    def columns(self, s):
+        return self.fin.at[:, pl.ds(pl.multiple_of(s * self.width, self.width), self.width)]
+
+    def turn(self, s):
+        return remote(self.t_v.at[s], self.columns(self.me), self.s3.at[s], self.r3.at[self.me], {"seq": s})
+
+    def turned(self, s):
+        return remote(self.columns(s), self.columns(s), self.s3.at[s], self.r3.at[s], {"seq": s})
+
+    def rows_of(self, d):
+        return self.out.at[pl.ds(pl.multiple_of(d * self.piece, self.piece), self.piece)]
+
+    def share_to(self, k, d):
+        return remote(self.fin, self.rows_of(self.mine), self.s4.at[k], self.r4.at[self.mine], {"dp": d})
+
+    def hand_on(self, row, k):
+        return remote(self.rows_of(row), self.rows_of(row), self.s4.at[k], self.r4.at[row], {"dp": self.x * 2 + 1 - self.c})
+
+    def shared(self, d):
+        return remote(self.rows_of(d), self.rows_of(d), self.s4.at[0], self.r4.at[d], {"dp": d})
+
+    def keep(self):
+        return pltpu.make_async_copy(self.fin, self.rows_of(self.mine), self.load.at[self.xs])
+
+    def others(self, fn):
+        def one(k, _):
+            fn(lax.rem(self.me + k, self.chunks))
+            return 0
+        lax.fori_loop(1, self.chunks, one, 0)
+
+    def column_peers(self):
+        return [lax.rem(self.x + j, self.xs) * 2 + self.c for j in range(1, self.xs)]
+
+    def begin(self):
+        for q in range(self.xs):
+            self.own(q).start()
+            self.to_core(q).start()
+
+    def chip(self):
+        for q in range(self.xs):
+            self.own(q).wait()
+            self.to_core(q).wait_recv()
+
+            def fold(s, _):
+                self.mine_v[q, s] = (self.mine_v[q, s].astype(F32) + self.g1[q, s].astype(F32)).astype(BF16)
+                return 0
+            lax.fori_loop(0, self.chunks, fold, 0)
+            pl.when(q != self.x)(lambda: self.across(q).start())
+
+    def spread(self):
+        for q in range(self.xs):
+            pl.when(q != self.x)(lambda: self.from_across(q).wait_recv())
+
+        def fold(s, _):
+            total = self.mine_v[self.x, s].astype(F32)
+            for j in range(1, self.xs):
+                total = total + self.g2[lax.rem(self.x + j, self.xs), s].astype(F32)
+            self.t_v[s] = total.astype(BF16)
+            return 0
+        lax.fori_loop(0, self.chunks, fold, 0)
+        self.others(lambda s: self.turn(s).start())
+        self.columns(self.me)[...] = self.t_v[self.me]
+
+    def share(self):
+        self.others(lambda s: self.turned(s).wait_recv())
+        for j, d in enumerate(self.column_peers()):
+            self.share_to(1 + j, d).start()
+        self.share_to(0, self.x * 2 + 1 - self.c).start()
+        self.keep().start()
+
+    def pass_on(self):
+        for j, d in enumerate(self.column_peers()):
+            self.shared(d).wait_recv()
+            self.hand_on(d, self.xs + j).start()
+
+    def finish(self):
+        self.keep().wait()
+        for j in range(self.xs):
+            self.shared(lax.rem(self.x + j, self.xs) * 2 + 1 - self.c).wait_recv()
+        for q in range(self.xs):
+            self.to_core(q).wait_send()
+            pl.when(q != self.x)(lambda: self.across(q).wait_send())
+        self.others(lambda s: self.turn(s).wait_send())
+        for j in range(self.xs):
+            self.share_to(j, self.mine).wait_send()
+        for j, d in enumerate(self.column_peers()):
+            self.hand_on(d, self.xs + j).wait_send()
+
+
+def exchange_scratch(chunks, copies, piece, width):
+    xs = copies // 2
+    dma = pltpu.SemaphoreType.DMA
+    slab = (chunks, piece, width)
+    bufs = [pltpu.VMEM((xs,) + slab, BF16), pltpu.VMEM((xs,) + slab, BF16), pltpu.VMEM((xs,) + slab, BF16), pltpu.VMEM(slab, BF16),
+            pltpu.VMEM((piece, chunks * width), BF16)]
+    return bufs + [dma((xs + 1,)), dma((xs,)), dma((xs,)), dma((xs,)), dma((xs,)), dma((chunks,)), dma((chunks,)), dma((2 * xs,)), dma((copies,))]
 
 
 def order_of(zs):
@@ -793,15 +981,17 @@
 
 
 def scatter_kernel(*refs, chunks, copies, split):
+    gc_ref, gg_ref, w_ref, late_ref = refs[:4]
+    norm_ref = refs[4] if split else None
+    refs = refs[4 + split:]
+    red_ref, sum_ref = refs[:2]
+    all_ref = refs[2] if split else None
+    refs = refs[2 + split:]
+    (ysend_v, yrecv_v, own_v, zrecv_v, lend_v, late_v, w_v, load_sem,
+     ysend, yrecv, zup, zdown, zrecv, lend_sem, lsend, lrecv) = refs[:16]
     if split:
-        (gc_ref, gg_ref, w_ref, late_ref, ginc_ref, ging_ref, red_ref, sum_ref, all_ref,
-         ysend_v, yrecv_v, own_v, zrecv_v, lend_v, late_v, w_v, g1_v, mine_v, g2_v, t_v, fin_v, load_sem,
-         ysend, yrecv, zup, zdown, zrecv, lend_sem, lsend, lrecv,
-         g1send, g1recv, g2send, g2recv, g3send, g3recv, g4send, g4recv) = refs
-    else:
-        (gc_ref, gg_ref, w_ref, late_ref, red_ref, sum_ref,
-         ysend_v, yrecv_v, own_v, zrecv_v, lend_v, late_v, w_v, load_sem,
-         ysend, yrecv, zup, zdown, zrecv, lend_sem, lsend, lrecv) = refs
+        gin_v, norm_v, norm_sem = refs[16:19]
+        trade = Exchange(gin_v, all_ref, refs[19:24], refs[24:33], chunks, copies)
     zs, ys = grid_of(chunks, copies)
     xs = copies // 2
     me, mine = lax.axis_index("seq"), lax.axis_index("dp")
@@ -822,16 +1012,13 @@
 
     w_in = pltpu.make_async_copy(w_ref, w_v, load_sem.at[0])
     w_in.start()
+
+    def norm_in(s):
+        cols = pl.ds(pl.multiple_of(s * norm_v.shape[-1], norm_v.shape[-1]), norm_v.shape[-1])
+        return pltpu.make_async_copy(norm_ref.at[:, :, cols], norm_v.at[s % 2], norm_sem.at[s % 2])
+
     if split:
-        piece, inner2 = fin_v.shape
-        inner = inner2 // 2
-        sides = (ginc_ref, ging_ref)
-        cols = [pl.ds(part * width, width) for part in range(2)]
-        loads = [[pltpu.make_async_copy(sides[part].at[:, q * 2 + c], mine_v.at[q, :, :, cols[part]], load_sem.at[1 + q * 2 + part]) for part in range(2)]
-                 for q in range(xs)]
-        for q in range(xs):
-            for part in range(2):
-                loads[q][part].start()
+        norm_in(0).start()
     meet(chunks, copies)
 
     def late_to(d):
@@ -846,13 +1033,6 @@
             return 0
         lax.fori_loop(1, copies, one, 0)
 
-    if split:
-        def g1(q, part):
-            return remote(sides[part].at[:, q * 2 + 1 - c], g1_v.at[q, :, :, cols[part]], g1send.at[q, part], g1recv.at[q, part], {"dp": x * 2 + 1 - c})
-
-        for q in range(xs):
-            for part in range(2):
-                g1(q, part).start()
     w_in.wait()
 
     def partial(s, out, at):
@@ -912,84 +1092,27 @@
                 pl.when(dest(i) == partner)(lambda: lend(i).start())
 
     if split:
-        def g2(q, part):
-            return remote(mine_v.at[q, :, :, cols[part]], g2_v.at[x, :, :, cols[part]], g2send.at[q, part], g2recv.at[x, part], {"dp": q * 2 + c})
-
-        def g2_from(q, part):
-            return remote(g2_v.at[q, :, :, cols[part]], g2_v.at[q, :, :, cols[part]], g2send.at[q, part], g2recv.at[q, part], {"dp": q * 2 + c})
-
         for i in range(min(2, zs)):
             outgoing(i)
-        for part in range(2):
-            for q in range(xs):
-                loads[q][part].wait()
-                g1(q, part).wait_recv()
-
-                def fold(s, _):
-                    mine_v[q, s, :, cols[part]] = (mine_v[q, s, :, cols[part]].astype(F32) + g1_v[q, s, :, cols[part]].astype(F32)).astype(BF16)
-                    return 0
-                lax.fori_loop(0, chunks, fold, 0)
-
-                @pl.when(q != x)
-                def _():
-                    g2(q, part).start()
-
-        def columns(part, s):
-            return pl.ds(pl.multiple_of(part * inner + s * width, width), width)
-
-        def g3(s, part):
-            return remote(t_v.at[s, :, cols[part]], fin_v.at[:, columns(part, me)], g3send.at[s, part], g3recv.at[me, part], {"seq": s})
-
-        def g3_from(s, part):
-            return remote(fin_v.at[:, columns(part, s)], fin_v.at[:, columns(part, s)], g3send.at[s, part], g3recv.at[s, part], {"seq": s})
-
-        def every_other(fn):
-            def one(k, _):
-                fn(lax.rem(me + k, chunks))
-                return 0
-            lax.fori_loop(1, chunks, one, 0)
-
-        def third(part):
-            for q in range(xs):
-                @pl.when(q != x)
-                def _():
-                    g2_from(q, part).wait_recv()
-
-            def fold(s, _):
-                total = mine_v[x, s, :, cols[part]].astype(F32)
-                for q in range(1, xs):
-                    total = total + g2_v[lax.rem(x + q, xs), s, :, cols[part]].astype(F32)
-                t_v[s, :, cols[part]] = total.astype(BF16)
-                return 0
-            lax.fori_loop(0, chunks, fold, 0)
-            every_other(lambda s: g3(s, part).start())
-            fin_v[:, columns(part, me)] = t_v[me, :, cols[part]]
-
-        def rows_of(d):
-            return pl.ds(pl.multiple_of(d * piece, piece), piece)
-
-        sides_of = [pl.ds(part * inner, inner) for part in range(2)]
-
-        def g4(d_src, k, d, part):
-            src = fin_v.at[:, sides_of[part]] if d_src is None else all_ref.at[rows_of(d_src), sides_of[part]]
-            row = mine if d_src is None else d_src
-            return remote(src, all_ref.at[rows_of(row), sides_of[part]], g4send.at[k, part], g4recv.at[row, part], {"dp": d})
-
-        def g4_from(d, part):
-            to = all_ref.at[rows_of(d), sides_of[part]]
-            return remote(to, to, g4send.at[0, part], g4recv.at[d, part], {"dp": d})
-
-        keep = [pltpu.make_async_copy(fin_v.at[:, sides_of[part]], all_ref.at[rows_of(mine), sides_of[part]], load_sem.at[part]) for part in range(2)]
-
-        def fourth(part):
-            every_other(lambda s: g3_from(s, part).wait_recv())
-            for j in range(1, xs):
-                g4(None, j, lax.rem(x + j, xs) * 2 + c, part).start()
-            g4(None, 0, x * 2 + 1 - c, part).start()
-            keep[part].start()
+
+        def weights(s, _):
+            @pl.when(s + 1 < chunks)
+            def _():
+                norm_in(s + 1).start()
+
+            norm_in(s).wait()
+            n_all = norm_v[s % 2].reshape(chunks * tokens, norm_v.shape[-1])
+            got = lax.dot_general(n_all, gc_ref[...].reshape(chunks * tokens, width), (((0,), (0,)), ((), ())), preferred_element_type=F32)
+            gin_v[s] = got.astype(BF16).reshape(gin_v.shape[1:])
+            return 0
+
+        lax.fori_loop(0, chunks, weights, 0)
+        trade.begin()
 
     for i in range(min(2, zs) if split else 0, zs):
         outgoing(i)
+    if split:
+        trade.chip()
     every_copy(lambda d: late_to(d).start())
 
     def arrived(i, j, h):
@@ -1056,11 +1179,9 @@
             def _():
                 sink(t, h).start()
         if split and i == 0:
-            third(0)
-            third(1)
+            trade.spread()
         if split and i == min(1, zs - 1):
-            fourth(0)
-            fourth(1)
+            trade.share()
         if i + ahead < zs:
             for j in range(1, ys):
                 for h in range(2):
@@ -1073,15 +1194,8 @@
         total = total + late_v[lax.rem(mine + k, copies)].astype(F32)
     sum_ref[...] = total
     if split:
-        for part in range(2):
-            for j in range(1, xs):
-                d = lax.rem(x + j, xs) * 2 + c
-                g4_from(d, part).wait_recv()
-                g4(d, xs - 1 + j, x * 2 + 1 - c, part).start()
-        for part in range(2):
-            keep[part].wait()
-            for j in range(xs):
-                g4_from(lax.rem(x + j, xs) * 2 + 1 - c, part).wait_recv()
+        trade.pass_on()
+        trade.finish()
 
     every_copy(lambda d: late_to(d).wait_send())
     count = zs * (ys - 1)
@@ -1100,22 +1214,9 @@
             @pl.when(t < z)
             def _():
                 sink(t, h).wait_send()
-    if split:
-        for part in range(2):
-            for q in range(xs):
-                g1(q, part).wait_send()
-
-                @pl.when(q != x)
-                def _():
-                    g2(q, part).wait_send()
-            every_other(lambda s: g3(s, part).wait_send())
-            for j in range(xs):
-                g4(None, j, mine, part).wait_send()
-            for j in range(1, xs):
-                g4(lax.rem(x + j, xs) * 2 + c, xs - 1 + j, mine, part).wait_send()
-
-
-def scatter_sums(gc, gg, w_all, late, ginc, ging, chunks, copies, split):
+
+
+def scatter_sums(gc, gg, w_all, late, normed, chunks, copies, split):
     tokens, width = gc.shape[1:]
     model = w_all.shape[0]
     zs, ys = grid_of(chunks, copies)
@@ -1133,17 +1234,16 @@
     scratch = [pltpu.VMEM((slots, tokens, model), BF16), pltpu.VMEM((others, tokens, model), BF16),
                pltpu.VMEM((zs, tokens, model), BF16), pltpu.VMEM((zs + 1, tokens, model), BF16), pltpu.VMEM((tokens // 2, model), BF16),
                pltpu.VMEM((copies,) + late.shape, BF16), pltpu.VMEM(w_all.shape, BF16)]
-    sems = [dma((1 + 2 * xs,)), dma((others, 2)), dma((others, 2)), dma((zs, 2)), dma((zs, 2)), dma((zs + 1, 2)), dma((2,)), dma((copies,)), dma((copies,))]
+    sems = [dma((1,)), dma((others, 2)), dma((others, 2)), dma((zs, 2)), dma((zs, 2)), dma((zs + 1, 2)), dma((2,)), dma((copies,)), dma((copies,))]
     if split:
-        piece = ginc.shape[2]
-        slab = (xs, chunks, piece, 2 * width)
-        args += [ginc, ging]
-        in_specs += [any_spec] * 2
+        share = model // chunks
+        piece = share // copies
+        args.append(normed)
+        in_specs.append(any_spec)
         out_specs.append(any_spec)
-        out_shape.append(sds((copies * piece, 2 * chunks * width), BF16))
-        scratch += [pltpu.VMEM(slab, BF16), pltpu.VMEM(slab, BF16), pltpu.VMEM(slab, BF16), pltpu.VMEM(slab[1:], BF16),
-                    pltpu.VMEM((piece, 2 * chunks * width), BF16)]
-        sems += [dma((xs, 2)), dma((xs, 2)), dma((xs, 2)), dma((xs, 2)), dma((chunks, 2)), dma((chunks, 2)), dma((2 * xs, 2)), dma((copies, 2))]
+        out_shape.append(sds((share, chunks * width), BF16))
+        sems += [pltpu.VMEM((chunks, copies, piece, width), BF16), pltpu.VMEM((2, chunks, tokens, share), BF16), dma((2,))]
+        sems += exchange_scratch(chunks, copies, piece, width)
     return pl.pallas_call(
         functools.partial(scatter_kernel, chunks=chunks, copies=copies, split=split),
         in_specs=in_specs,
@@ -1153,26 +1253,32 @@
         compiler_params=pltpu.CompilerParams(collective_id=3, has_side_effects=True, vmem_limit_bytes=62 * 1024 * 1024),
         name="scatter_sums",
     )(*args)
-def backward_kernel(*refs, chunks, copies, n, inside, extra):
-    ins = 15 + (1 if inside else 0) + (1 if extra else 0)
-    (gg_ref, gact_ref, tail_ref, x_ref, dt_ref, slope_ref, start_ref, sel_ref, ci_ref, stepw_ref, decay_ref, skip_ref,
-     taps_ref, cbias_ref, selw_ref) = refs[:15]
-    mixed_ref = refs[15] if inside else None
+def backward_kernel(*refs, chunks, copies, n, inside, extra, split):
+    ins = 14 + (1 if inside else 0) + (1 if split else 0) + (1 if extra else 0)
+    (gg_ref, gact_ref, x_ref, dt_ref, slope_ref, start_ref, sel_ref, ci_ref, stepw_ref, decay_ref, skip_ref,
+     taps_ref, cbias_ref, selw_ref) = refs[:14]
+    mixed_ref = refs[14] if inside else None
+    gin_ref = refs[ins - 1 - extra] if split else None
     gout_ref = refs[ins - 1] if extra else None
-    outs = 9 + (1 if inside else 0) + (1 if extra else 0)
-    (ggate_ref, gci_ref, gstepw_ref, gsbias_ref, gdecay_ref, gskip_ref, gtaps_ref, gcbias_ref, gselw_ref) = refs[ins:ins + 9]
-    red_ref = refs[ins + 9] if inside else None
+    outs = 2 + (1 if inside else 0) + (1 if split else 0) + (1 if extra else 0)
+    gci_ref, late_ref = refs[ins:ins + 2]
+    red_ref = refs[ins + 2] if inside else None
+    all_ref = refs[ins + outs - 1 - extra] if split else None
     gsum_ref = refs[ins + outs - 1] if extra else None
     refs = refs[ins + outs:]
-    (gg_v, gact_v, tail_v, x_v, dt_v, slope_v, start_v, ggate_v, gci_v, gvals_v, part_v, recv_v, sel2_v,
+    (gg_v, gact_v, x_v, dt_v, slope_v, start_v, gci_v, gvals_v, part_v, recv_v, sel2_v,
      u_s, gy_s, gu_s, ah_s, bcoef_s, bt_s, hist_s, adj_a, harm_a, adj_b, harm_b, db_s, dc_s, carry_s, gd_s, rate_s, factor_s, kept_s,
-     ext_s, gext_s, in_sem, ggate_sem, gci_sem, send1, recv1, send2, recv2) = refs[:40]
-    refs = refs[40:]
+     gstepw_ref, gsbias_ref, gskip_ref, gtaps_ref, gcbias_ref, gselw_ref,
+     ext_s, gext_s, in_sem, gci_sem, send1, recv1, send2, recv2) = refs[:43]
+    refs = refs[43:]
     if inside:
         own_v, yrecv_v, zrecv_v, own_sem, ysend, yrecv, zup, zdown, zrecv = refs[:9]
         refs = refs[9:]
     if extra:
-        core_v, half_v, far_v, esend, erecv, asend, arecv, bsend, brecv = refs
+        core_v, half_v, far_v, esend, erecv, asend, arecv, bsend, brecv = refs[:9]
+        refs = refs[9:]
+    if split:
+        trade = Exchange(gin_ref, all_ref, refs[:5], refs[5:14], chunks, copies)
     zs, ys = grid_of(chunks, copies)
     xs = copies // 2
     me, mine = lax.axis_index("seq"), lax.axis_index("dp")
@@ -1185,7 +1291,7 @@
     def where_of(i):
         return chunks - 1 - i % chunks, i // chunks
 
-    streams = ((gg_ref, gg_v), (gact_ref, gact_v), (tail_ref, tail_v), (x_ref, x_v), (dt_ref, dt_v), (slope_ref, slope_v), (start_ref, start_v))
+    streams = ((gg_ref, gg_v), (gact_ref, gact_v), (x_ref, x_v), (dt_ref, dt_v), (slope_ref, slope_v), (start_ref, start_v))
 
     def fetch(i):
         c, r = where_of(i)
@@ -1201,6 +1307,9 @@
             one.start()
     meet(chunks, copies if extra else 1)
 
+    if split:
+        trade.begin()
+
     if inside:
         tables = order_of(zs)
 
@@ -1356,10 +1465,6 @@
         ref[...] = jnp.zeros_like(ref)
     rate_s[...] = -jnp.exp(decay_ref[...].astype(F32)) * LOG2E
 
-    def ggate_out(i):
-        c, r = where_of(i)
-        return pltpu.make_async_copy(ggate_v.at[i % 2], ggate_ref.at[c, r], ggate_sem.at[i % 2])
-
     def gci_out(i):
         c, r = where_of(i)
         return pltpu.make_async_copy(gci_v.at[i % 2], gci_ref.at[c, r], gci_sem.at[i % 2])
@@ -1373,17 +1478,12 @@
             for one in fetch(i + 1):
                 one.start()
 
-        @pl.when(i >= 2)
-        def _():
-            ggate_out(i - 2).wait()
-
         for one in fetch(i):
             one.wait()
-        back_step(sel_ref[c, r].astype(F32), x_v[slot].astype(F32), i % chunks == 0, gact_v.at[slot], gg_v.at[slot], tail_v.at[slot],
+        back_step(sel_ref[c, r].astype(F32), x_v[slot].astype(F32), i % chunks == 0, gact_v.at[slot], gg_v.at[slot],
                   start_v.at[slot], dt_v.at[slot], slope_v.at[slot], stepw_ref, skip_ref,
-                  ggate_v.at[slot], gvals_v.at[c, r], part_v.at[c, r], gstepw_ref, gsbias_ref, gskip_ref,
+                  gvals_v.at[c, r], part_v.at[c, r], gstepw_ref, gsbias_ref, gskip_ref,
                   u_s, gy_s, gu_s, ah_s, bcoef_s, bt_s, hist_s, adj_a, harm_a, adj_b, harm_b, db_s, dc_s, carry_s, gd_s, rate_s, factor_s, kept_s, rank, n)
-        ggate_out(i).start()
         late = min(3, chunks - 1)
 
         @pl.when((i % chunks == chunks - 1) & (r + 1 < rows))
@@ -1394,6 +1494,10 @@
         def _():
             sum_row(r - 1)
 
+        if split:
+            pl.when(i == 1)(trade.chip)
+            pl.when(i == 5)(trade.spread)
+            pl.when(i == 14)(trade.share)
         if extra:
             pl.when(i == 2)(chip_sum)
             pl.when(i == 8)(whole_sum)
@@ -1414,9 +1518,6 @@
 
     lax.fori_loop(0, count, scan, 0)
     send_row(rows - 1)
-    gdecay_ref[...] = gd_s[...] * rate_s[...] * (1.0 / LOG2E)
-    for i in range(max(0, count - 2), count):
-        ggate_out(i).wait()
 
     def conv(i, _):
         c, r = where_of(i)
@@ -1437,10 +1538,20 @@
     if inside:
         settle(zs - 1)
         red_ref[...] = own_v[z]
+    if split:
+        trade.pass_on()
     every_other(lambda s: landed_second(s, rows - 1).wait_recv())
     lax.fori_loop(count - chunks, count, conv, 0)
+    picked, taps = gselw_ref.shape[0], gtaps_ref.shape[0]
+    late_ref[0:picked, :] = gselw_ref[...].astype(BF16)
+    late_ref[picked:picked + rank, :] = gstepw_ref[...].astype(BF16)
+    late_ref[picked + rank:picked + rank + n, :] = (gd_s[...] * rate_s[...] * (1.0 / LOG2E)).astype(BF16)
+    filler = jnp.zeros((13 - taps, gtaps_ref.shape[1]), F32)
+    late_ref[picked + rank + n:, :] = jnp.concatenate([gtaps_ref[...], gsbias_ref[...], gskip_ref[...], gcbias_ref[...], filler], axis=0).astype(BF16)
     for i in range(max(0, count - 2), count):
         gci_out(i).wait()
+    if split:
+        trade.finish()
     for r in range(rows):
         every_other(lambda s: first(s, r).wait_send())
         every_other(lambda s: second(s, r).wait_send())
@@ -1465,7 +1576,7 @@
                     sink(t, h).wait_send()
 
 
-def backward(gg, gact, tail, x, dt, slope, starts, sel, ci, stepw, decay, skip, taps, cbias, selw, mixed, gout, copies, n):
+def backward(gg, gact, x, dt, slope, starts, sel, ci, stepw, decay, skip, taps, cbias, selw, mixed, ging, gout, copies, n):
     chunks, rows, length, width = ci.shape
     rank = stepw.shape[0]
     zs, ys = grid_of(chunks, copies)
@@ -1473,19 +1584,19 @@
     wide = BLOCK * n
     inside = mixed is not None
     extra = copies % 2 == 0
+    split = ging is not None
     sds = jax.ShapeDtypeStruct
     dma = pltpu.SemaphoreType.DMA
     vmem = pl.BlockSpec(memory_space=pltpu.VMEM)
     hbm = pl.BlockSpec(memory_space=pl.ANY)
-    args = [gg, gact, tail, x, dt, slope, starts, sel, ci, stepw, decay, skip, taps, cbias, selw]
-    in_specs = [hbm] * 7 + [vmem] * 8
-    out_specs = [hbm] * 2 + [vmem] * 7
-    out_shape = [sds(ci.shape, BF16), sds(ci.shape, BF16), sds((rank, width), F32), sds((1, width), F32), sds((n, width), F32), sds((1, width), F32),
-                 sds(taps.shape, F32), sds((1, width), F32), sds(selw.shape, F32)]
+    args = [gg, gact, x, dt, slope, starts, sel, ci, stepw, decay, skip, taps, cbias, selw]
+    in_specs = [hbm] * 6 + [vmem] * 8
+    out_specs = [hbm, vmem]
+    out_shape = [sds(ci.shape, BF16), sds((selw.shape[0] + rank + n + 16, width), BF16)]
     tile, coef = (length, width), sel.shape
-    scratch = [pltpu.VMEM((2,) + tile, F32), pltpu.VMEM((2,) + tile, F32), pltpu.VMEM((2,) + tile, BF16), pltpu.VMEM((2,) + tile, BF16),
+    scratch = [pltpu.VMEM((2,) + tile, F32), pltpu.VMEM((2,) + tile, F32), pltpu.VMEM((2,) + tile, BF16),
                pltpu.VMEM((2,) + tile, F32), pltpu.VMEM((2,) + tile, F32), pltpu.VMEM((2, n, width), F32),
-               pltpu.VMEM((2,) + tile, BF16), pltpu.VMEM((2,) + tile, BF16), pltpu.VMEM(ci.shape, F32),
+               pltpu.VMEM((2,) + tile, BF16), pltpu.VMEM(ci.shape, F32),
                pltpu.VMEM(coef, BF16), pltpu.VMEM(coef, BF16), pltpu.VMEM(coef, BF16),
                pltpu.VMEM(tile, F32), pltpu.VMEM(tile, F32), pltpu.VMEM(tile, F32), pltpu.VMEM(tile, F32),
                pltpu.VMEM((length, wide), BF16), pltpu.VMEM((2 * n, length), F32), pltpu.VMEM((length * n, width), BF16),
@@ -1493,8 +1604,10 @@
                pltpu.VMEM((length, wide), F32), pltpu.VMEM((length, wide), F32),
                pltpu.VMEM((n, width), F32), pltpu.VMEM((n, width), F32), pltpu.VMEM((n, width), F32),
                pltpu.VMEM((length * n, width), F32), pltpu.VMEM((length * n, width), F32),
+               pltpu.VMEM((rank, width), F32), pltpu.VMEM((1, width), F32), pltpu.VMEM((1, width), F32),
+               pltpu.VMEM(taps.shape, F32), pltpu.VMEM((1, width), F32), pltpu.VMEM(selw.shape, F32),
                pltpu.VMEM((length + 8, width), F32), pltpu.VMEM((length + 8, width), F32),
-               dma((7, 2)), dma((2,)), dma((2,)), dma((chunks, rows)), dma((chunks, rows)), dma((chunks, rows)), dma((chunks, rows))]
+               dma((6, 2)), dma((2,)), dma((chunks, rows)), dma((chunks, rows)), dma((chunks, rows)), dma((chunks, rows))]
     if inside:
         tokens, model = mixed.shape[1:]
         args.append(mixed)
@@ -1503,6 +1616,11 @@
         out_shape.append(sds((tokens, model), BF16))
         scratch += [pltpu.VMEM((zs, tokens, model), BF16), pltpu.VMEM((zs, tokens, model), BF16), pltpu.VMEM((zs + 1, tokens, model), BF16),
                     dma((zs,)), dma((zs, 2)), dma((zs, 2)), dma((zs, 2)), dma((zs, 2)), dma((zs + 1, 2))]
+    if split:
+        args.append(ging)
+        in_specs.append(hbm)
+        out_specs.append(hbm)
+        out_shape.append(sds((copies * ging.shape[2], chunks * width), BF16))
     if extra:
         args.append(gout)
         in_specs.append(vmem)
@@ -1511,8 +1629,10 @@
         part = (gout.shape[0] // 2, gout.shape[1])
         scratch += [pltpu.VMEM(part, BF16), pltpu.VMEM(part, BF16), pltpu.VMEM((xs,) + part, BF16),
                     dma(()), dma(()), dma((xs,)), dma((xs,)), dma(()), dma(())]
+    if split:
+        scratch += exchange_scratch(chunks, copies, ging.shape[2], width)
     return pl.pallas_call(
-        functools.partial(backward_kernel, chunks=chunks, copies=copies, n=n, inside=inside, extra=extra),
+        functools.partial(backward_kernel, chunks=chunks, copies=copies, n=n, inside=inside, extra=extra, split=split),
         in_specs=in_specs,
         out_specs=out_specs,
         out_shape=out_shape,
@@ -1549,37 +1669,33 @@
     bias_row = conv_bias.reshape(1, width)
     step_row = step_bias.reshape(1, width)
     skip_row = skip_weight.reshape(1, width)
-    gm, sel, x, gated, gact, tail, dt, slope, starts = forward(
+    gm, sel, x, gated, gact, dt, slope, starts, mixed, gg, ggate = forward(
         ci, gate, cotangent.astype(BF16).reshape(rows * length, model), conv_weight, bias_row, select_weight,
-        step_weight, step_row, decay_log, skip_row, copies, n)
+        step_weight, step_row, decay_log, skip_row, output_weight, copies, n)
     gm = gm.reshape(tokens, model)
     gated2 = gated.reshape(tokens, width)
-    mixed = shaped(jnp.dot(gated2, output_weight, preferred_element_type=F32).astype(BF16))
+    ggate = ggate.reshape(tokens, width)
     zs, ys = grid_of(chunks, copies)
     inside = ys == 2 and zs == 4
     source = hidden.astype(F32)
-    gg = shaped(lax.dot_general(gm, output_weight, (((1,), (1,)), ((), ())), preferred_element_type=F32))
     tn = lambda a, b: lax.dot_general(a, b, (((0,), (0,)), ((), ())), preferred_element_type=F32)
+    blocks = lambda g: tn(normed, g).astype(BF16).reshape(chunks, copies, share // copies, width)
+    ging = blocks(ggate)
     gout = tn(gated2, gm).astype(BF16)
     flat = lambda a: a.reshape(chunks, rows * length, a.shape[-1])
-    got = backward(gg, gact, tail, x, dt, slope, starts, sel, ci, step_weight, decay_log, skip_row, conv_weight, bias_row, select_weight,
-                   flat(mixed) if inside else None, gout, copies, n)
-    ggate, gci, gstepw, gstepb, gdecay, gskip, gtaps, gconvb, gselw = got[:9]
-    mixed = got[9].reshape(rows, length, model) if inside else lax.psum_scatter(mixed, "seq", scatter_dimension=0, tiled=False)
+    got = backward(gg, gact, x, dt, slope, starts, sel, ci, step_weight, decay_log, skip_row, conv_weight, bias_row, select_weight,
+                   mixed if inside else None, ging if split else None, gout, copies, n)
+    gci, late = got[:2]
+    mixed = got[2].reshape(rows, length, model) if inside else lax.psum_scatter(shaped(mixed), "seq", scatter_dimension=0, tiled=False)
     gout = got[-1].astype(F32)
     output = ((source + mixed.astype(F32)) * valid).astype(BF16)
-    tap_count = gtaps.shape[0]
-    gci2 = gci.reshape(tokens, width)
-    ggate2 = ggate.reshape(tokens, width)
-    ginc, ging = (tn(normed, g).astype(BF16).reshape(chunks, copies, share // copies, width) for g in (gci2, ggate2))
-    late = jnp.concatenate([gselw, gstepw, gdecay, gtaps, gstepb, gskip, gconvb], axis=0).astype(BF16)
-    late = jnp.pad(late, ((0, -late.shape[0] % 16), (0, 0)))
-    got = scatter_sums(flat(gci), flat(ggate), w_all, late, ginc, ging, chunks, copies, split)
-    scaled, late = got[:2]
+    tap_count = conv_weight.shape[0]
+    done = scatter_sums(flat(gci), ggate.reshape(chunks, rows * length, width), w_all, late, flat(shaped(normed)), chunks, copies, split)
+    scaled, late = done[:2]
     if split:
-        gin = got[2].astype(F32)
+        gin = jnp.concatenate([done[2], got[-2]], axis=1).astype(F32)
     else:
-        gin = jnp.stack([ginc, ging], axis=3)
+        gin = jnp.stack([blocks(gci.reshape(tokens, width)), ging], axis=3)
         gin = lax.psum_scatter(gin, "dp", scatter_dimension=1, tiled=False)
         gin = lax.all_to_all(gin, "seq", split_axis=0, concat_axis=2, tiled=False)
         gin = lax.all_gather(gin.reshape(share // copies, 2 * chunks * width), "dp", axis=0, tiled=True).astype(F32)
@@ -1587,7 +1703,7 @@
     scaled = scaled.reshape(rows, length, model).astype(F32) * gain_row
     inverse = lax.rsqrt(jnp.mean(source * source, axis=-1, keepdims=True) + EPSILON)
     ghidden = inverse * scaled - source * inverse ** 3 * jnp.mean(scaled * source, axis=-1, keepdims=True) + cotangent
-    sizes = (gselw.shape[0], rank, n, tap_count)
+    sizes = (select_weight.shape[0], rank, n, tap_count)
     ends = [sum(sizes[:k + 1]) for k in range(len(sizes))]
     gselw, gstepw, gdecay, gtaps = (late[e - k:e] for e, k in zip(ends, sizes))
     gstepb, gskip, gconvb = (late[ends[-1] + k] for k in range(3))

time: 598 us -> 572 us (0.957)
  matrix products: 42 us -> 15.8 us
  Pallas kernels: 511 us -> 520 us
  other arithmetic: 22.5 us -> 16.3 us
    pallas_call x1, Pallas kernels: 116 us -> 147 us  [forward(): pl.pallas_call(functools.partial(forward_kernel, chunks=chunks, copies=co...]
    pallas_call x1, Pallas kernels: 139 us -> 116 us  [gather_project(): pl.pallas_call(functools.partial(gather_project_kernel, chunks=chunks, co...]
    dot_general x3 -> x2, matrix products: 29.1 us -> 15.8 us  [local(): lax.dot_general(a, b, (((0,), (0,)), ((), ())), preferred_element_type=F32)]
    dot_general x2 -> x0, matrix products: 12.9 us -> none  [the longest x1 6.73 us: local(): jnp.dot(gated2, output_weight, preferred_element_type=F32).astype(BF16)]
    pallas_call x1, Pallas kernels: 142 us -> 149 us  [backward(): pl.pallas_call(functools.partial(backward_kernel, chunks=chunks, copies=c...]
where the time goes in v5:
time: 572 us; the launch traced here: 566 us
  Pallas kernels  520 us (91%)
  other arithmetic  16.3 us (3%)
  matrix products  15.8 us (3%)
  local copies, waits for them, and re-layouts  13 us (2%)
    pallas_call x1, Pallas kernels, backward(): pl.pallas_call(functools.partial(backward_kernel, chunks=chunks, copies=c...  149 us
    pallas_call x1, Pallas kernels, forward(): pl.pallas_call(functools.partial(forward_kernel, chunks=chunks, copies=co...  147 us
    pallas_call x1, Pallas kernels, gather_project(): pl.pallas_call(functools.partial(gather_project_kernel, chunks=chunks, co...  116 us
    pallas_call x1, Pallas kernels, scatter_sums(): pl.pallas_call(functools.partial(scatter_kernel, chunks=chunks, copies=co...  109 us
    dot_general x2, matrix products, local(): lax.dot_general(a, b, (((0,), (0,)), ((), ())), preferred_element_type=F32)  15.8 us

profile of v5, /device:TPU:0, one launch (start us, length us, event | category | flops | bytes accessed | tf_op | source)
XLA Modules:
  0.0 566.4 jit_solution(5371426053182437956)
XLA Ops:
  0.7 0.7 compare_convert_fusion
  1.4 1.2 convert_element_type.51
  2.6 1.3 reshape.122.cbias_ref.refs_12_
  3.9 1.3 reshape.124.skip_ref.refs_10_
  5.1 1.3 reshape.123.sbias_ref
  6.4 2.4 fusion.8
  8.8 115.8 %gather_project.1 = (bf16[8,256,2048]{2,1,0:T(8,128)(2,1)}, bf16[8,256,512]{2,1,0:T(8,128)(2,1)}, f32[8,256,512]{2,1,0:T(8,128)}, bf16[2048,1024]{1,0:T(8,128)(2,1)}, f32[1,2048]{1,0:T(1,128)}) custom-call(bf16[256,2048]{1,0:T(8,128)(2,1)} %bitcast.25, bf16[256,8192]{1,0:T(8,128)(2,1)} %wq_ref.1, f32[1,256]{1,0:T(1,128)} %bitcast.42), custom_call_target="tpu_custom_call" | custom-call | tf_op jit(solution)/shard_map/gather_project/pallas_call | solution.py:559
  124.6 146.8 %forward.1 = (bf16[8,256,2048]{2,1,0:T(8,128)(2,1)}, bf16[8,2,160,128]{3,2,1,0:T(8,128)(2,1)}, bf16[8,2,128,512]{3,2,1,0:T(8,128)(2,1)}, bf16[8,2,128,512]{3,2,1...) custom-call(bf16[8,2,128,512]{3,2,1,0:T(8,128)(2,1)} %bitcast.27, ...), custom_call_target="tpu_custom_call" | custom-call | tf_op jit(solution)/shard_map/forward/pallas_call | solution.py:838
  271.4 10.0 %convolution_convert_fusion.refs_16_ = bf16[512,2048]{1,0:T(8,128)(2,1)} fusion(bf16[2048,512]{1,0:T(8,128)(2,1)} %bitcast.44, bf16[2048,2048]{1,0:T(8,128)(2,1)} %bitcast.43), kind=kOutput, calls=%fused_computation.6 | convolution fusion | flops 4296015872 | bytes 12582912 | tf_op jit(solution)/shard_map/dot_general | solution.py:1681
  281.5 5.7 %convolution_convert_fusion.1 = bf16[2048,512]{1,0:T(8,128)(2,1)} fusion(bf16[2048,2048]{1,0:T(8,128)(2,1)S(1)} %bitcast.26, bf16[2048,512]{1,0:T(8,128)(2,1)S(1)} %bitcast.33), kind=kOutput, calls=%fused_computation.7 | convolution fusion | flops 4296015872 | bytes 12582912 | tf_op jit(solution)/shard_map/dot_general | solution.py:1681
  287.2 148.7 %backward.1 = (bf16[8,2,128,512]{3,2,1,0:T(8,128)(2,1)}, bf16[320,512]{1,0:T(8,128)(2,1)}, bf16[256,2048]{1,0:T(8,128)(2,1)}, bf16[256,4096]{1,0:T(8,128)(2,1)}, bf16[512,2048]{1,0:T(8,128)(2,1)}) custom-call(f32[8,2,128,512]{3,2,1,0:T(8,128)} %get-tuple-element.38.refs_0_, f32[8,2,128,512]{3,2,1,0:T(8,128)} %get-tuple-element.39.refs_1_, ...), custom_call_target="tpu_custom_call" | custom-call | tf_op jit(solution)/shard_map/backward/pallas_call | solution.py:1634
  435.9 0.0 copy-start.1
  435.9 109.2 %scatter_sums.1 = (bf16[256,2048]{1,0:T(8,128)(2,1)}, f32[320,512]{1,0:T(8,128)}, bf16[256,4096]{1,0:T(8,128)(2,1)}) custom-call(bf16[8,256,512]{2,1,0:T(8,128)(2,1)} %bitcast.34, bf16[8,256,512]{2,1,0:T(8,128)(2,1)} %bitcast.32, bf16[2048,1024]{1,0:T(8,128)(2,1)} %get-tuple-element.52.refs_2_, bf16[320,512]{1,0:T(8,128)(2,1)} %get-tuple-element.53.refs_3_, ...), custom_call_target="tpu_custom_call" | custom-call | tf_op jit(solution)/shard_map/scatter_sums/pallas_call | solution.py:1247
  545.1 0.0 copy-start.4
  545.2 0.0 copy-start.9
  545.2 0.0 copy-done.1
  545.2 0.0 copy-done.10
  545.2 1.9 fusion.2
  547.1 1.4 fusion.9
  548.6 1.3 slice.21
  549.9 1.4 slice.26
  551.3 1.7 slice.24
  552.9 1.7 slice.23
  554.7 0.0 copy-done.3
  554.7 0.0 copy-done.9
  554.7 2.8 fusion.5
  557.5 2.7 convert_element_type.64
  560.2 0.0 copy-done.7
  560.2 1.0 copy-done
  561.2 0.7 copy-done.5
  561.9 4.0 multiply_reduce_fusion
  565.8 0.6 convert_divide_fusion
  (16 shorter events, 0.0 us)
Async XLA Ops:
  271.4 10.1 %copy-start.2 = (bf16[8,256,2048]{2,1,0:T(8,128)(2,1)S(1)}, bf16[8,256,2048]{2,1,0:T(8,128)(2,1)}, u32[]{:S(2)}) copy-start(bf16[8,256,2048]{2,1,0:T(8,128)(2,1)} %get-tuple-element.46.refs_4_) | copy-start | bytes 25165828
  271.4 10.1 %copy-start.8 = (bf16[8,2,128,512]{3,2,1,0:T(8,128)(2,1)S(1)}, bf16[8,2,128,512]{3,2,1,0:T(8,128)(2,1)}, u32[]{:S(2)}) copy-start(bf16[8,2,128,512]{3,2,1,0:T(8,128)(2,1)} %get-tuple-element.47) | copy-start | bytes 6291460
  435.9 109.3 %copy-start.1 = (bf16[2,128,2048]{2,1,0:T(8,128)(2,1)S(1)}, bf16[2,128,2048]{2,1,0:T(8,128)(2,1)}, u32[]{:S(2)}) copy-start(bf16[2,128,2048]{2,1,0:T(8,128)(2,1)} %param.13) | copy-start | bytes 3145732
  435.9 109.3 %copy-start.10 = (f32[1,2048]{1,0:T(1,128)S(1)}, f32[1,2048]{1,0:T(1,128)}, u32[]{:S(2)}) copy-start(f32[1,2048]{1,0:T(1,128)} %get-tuple-element.55) | copy-start | bytes 24580
  545.1 9.5 %copy-start.3 = (bf16[256,2048]{1,0:T(8,128)(2,1)S(1)}, bf16[256,2048]{1,0:T(8,128)(2,1)}, u32[]{:S(2)}) copy-start(bf16[256,2048]{1,0:T(8,128)(2,1)} %get-tuple-element.54) | copy-start | bytes 3145732
  545.1 9.5 %copy-start.4 = (bf16[2,128,2048]{2,1,0:T(8,128)(2,1)S(1)}, bf16[2,128,2048]{2,1,0:T(8,128)(2,1)}, u32[]{:S(2)}) copy-start(bf16[2,128,2048]{2,1,0:T(8,128)(2,1)} %param.14) | copy-start | bytes 3145732
  545.2 9.5 %copy-start.9 = (bf16[256,2048]{1,0:T(8,128)(2,1)S(1)}, bf16[256,2048]{1,0:T(8,128)(2,1)}, u32[]{:S(2)}) copy-start(bf16[256,2048]{1,0:T(8,128)(2,1)} %get-tuple-element.50) | copy-start | bytes 3145732
  554.7 2.8 copy-start.6
  554.7 5.5 copy-start.7
  557.5 3.7 copy-start
  557.5 4.4 copy-start.5
  561.9 4.0 copy-start.11

commit v6 on v5

--- a/solution.py
+++ b/solution.py
@@ -574,15 +574,15 @@
     )(hidden, wq, gain)
 
 
-SPLIT = 9
+SPLITS = (8, 14)
 
 
 def forward_kernel(ci_ref, gate_ref, gm_ref, taps_ref, cbias_ref, selw_ref, stepw_ref, sbias_ref, decay_ref, skip_ref, wout_ref,
-                   gmall_ref, sel_ref, x_ref, gated_ref, gact_ref, dt_ref, slope_ref, start_ref, mixed_ref, gg_ref, ggate_ref,
+                   gmall_ref, sel_ref, x_ref, gated_ref, gact_ref, tail_ref, dt_ref, slope_ref, start_ref, mixed_ref,
                    gate_v, part_v, recv_v, x_v, gated_v, gact_v, tail_v, dt_v, slope_v, start_v,
-                   gm_v, mixed_v, gg_v, ggate_v,
+                   mixed_v,
                    ext_s, u_s, y_s, coef_s, bt_s, hist_a, hist_b, state_s, rate_s,
-                   load_sem, own_sem, out_sem, gm_sem, mixed_sem, gg_sem, grecv, gside, gup, gdown, glend, send1, recv1, send2, recv2, *, chunks, copies, n):
+                   load_sem, own_sem, out_sem, mixed_sem, grecv, gside, gup, gdown, glend, send1, recv1, send2, recv2, *, chunks, copies, n):
     zs, ys = grid_of(chunks, copies)
     me = lax.axis_index("seq")
     z, y = me // ys, me % ys
@@ -666,21 +666,17 @@
         part_v[c, r] = part
         return 0
 
-    lax.fori_loop(0, rows * chunks, conv, 0)
-    x_out = pltpu.make_async_copy(x_v, x_ref, out_sem.at[0, 0])
-    x_out.start()
-
-    def first(s):
-        return remote(part_v.at[s], recv_v.at[me], send1.at[s], recv1.at[me], {"seq": s})
-
-    def landed_first(s):
-        return remote(part_v.at[s], recv_v.at[s], send1.at[s], recv1.at[s], {"seq": s})
-
-    def second(s):
-        return remote(sel_ref.at[me], sel_ref.at[me], send2.at[s], recv2.at[me], {"seq": s})
-
-    def landed_second(s):
-        return remote(sel_ref.at[s], sel_ref.at[s], send2.at[s], recv2.at[s], {"seq": s})
+    def first(s, r):
+        return remote(part_v.at[s, r], recv_v.at[me, r], send1.at[s, r], recv1.at[me, r], {"seq": s})
+
+    def landed_first(s, r):
+        return remote(part_v.at[s, r], recv_v.at[s, r], send1.at[s, r], recv1.at[s, r], {"seq": s})
+
+    def second(s, r):
+        return remote(sel_ref.at[me, r], sel_ref.at[me, r], send2.at[s, r], recv2.at[me, r], {"seq": s})
+
+    def landed_second(s, r):
+        return remote(sel_ref.at[s, r], sel_ref.at[s, r], send2.at[s, r], recv2.at[s, r], {"seq": s})
 
     def every_other(fn):
         def one(k, _):
@@ -688,28 +684,38 @@
             return 0
         lax.fori_loop(1, chunks, one, 0)
 
-    every_other(lambda s: first(s).start())
-    first_sends(1)
-    recv_v[me] = part_v[me]
-    every_other(lambda s: landed_first(s).wait_recv())
-    total = recv_v[0].astype(F32)
-    for s in range(1, chunks):
-        total = total + recv_v[s].astype(F32)
-    sel_ref[me] = total.astype(BF16)
-    every_other(lambda s: second(s).start())
+    for r in range(rows):
+        lax.fori_loop(r * chunks, (r + 1) * chunks, conv, 0)
+        every_other(lambda s: first(s, r).start())
+        recv_v[me, r] = part_v[me, r]
+        if r == 0:
+            first_sends(1)
+    x_out = pltpu.make_async_copy(x_v, x_ref, out_sem.at[0, 0])
+    x_out.start()
+    for r in range(rows):
+        every_other(lambda s: landed_first(s, r).wait_recv())
+        total = recv_v[0, r].astype(F32)
+        for s in range(1, chunks):
+            total = total + recv_v[s, r].astype(F32)
+        sel_ref[me, r] = total.astype(BF16)
+        every_other(lambda s: second(s, r).start())
     if zs > 1:
         relay(1)
     if zs <= 2:
         lend_on()
-    every_other(lambda s: landed_second(s).wait_recv())
     load.wait()
-    pairs = ((gated_v, gated_ref), (gact_v, gact_ref), (dt_v, dt_ref), (slope_v, slope_ref), (start_v, start_ref))
+    pairs = ((gated_v, gated_ref), (gact_v, gact_ref), (tail_v, tail_ref), (dt_v, dt_ref), (slope_v, slope_ref), (start_v, start_ref))
 
     def outs(c, r):
         return [pltpu.make_async_copy(src.at[c, r], dst.at[c, r], out_sem.at[1 + k, c * rows + r]) for k, (src, dst) in enumerate(pairs)]
 
     def scan(i, _):
         r, c = i // chunks, i % chunks
+
+        @pl.when(c == 0)
+        def _():
+            every_other(lambda s: landed_second(s, r).wait_recv())
+
         start_v[c, r] = jnp.where(c == 0, 0.0, state_s[...])
         scan_step(sel_ref[c, r].astype(F32), x_v[c, r].astype(F32), gate_v[c, r], c == 0, stepw_ref, sbias_ref, skip_ref,
                   gated_v.at[c, r], gact_v.at[c, r], tail_v.at[c, r], dt_v.at[c, r], slope_v.at[c, r],
@@ -719,14 +725,13 @@
         return 0
 
     count = rows * chunks
-    if zs > 2:
-        relay(2)
-        lend_on()
-    cuts = [count * SPLIT // 16 + (count - count * SPLIT // 16) * k // max(1, zs - 3) for k in range(zs - 2)] if zs > 3 else []
     at = 0
-    for k, cut in enumerate(cuts[:-1]):
+    for k in range(2, zs):
+        cut = min(count, count * (SPLITS[k - 2] if zs == 4 else 16 * (k - 1) // zs) // 16)
         lax.fori_loop(at, cut, scan, 0)
-        relay(3 + k)
+        relay(k)
+        if k == 2:
+            lend_on()
         at = cut
     lax.fori_loop(at, count, scan, 0)
 
@@ -754,44 +759,17 @@
     for s in range(chunks - 2, chunks):
         mixed_out(s).wait()
 
-    own.wait()
-
-    def bring(s):
-        return pltpu.make_async_copy(gmall_ref.at[s], gm_v, gm_sem)
-
-    def back(s):
-        bring(s).start()
-        bring(s).wait()
-        got = nt_dot(gm_v[...], wout_ref[...])
-        gg_v[...] = got.reshape(gg_v.shape)
-        ggate_v[...] = (got * tail_v[s].reshape(tokens, width).astype(F32)).astype(BF16).reshape(ggate_v.shape)
-        one, two = pltpu.make_async_copy(gg_v, gg_ref.at[s], gg_sem.at[0]), pltpu.make_async_copy(ggate_v, ggate_ref.at[s], gg_sem.at[1])
-        one.start()
-        two.start()
-        one.wait()
-        two.wait()
-
-    last = [[k] + [q for q in range(zs) if q not in (k, k + 1 - 2 * (k % 2))] + [k + 1 - 2 * (k % 2)] for k in range(zs)] if even else [list(range(zs))] * zs
-
-    def others(i, _):
-        lower, k = i // zs, i % zs
-        o = 0
-        for p in range(zs):
-            for q in range(zs):
-                o = o + jnp.where((z == p) & (k == q), last[p][q], 0)
-
-        @pl.when(lower > 0)
-        def _():
-            landed(o, lax.rem(y + lower, ys), 0).wait_recv()
+    def others(o, _):
+        for j in range(1, ys):
+            landed(o, lax.rem(y + j, ys), 0).wait_recv()
             if even:
                 when(o != z, lambda: landed(o, 1 - y, 1).wait_recv())
             else:
-                landed(o, lax.rem(y + lower, ys), 1).wait_recv()
-
-        back(o * ys + lax.rem(y + lower, ys))
+                landed(o, lax.rem(y + j, ys), 1).wait_recv()
         return 0
 
-    lax.fori_loop(0, ys * zs, others, 0)
+    lax.fori_loop(0, zs, others, 0)
+    own.wait()
     x_out.wait()
 
     def settle(i, _):
@@ -800,8 +778,9 @@
         return 0
 
     lax.fori_loop(0, count, settle, 0)
-    every_other(lambda s: first(s).wait_send())
-    every_other(lambda s: second(s).wait_send())
+    for r in range(rows):
+        every_other(lambda s: first(s, r).wait_send())
+        every_other(lambda s: second(s, r).wait_send())
 
     def drain(k, _):
         for h in range(2):
@@ -838,18 +817,18 @@
     return pl.pallas_call(
         functools.partial(forward_kernel, chunks=chunks, copies=copies, n=n),
         in_specs=[vmem, hbm] + [vmem] * 9,
-        out_specs=[hbm, vmem] + [hbm] * 9,
-        out_shape=[sds((chunks, tokens, model), BF16), sds(coef, BF16), sds(full, BF16), sds(full, BF16), sds(full, F32),
-                   sds(full, F32), sds(full, F32), sds(starts, F32), sds((chunks, tokens, model), BF16), sds(full, F32), sds(full, BF16)],
+        out_specs=[hbm, vmem] + [hbm] * 8,
+        out_shape=[sds((chunks, tokens, model), BF16), sds(coef, BF16), sds(full, BF16), sds(full, BF16), sds(full, F32), sds(full, BF16),
+                   sds(full, F32), sds(full, F32), sds(starts, F32), sds((chunks, tokens, model), BF16)],
         scratch_shapes=[
             pltpu.VMEM(full, F32), pltpu.VMEM(coef, BF16), pltpu.VMEM(coef, BF16), pltpu.VMEM(full, BF16), pltpu.VMEM(full, BF16),
             pltpu.VMEM(full, F32), pltpu.VMEM(full, BF16), pltpu.VMEM(full, F32), pltpu.VMEM(full, F32), pltpu.VMEM(starts, F32),
-            pltpu.VMEM((tokens, model), BF16), pltpu.VMEM((2, tokens, model), BF16), pltpu.VMEM(full[1:], F32), pltpu.VMEM(full[1:], BF16),
+            pltpu.VMEM((2, tokens, model), BF16),
             pltpu.VMEM((length + 8, width), F32), pltpu.VMEM((length, width), F32), pltpu.VMEM((length, width), F32),
             pltpu.VMEM((length, wide), BF16), pltpu.VMEM((2 * n, length), F32), pltpu.VMEM((wide, width), BF16), pltpu.VMEM((wide, width), BF16),
             pltpu.VMEM((n, width), F32), pltpu.VMEM((n, width), F32),
-            dma(()), dma(()), dma((7, rows * chunks)), dma(()), dma((2,)), dma((2,)), dma((chunks, 2)), dma((zs, max(1, ys - 1), 2)), dma((zs, 2)), dma((zs, 2)), dma(()),
-            dma((chunks,)), dma((chunks,)), dma((chunks,)), dma((chunks,)),
+            dma(()), dma(()), dma((7, rows * chunks)), dma((2,)), dma((chunks, 2)), dma((zs, max(1, ys - 1), 2)), dma((zs, 2)), dma((zs, 2)), dma(()),
+            dma((chunks, rows)), dma((chunks, rows)), dma((chunks, rows)), dma((chunks, rows)),
         ],
         compiler_params=pltpu.CompilerParams(collective_id=1, has_side_effects=True, vmem_limit_bytes=60 * 1024 * 1024),
         name="forward",
@@ -1669,12 +1648,13 @@
     bias_row = conv_bias.reshape(1, width)
     step_row = step_bias.reshape(1, width)
     skip_row = skip_weight.reshape(1, width)
-    gm, sel, x, gated, gact, dt, slope, starts, mixed, gg, ggate = forward(
+    gm, sel, x, gated, gact, tail, dt, slope, starts, mixed = forward(
         ci, gate, cotangent.astype(BF16).reshape(rows * length, model), conv_weight, bias_row, select_weight,
         step_weight, step_row, decay_log, skip_row, output_weight, copies, n)
     gm = gm.reshape(tokens, model)
     gated2 = gated.reshape(tokens, width)
-    ggate = ggate.reshape(tokens, width)
+    gg = lax.dot_general(gm, output_weight, (((1,), (1,)), ((), ())), preferred_element_type=F32)
+    ggate = (gg * tail.reshape(tokens, width).astype(F32)).astype(BF16)
     zs, ys = grid_of(chunks, copies)
     inside = ys == 2 and zs == 4
     source = hidden.astype(F32)
@@ -1683,7 +1663,7 @@
     ging = blocks(ggate)
     gout = tn(gated2, gm).astype(BF16)
     flat = lambda a: a.reshape(chunks, rows * length, a.shape[-1])
-    got = backward(gg, gact, x, dt, slope, starts, sel, ci, step_weight, decay_log, skip_row, conv_weight, bias_row, select_weight,
+    got = backward(shaped(gg), gact, x, dt, slope, starts, sel, ci, step_weight, decay_log, skip_row, conv_weight, bias_row, select_weight,
                    mixed if inside else None, ging if split else None, gout, copies, n)
     gci, late = got[:2]
     mixed = got[2].reshape(rows, length, model) if inside else lax.psum_scatter(shaped(mixed), "seq", scatter_dimension=0, tiled=False)

time: 572 us -> 549 us (0.960)
  Pallas kernels: 520 us -> 490 us
  matrix products: 15.8 us -> 22.5 us
    pallas_call x1, Pallas kernels: 147 us -> 119 us  [forward(): pl.pallas_call(functools.partial(forward_kernel, chunks=chunks, copies=co...]
    dot_general x0 -> x1, matrix products: none -> 6.71 us  [local(): lax.dot_general(gm, output_weight, (((1,), (1,)), ((), ())), preferred_el...]
where the time goes in v6:
time: 549 us; the launch traced here: 543 us
  Pallas kernels  490 us (89%)
  matrix products  22.5 us (4%)
  other arithmetic  16.3 us (3%)
  local copies, waits for them, and re-layouts  13.1 us (2%)
    pallas_call x1, Pallas kernels, backward(): pl.pallas_call(functools.partial(backward_kernel, chunks=chunks, copies=c...  146 us
    pallas_call x1, Pallas kernels, forward(): pl.pallas_call(functools.partial(forward_kernel, chunks=chunks, copies=co...  119 us
    pallas_call x1, Pallas kernels, gather_project(): pl.pallas_call(functools.partial(gather_project_kernel, chunks=chunks, co...  116 us
    pallas_call x1, Pallas kernels, scatter_sums(): pl.pallas_call(functools.partial(scatter_kernel, chunks=chunks, copies=co...  110 us
    dot_general x2, matrix products, local(): lax.dot_general(a, b, (((0,), (0,)), ((), ())), preferred_element_type=F32)  15.8 us

profile of v6, /device:TPU:0, one launch (start us, length us, event | category | flops | bytes accessed | tf_op | source)
XLA Modules:
  0.0 543.1 jit_solution(3808877802165176477)
XLA Ops:
  0.7 0.7 compare_convert_fusion
  1.4 1.2 convert_element_type.60
  2.6 1.3 reshape.128.cbias_ref.refs_12_
  3.9 1.3 reshape.130.skip_ref.refs_10_
  5.1 1.3 reshape.129.sbias_ref
  6.4 2.4 fusion.9
  8.8 115.8 %gather_project.1 = (bf16[8,256,2048]{2,1,0:T(8,128)(2,1)}, bf16[8,256,512]{2,1,0:T(8,128)(2,1)}, f32[8,256,512]{2,1,0:T(8,128)}, bf16[2048,1024]{1,0:T(8,128)(2,1)}, f32[1,2048]{1,0:T(1,128)}) custom-call(bf16[256,2048]{1,0:T(8,128)(2,1)} %bitcast.30, bf16[256,8192]{1,0:T(8,128)(2,1)} %wq_ref.1, f32[1,256]{1,0:T(1,128)} %bitcast.49), custom_call_target="tpu_custom_call" | custom-call | tf_op jit(solution)/shard_map/gather_project/pallas_call | solution.py:559
  124.6 119.3 %forward.1 = (bf16[8,256,2048]{2,1,0:T(8,128)(2,1)}, bf16[8,2,160,128]{3,2,1,0:T(8,128)(2,1)}, bf16[8,2,128,512]{3,2,1,0:T(8,128)(2,1)}, bf16[8,2,128,512]{3,2,1...) custom-call(bf16[8,2,128,512]{3,2,1,0:T(8,128)(2,1)} %bitcast.34, ...), custom_call_target="tpu_custom_call" | custom-call | tf_op jit(solution)/shard_map/forward/pallas_call | solution.py:817
  244.0 0.0 copy-start.7
  244.0 0.0 slice-start
  244.0 10.0 %convolution_convert_fusion.refs_16_ = bf16[512,2048]{1,0:T(8,128)(2,1)} fusion(bf16[2048,512]{1,0:T(8,128)(2,1)} %bitcast.52, bf16[2048,2048]{1,0:T(8,128)(2,1)} %bitcast.50), kind=kOutput, calls=%fused_computation.8 | convolution fusion | flops 4296015872 | bytes 12582912 | tf_op jit(solution)/shard_map/dot_general | solution.py:1661
  254.1 0.0 copy-done.12
  254.1 0.0 slice-start.1
  254.1 6.7 %fusion = (bf16[2048,512]{1,0:T(8,128)(2,1)S(1)}, f32[2048,512]{1,0:T(8,128)}) fusion(bf16[8,2,128,512]{3,2,1,0:T(8,128)(2,1)S(1)} %copy-done.13, bf16[2048,2048]{1,0:T(8,128)(2,1)S(1)} %bitcast.51, bf16[512,2048]{1,0:T(8,128)(2,1)S(1)} %copy-done.7), kind=kOutput, calls=%fused_computation.3 | convolution fusion | flops 4298113024 | bytes 18874368 | tf_op jit(solution)/shard_map/dot_general | solution.py:1656
  260.8 0.0 slice-done
  260.8 5.7 %convolution_convert_fusion.1 = bf16[2048,512]{1,0:T(8,128)(2,1)} fusion(bf16[2048,2048]{1,0:T(8,128)(2,1)S(1)} %bitcast.33, bf16[2048,512]{1,0:T(8,128)(2,1)S(1)} %get-tuple-element.69), kind=kOutput, calls=%fused_computation.9 | convolution fusion | flops 4296015872 | bytes 12582912 | tf_op jit(solution)/shard_map/dot_general | solution.py:1661
  266.6 145.5 %backward.1 = (bf16[8,2,128,512]{3,2,1,0:T(8,128)(2,1)}, bf16[320,512]{1,0:T(8,128)(2,1)}, bf16[256,2048]{1,0:T(8,128)(2,1)}, bf16[256,4096]{1,0:T(8,128)(2,1)}, bf16[512,2048]{1,0:T(8,128)(2,1)}) custom-call(f32[8,2,128,512]{3,2,1,0:T(8,128)} %bitcast.39, f32[8,2,128,512]{3,2,1,0:T(8,128)} %get-tuple-element.38.refs_1_, ...), custom_call_target="tpu_custom_call" | custom-call | tf_op jit(solution)/shard_map/backward/pallas_call | solution.py:1613
  412.1 0.0 copy-start.1
  412.1 109.7 %scatter_sums.1 = (bf16[256,2048]{1,0:T(8,128)(2,1)}, f32[320,512]{1,0:T(8,128)}, bf16[256,4096]{1,0:T(8,128)(2,1)}) custom-call(bf16[8,256,512]{2,1,0:T(8,128)(2,1)} %bitcast.41, bf16[8,256,512]{2,1,0:T(8,128)(2,1)} %bitcast.40, bf16[2048,1024]{1,0:T(8,128)(2,1)} %get-tuple-element.50.refs_2_, bf16[320,512]{1,0:T(8,128)(2,1)} %get-tuple-element.51.refs_3_, ...), custom_call_target="tpu_custom_call" | custom-call | tf_op jit(solution)/shard_map/scatter_sums/pallas_call | solution.py:1226
  521.9 0.0 copy-start.3
  521.9 1.9 fusion.3
  523.9 1.4 fusion.10
  525.3 1.3 slice.21
  526.6 1.4 slice.26
  528.0 1.7 slice.24
  529.6 1.7 slice.23
  531.4 2.8 fusion.6
  534.2 2.7 convert_element_type.76
  536.9 1.0 copy-done
  537.9 0.7 copy-done.4
  538.6 4.0 multiply_reduce_fusion
  542.5 0.6 convert_divide_fusion
  (26 shorter events, 0.1 us)
Async XLA Ops:
  244.0 10.1 %copy-start.7 = (bf16[512,2048]{1,0:T(8,128)(2,1)S(1)}, bf16[512,2048]{1,0:T(8,128)(2,1)}, u32[]{:S(2)}) copy-start(bf16[512,2048]{1,0:T(8,128)(2,1)} %wout_ref.1) | copy-start | bytes 6291460
  244.0 10.1 %copy-start.12 = (bf16[8,256,2048]{2,1,0:T(8,128)(2,1)S(1)}, bf16[8,256,2048]{2,1,0:T(8,128)(2,1)}, u32[]{:S(2)}) copy-start(bf16[8,256,2048]{2,1,0:T(8,128)(2,1)} %get-tuple-element.37) | copy-start | bytes 25165828
  244.0 10.1 %copy-start.13 = (bf16[8,2,128,512]{3,2,1,0:T(8,128)(2,1)S(1)}, bf16[8,2,128,512]{3,2,1,0:T(8,128)(2,1)}, u32[]{:S(2)}) copy-start(bf16[8,2,128,512]{3,2,1,0:T(8,128)(2,1)} %get-tuple-element.46) | copy-start | bytes 6291460
  244.0 16.8 %slice-start = ((s8[8388608]{0:T(1024)(128)(4,1)}), s8[4194304]{0:T(1024)(128)(4,1)S(1)}, s32[]{:S(2)}) async-start(s8[8388608]{0:T(1024)(128)(4,1)} %bitcast.31), calls=%async_computation | async-start | bytes 8388608
  254.1 6.7 %slice-start.1 = ((s8[8388608]{0:T(1024)(128)(4,1)}), s8[4194304]{0:T(1024)(128)(4,1)S(1)}, s32[]{:S(2)}) async-start(s8[8388608]{0:T(1024)(128)(4,1)} %bitcast.31), calls=%async_computation.1 | async-start | bytes 8388608
  260.8 5.7 %copy-start.8 = (bf16[2048,512]{1,0:T(8,128)(2,1)}, bf16[2048,512]{1,0:T(8,128)(2,1)S(1)}, u32[]{:S(2)}) copy-start(bf16[2048,512]{1,0:T(8,128)(2,1)S(1)} %get-tuple-element.69) | copy-start | bytes 6291460
  412.1 109.8 %copy-start.1 = (bf16[2,128,2048]{2,1,0:T(8,128)(2,1)S(1)}, bf16[2,128,2048]{2,1,0:T(8,128)(2,1)}, u32[]{:S(2)}) copy-start(bf16[2,128,2048]{2,1,0:T(8,128)(2,1)} %param.13) | copy-start | bytes 3145732
  412.1 109.8 %copy-start.10 = (f32[1,2048]{1,0:T(1,128)S(1)}, f32[1,2048]{1,0:T(1,128)}, u32[]{:S(2)}) copy-start(f32[1,2048]{1,0:T(1,128)} %get-tuple-element.53) | copy-start | bytes 24580
  521.8 9.5 %copy-start.2 = (bf16[256,2048]{1,0:T(8,128)(2,1)S(1)}, bf16[256,2048]{1,0:T(8,128)(2,1)}, u32[]{:S(2)}) copy-start(bf16[256,2048]{1,0:T(8,128)(2,1)} %get-tuple-element.52) | copy-start | bytes 3145732
  521.9 9.5 %copy-start.3 = (bf16[2,128,2048]{2,1,0:T(8,128)(2,1)S(1)}, bf16[2,128,2048]{2,1,0:T(8,128)(2,1)}, u32[]{:S(2)}) copy-start(bf16[2,128,2048]{2,1,0:T(8,128)(2,1)} %param.14) | copy-start | bytes 3145732
  521.9 9.5 %copy-start.9 = (bf16[256,2048]{1,0:T(8,128)(2,1)S(1)}, bf16[256,2048]{1,0:T(8,128)(2,1)}, u32[]{:S(2)}) copy-start(bf16[256,2048]{1,0:T(8,128)(2,1)} %get-tuple-element.48) | copy-start | bytes 3145732
  531.4 2.8 copy-start.5
  531.4 5.5 %copy-start.6 = (bf16[256,4096]{1,0:T(8,128)(2,1)S(1)}, bf16[256,4096]{1,0:T(8,128)(2,1)}, u32[]{:S(2)}) copy-start(bf16[256,4096]{1,0:T(8,128)(2,1)} %get-tuple-element.54) | copy-start | bytes 6291460
  534.2 3.7 copy-start
  534.2 4.4 copy-start.4
  538.6 4.0 copy-start.11

commit v7 on v6

--- a/solution.py
+++ b/solution.py
@@ -1028,7 +1028,7 @@
         return remote(ysend_v.at[k % ysend_v.shape[0], rows], yrecv_v.at[k, rows], ysend.at[k, h], yrecv.at[k, h], {"seq": z * ys + lax.rem(y + j, ys)})
 
     slots = ysend_v.shape[0]
-    even = ys == 2 and zs % 2 == 0 and slots == zs
+    even = False
 
     def lend(i):
         return remote(ysend_v.at[i, pl.ds(half, half)], lend_v, lend_sem.at[0], lend_sem.at[1], {"seq": partner * ys + y})

time: 549 us -> 543 us (0.989)
  no operation moved by 1% of the time
where the time goes in v7:
time: 543 us; the launch traced here: 541 us
  Pallas kernels  489 us (90%)
  matrix products  22.5 us (4%)
  other arithmetic  16.3 us (3%)
  local copies, waits for them, and re-layouts  13.1 us (2%)
    pallas_call x1, Pallas kernels, backward(): pl.pallas_call(functools.partial(backward_kernel, chunks=chunks, copies=c...  146 us
    pallas_call x1, Pallas kernels, forward(): pl.pallas_call(functools.partial(forward_kernel, chunks=chunks, copies=co...  119 us
    pallas_call x1, Pallas kernels, gather_project(): pl.pallas_call(functools.partial(gather_project_kernel, chunks=chunks, co...  116 us
    pallas_call x1, Pallas kernels, scatter_sums(): pl.pallas_call(functools.partial(scatter_kernel, chunks=chunks, copies=co...  108 us
    dot_general x2, matrix products, local(): lax.dot_general(a, b, (((0,), (0,)), ((), ())), preferred_element_type=F32)  15.8 us

profile of v7, /device:TPU:0, one launch (start us, length us, event | category | flops | bytes accessed | tf_op | source)
XLA Modules:
  0.0 541.5 jit_solution(12964101026842608587)
XLA Ops:
  0.7 0.7 compare_convert_fusion
  1.4 1.2 convert_element_type.60
  2.6 1.3 reshape.128.cbias_ref.refs_12_
  3.9 1.3 reshape.130.skip_ref.refs_10_
  5.1 1.3 reshape.129.sbias_ref
  6.4 2.4 fusion.9
  8.8 115.8 %gather_project.1 = (bf16[8,256,2048]{2,1,0:T(8,128)(2,1)}, bf16[8,256,512]{2,1,0:T(8,128)(2,1)}, f32[8,256,512]{2,1,0:T(8,128)}, bf16[2048,1024]{1,0:T(8,128)(2,1)}, f32[1,2048]{1,0:T(1,128)}) custom-call(bf16[256,2048]{1,0:T(8,128)(2,1)} %bitcast.30, bf16[256,8192]{1,0:T(8,128)(2,1)} %wq_ref.1, f32[1,256]{1,0:T(1,128)} %bitcast.49), custom_call_target="tpu_custom_call" | custom-call | tf_op jit(solution)/shard_map/gather_project/pallas_call | solution.py:559
  124.6 119.3 %forward.1 = (bf16[8,256,2048]{2,1,0:T(8,128)(2,1)}, bf16[8,2,160,128]{3,2,1,0:T(8,128)(2,1)}, bf16[8,2,128,512]{3,2,1,0:T(8,128)(2,1)}, bf16[8,2,128,512]{3,2,1...) custom-call(bf16[8,2,128,512]{3,2,1,0:T(8,128)(2,1)} %bitcast.34, ...), custom_call_target="tpu_custom_call" | custom-call | tf_op jit(solution)/shard_map/forward/pallas_call | solution.py:817
  244.0 0.0 copy-start.7
  244.0 0.0 slice-start
  244.0 10.0 %convolution_convert_fusion.refs_16_ = bf16[512,2048]{1,0:T(8,128)(2,1)} fusion(bf16[2048,512]{1,0:T(8,128)(2,1)} %bitcast.52, bf16[2048,2048]{1,0:T(8,128)(2,1)} %bitcast.50), kind=kOutput, calls=%fused_computation.8 | convolution fusion | flops 4296015872 | bytes 12582912 | tf_op jit(solution)/shard_map/dot_general | solution.py:1661
  254.1 0.0 copy-done.12
  254.1 0.0 slice-start.1
  254.1 6.7 %fusion = (bf16[2048,512]{1,0:T(8,128)(2,1)S(1)}, f32[2048,512]{1,0:T(8,128)}) fusion(bf16[8,2,128,512]{3,2,1,0:T(8,128)(2,1)S(1)} %copy-done.13, bf16[2048,2048]{1,0:T(8,128)(2,1)S(1)} %bitcast.51, bf16[512,2048]{1,0:T(8,128)(2,1)S(1)} %copy-done.7), kind=kOutput, calls=%fused_computation.3 | convolution fusion | flops 4298113024 | bytes 18874368 | tf_op jit(solution)/shard_map/dot_general | solution.py:1656
  260.8 0.0 slice-done
  260.8 5.7 %convolution_convert_fusion.1 = bf16[2048,512]{1,0:T(8,128)(2,1)} fusion(bf16[2048,2048]{1,0:T(8,128)(2,1)S(1)} %bitcast.33, bf16[2048,512]{1,0:T(8,128)(2,1)S(1)} %get-tuple-element.69), kind=kOutput, calls=%fused_computation.9 | convolution fusion | flops 4296015872 | bytes 12582912 | tf_op jit(solution)/shard_map/dot_general | solution.py:1661
  266.6 145.5 %backward.1 = (bf16[8,2,128,512]{3,2,1,0:T(8,128)(2,1)}, bf16[320,512]{1,0:T(8,128)(2,1)}, bf16[256,2048]{1,0:T(8,128)(2,1)}, bf16[256,4096]{1,0:T(8,128)(2,1)}, bf16[512,2048]{1,0:T(8,128)(2,1)}) custom-call(f32[8,2,128,512]{3,2,1,0:T(8,128)} %bitcast.39, f32[8,2,128,512]{3,2,1,0:T(8,128)} %get-tuple-element.38.refs_1_, ...), custom_call_target="tpu_custom_call" | custom-call | tf_op jit(solution)/shard_map/backward/pallas_call | solution.py:1613
  412.1 0.0 copy-start.1
  412.1 108.1 %scatter_sums.1 = (bf16[256,2048]{1,0:T(8,128)(2,1)}, f32[320,512]{1,0:T(8,128)}, bf16[256,4096]{1,0:T(8,128)(2,1)}) custom-call(bf16[8,256,512]{2,1,0:T(8,128)(2,1)} %bitcast.41, bf16[8,256,512]{2,1,0:T(8,128)(2,1)} %bitcast.40, bf16[2048,1024]{1,0:T(8,128)(2,1)} %get-tuple-element.50.refs_2_, bf16[320,512]{1,0:T(8,128)(2,1)} %get-tuple-element.51.refs_3_, ...), custom_call_target="tpu_custom_call" | custom-call | tf_op jit(solution)/shard_map/scatter_sums/pallas_call | solution.py:1226
  520.2 0.0 copy-start.3
  520.3 1.9 fusion.3
  522.2 1.4 fusion.10
  523.7 1.3 slice.21
  525.0 1.4 slice.26
  526.3 1.7 slice.24
  528.0 1.7 slice.23
  529.8 2.8 fusion.6
  532.6 2.7 convert_element_type.76
  535.2 1.0 copy-done
  536.3 0.7 copy-done.4
  537.0 4.0 multiply_reduce_fusion
  540.9 0.6 convert_divide_fusion
  (26 shorter events, 0.1 us)
Async XLA Ops:
  244.0 10.1 %copy-start.7 = (bf16[512,2048]{1,0:T(8,128)(2,1)S(1)}, bf16[512,2048]{1,0:T(8,128)(2,1)}, u32[]{:S(2)}) copy-start(bf16[512,2048]{1,0:T(8,128)(2,1)} %wout_ref.1) | copy-start | bytes 6291460
  244.0 10.1 %copy-start.12 = (bf16[8,256,2048]{2,1,0:T(8,128)(2,1)S(1)}, bf16[8,256,2048]{2,1,0:T(8,128)(2,1)}, u32[]{:S(2)}) copy-start(bf16[8,256,2048]{2,1,0:T(8,128)(2,1)} %get-tuple-element.37) | copy-start | bytes 25165828
  244.0 10.1 %copy-start.13 = (bf16[8,2,128,512]{3,2,1,0:T(8,128)(2,1)S(1)}, bf16[8,2,128,512]{3,2,1,0:T(8,128)(2,1)}, u32[]{:S(2)}) copy-start(bf16[8,2,128,512]{3,2,1,0:T(8,128)(2,1)} %get-tuple-element.46) | copy-start | bytes 6291460
  244.0 16.8 %slice-start = ((s8[8388608]{0:T(1024)(128)(4,1)}), s8[4194304]{0:T(1024)(128)(4,1)S(1)}, s32[]{:S(2)}) async-start(s8[8388608]{0:T(1024)(128)(4,1)} %bitcast.31), calls=%async_computation | async-start | bytes 8388608
  254.1 6.7 %slice-start.1 = ((s8[8388608]{0:T(1024)(128)(4,1)}), s8[4194304]{0:T(1024)(128)(4,1)S(1)}, s32[]{:S(2)}) async-start(s8[8388608]{0:T(1024)(128)(4,1)} %bitcast.31), calls=%async_computation.1 | async-start | bytes 8388608
  260.8 5.7 %copy-start.8 = (bf16[2048,512]{1,0:T(8,128)(2,1)}, bf16[2048,512]{1,0:T(8,128)(2,1)S(1)}, u32[]{:S(2)}) copy-start(bf16[2048,512]{1,0:T(8,128)(2,1)S(1)} %get-tuple-element.69) | copy-start | bytes 6291460
  412.1 108.2 %copy-start.1 = (bf16[2,128,2048]{2,1,0:T(8,128)(2,1)S(1)}, bf16[2,128,2048]{2,1,0:T(8,128)(2,1)}, u32[]{:S(2)}) copy-start(bf16[2,128,2048]{2,1,0:T(8,128)(2,1)} %param.13) | copy-start | bytes 3145732
  412.1 108.2 %copy-start.10 = (f32[1,2048]{1,0:T(1,128)S(1)}, f32[1,2048]{1,0:T(1,128)}, u32[]{:S(2)}) copy-start(f32[1,2048]{1,0:T(1,128)} %get-tuple-element.53) | copy-start | bytes 24580
  520.2 9.5 %copy-start.2 = (bf16[256,2048]{1,0:T(8,128)(2,1)S(1)}, bf16[256,2048]{1,0:T(8,128)(2,1)}, u32[]{:S(2)}) copy-start(bf16[256,2048]{1,0:T(8,128)(2,1)} %get-tuple-element.52) | copy-start | bytes 3145732
  520.2 9.5 %copy-start.3 = (bf16[2,128,2048]{2,1,0:T(8,128)(2,1)S(1)}, bf16[2,128,2048]{2,1,0:T(8,128)(2,1)}, u32[]{:S(2)}) copy-start(bf16[2,128,2048]{2,1,0:T(8,128)(2,1)} %param.14) | copy-start | bytes 3145732
  520.2 9.5 %copy-start.9 = (bf16[256,2048]{1,0:T(8,128)(2,1)S(1)}, bf16[256,2048]{1,0:T(8,128)(2,1)}, u32[]{:S(2)}) copy-start(bf16[256,2048]{1,0:T(8,128)(2,1)} %get-tuple-element.48) | copy-start | bytes 3145732
  529.7 2.8 copy-start.5
  529.8 5.5 %copy-start.6 = (bf16[256,4096]{1,0:T(8,128)(2,1)S(1)}, bf16[256,4096]{1,0:T(8,128)(2,1)}, u32[]{:S(2)}) copy-start(bf16[256,4096]{1,0:T(8,128)(2,1)} %get-tuple-element.54) | copy-start | bytes 6291460
  532.6 3.7 copy-start
  532.6 4.4 copy-start.4
  536.9 4.0 copy-start.11
